TPU v7x, 128 devices: a whole 4x4x4 slice. The times are simulated.
128 devices in a mesh: gx: 16 (over y, x), gy: 2 (over core), gz: 4 (over z).
Axes of the slice: x: 4, y: 4, z: 4, core: 2. Of those that a mesh axis runs over, the one named last changes fastest.
Arguments:
- potential: float32 [960, 120, 512], P('gx', 'gy', 'gz'), may hold values from -6 to 6
- frag_root: int32 [3, 512], P(None, ('gx', 'gy', 'gz')), may hold values from 0 to 959, as said below
Outputs:
- frag_fields: float32 [512, 110592], P(('gx', 'gy', 'gz'))
Inputs may be any that keep to these rules, and one draw needn't show every extreme that they name: `frag_root`: fragment f is held by the device of linear index f // 4 (gx slowest). Along each dimension the box's first cell is the start of a block plus an offset in [-34, B - 34), B being that dimension's cells of one device. Along y and z that block is the holding device's own; along x it is the block of some device with the same gy and gz index, the anchor. Every anchor of a device supplies exactly 1 of its fragments.
All inputs are finite; a program needn't handle non-finite values.
Results may differ from a plain program's by a relative error of at most 0.00007.
Values sent between devices are 32-bit elements; how exact they have to be, the bound alone decides.
No kernel may reach another device: no remote copies, remote signals or barrier semaphores. Data moves between devices by JAX's collectives and lax.ppermute only.
A program may use at most 320 MiB of HBM per device.

v0:
```python
import math

import jax
import jax.numpy as jnp
import numpy as np
from jax import lax
from jax.experimental import pallas as pl
from jax.experimental.pallas import tpu as pltpu
from jax.sharding import PartitionSpec as P


G = 48
BOX = 68
HALO = 34
NY_LOCAL = 60
YPAD = 64
ROWS = G * G * G // 128
F32 = jnp.float32
BF16 = jnp.bfloat16
MID_COST = 10
FIELD_COST = 3
ANY = pl.ANY
VMEM = pltpu.VMEM
SMEM = pltpu.SMEM

GROUPS = (
    ((0, 1), (3, 0), (1, 0), (0, 3)),
    ((2, 2), (2, 0), (0, 2), (1, 1)),
    ((3, 3), (1, 3), (3, 1), (1, 2)),
    ((2, 1), (3, 2), (2, 3), (0, 0)),
)


def interp_matrix():
    a = np.arange(G, dtype=np.float64)[:, None]
    x = np.arange(BOX, dtype=np.float64)[None, :]
    total = np.ones((G, BOX))
    for k in range(1, G // 2):
        total = total + 2.0 * np.cos(2.0 * math.pi * k * (a / G - x / BOX))
    return (total / BOX).astype(np.float32)


def cost(us):
    return pl.CostEstimate(flops=int(us * 1e9), bytes_accessed=0, transcendentals=0)


def vm(limit=48):
    return pltpu.CompilerParams(vmem_limit_bytes=limit << 20)


def pack_rows(p_ref, x0, n, side, i, lane):
    base, first = (0, 40) if side == 0 else (128 - HALO, 0)
    rows = []
    for g in range(3):
        v = p_ref[x0 + g * n + i]
        shift = (first + HALO * g - base) % 128
        rows.append(pltpu.roll(v, shift, 1) if shift else v)
    at = jnp.where(lane < first, lane + 128 - first, lane - first)
    return jnp.where(at < HALO, rows[0], jnp.where(at < 2 * HALO, rows[1], rows[2]))


def pack_kernel(p_ref, za, zb, lo_a, hi_a, lo_b, hi_b):
    lane = lax.broadcasted_iota(jnp.int32, (NY_LOCAL, 128), 1)
    for i in range(20):
        za[i] = pack_rows(p_ref, 0, 20, 0, i, lane)
        zb[i] = pack_rows(p_ref, 0, 20, 1, i, lane)
    for i in range(12):
        lo_a[i] = pack_rows(p_ref, 0, 12, 0, i, lane)
        hi_a[i] = pack_rows(p_ref, 24, 12, 0, i, lane)
        lo_b[i] = pack_rows(p_ref, 0, 12, 1, i, lane)
        hi_b[i] = pack_rows(p_ref, 24, 12, 1, i, lane)


def pack(p):
    big = jax.ShapeDtypeStruct((20, NY_LOCAL, 128), F32)
    small = jax.ShapeDtypeStruct((12, NY_LOCAL, 128), F32)
    return pl.pallas_call(
        pack_kernel,
        out_shape=(big, big, small, small, small, small),
        compiler_params=vm(),
        name="pack",
    )(p)


def turn(src, out, count):
    for y in range(NY_LOCAL):
        out[:, y, :] = src[:, y, :].T[:count]
    out[:, NY_LOCAL:, :] = jnp.zeros((count, YPAD - NY_LOCAL, 128), F32)


def mid_kernel(before, own, after, packed, out, x_ref, sems):
    copies = [
        pltpu.make_async_copy(before, x_ref.at[pl.ds(0, HALO)], sems.at[0]),
        pltpu.make_async_copy(own, x_ref.at[pl.ds(HALO, 60)], sems.at[1]),
        pltpu.make_async_copy(after, x_ref.at[pl.ds(HALO + 60, HALO)], sems.at[2]),
    ]
    for c in copies:
        c.start()
    for c in copies:
        c.wait()
    turn(x_ref, out, 128)


def middle(before, own, after, packed):
    return pl.pallas_call(
        mid_kernel,
        out_shape=jax.ShapeDtypeStruct((128, YPAD, 128), F32),
        in_specs=[pl.BlockSpec(memory_space=ANY)] * 4,
        scratch_shapes=[VMEM((128, NY_LOCAL, 128), F32), pltpu.SemaphoreType.DMA((3,))],
        compiler_params=vm(),
        cost_estimate=cost(MID_COST),
        name="middle",
    )(before, own, after, packed)


def halo_kernel(zb, za, lb, la, rb, ra, roots, out, x_ref):
    lane = lax.broadcasted_iota(jnp.int32, (NY_LOCAL, 128), 1)

    def place(b_ref, a_ref, i, g, row):
        mine = jnp.logical_and(lane >= HALO * g, lane < HALO * g + HALO)
        v = jnp.where(mine, b_ref[i], a_ref[i])
        x_ref[row] = pltpu.roll(v, 128 - HALO * g, 1) if g else v

    for g in range(3):
        for i in range(20):
            place(zb, za, i, g, HALO + 20 * g + i)
        for i in range(12):
            x = 12 * g + i - 2
            if x >= 0:
                place(lb, la, i, g, x)
            x = 12 * g + i
            if x < HALO:
                place(rb, ra, i, g, HALO + 60 + x)
    turn(x_ref, out, 80)


def halos(zb, za, lb, la, rb, ra, roots):
    return pl.pallas_call(
        halo_kernel,
        out_shape=jax.ShapeDtypeStruct((80, YPAD, 128), F32),
        in_specs=[pl.BlockSpec(memory_space=VMEM)] * 6 + [pl.BlockSpec(memory_space=SMEM)],
        scratch_shapes=[VMEM((128, NY_LOCAL, 128), F32)],
        compiler_params=vm(),
        cost_estimate=cost(5),
        name="halos",
    )(zb, za, lb, la, rb, ra, roots)


def split_rows(f):
    hi = f.astype(BF16).astype(F32)
    return jnp.concatenate([hi, f - hi], axis=0).astype(BF16)


def placed(table_hi, table_lo, hot):
    hot = jnp.where(hot, 1.0, 0.0).astype(BF16)
    hi = jnp.dot(table_hi, hot, preferred_element_type=F32)
    lo = jnp.dot(table_lo, hot, preferred_element_type=F32)
    top = jnp.concatenate([hi, hi], axis=1)
    low = jnp.concatenate([lo, jnp.zeros_like(lo)], axis=1)
    return jnp.concatenate([top, low], axis=0).astype(BF16)


def folded(r):
    return r[:G] + r[G:]


def locate(roots, place, sizes, slot, holder):
    nx, ny, nz, bx, by, bz = sizes
    ok = jnp.int32(0)
    x0 = y0 = z0 = jnp.int32(0)
    for s in range(slot):
        def rel(dim, origin, total):
            v = roots[holder, dim, s] + HALO - origin
            return jnp.where(v < 0, v + total, jnp.where(v >= total, v - total, v))

        rx = rel(0, place[0] * bx, nx)
        mine = rx < bx
        ok = jnp.where(mine, 1, ok)
        x0 = jnp.where(mine, rx, x0)
        y0 = jnp.where(mine, rel(1, place[1] * by, ny) - HALO, y0)
        z0 = jnp.where(mine, rel(2, place[2] * bz, nz), z0)
    return ok, x0, y0, z0


def field_kernel(shifts, sizes, slot, roots, place, thi, tlo, a2_ref, own_m, part_m, own_h, part_h, *rest):
    n = len(shifts)
    outs = rest[:n]
    w_own, w_part, t1, t2, obuf, info, in_sems, out_sems = rest[n:]
    gx = place[0]
    py = gx // 4
    px = gx % 4

    for j, (dy, dx) in enumerate(shifts):
        holder = ((py + dy) % 4) * 4 + (px + dx) % 4
        ok, x0, y0, z0 = locate(roots, place, sizes, slot, holder)
        info[0, j] = ok
        info[1, j] = x0
        info[2, j] = y0
        info[3, j] = z0
    info[0, n] = jnp.int32(0)

    def copies(j, b):
        z0 = info[3, j]
        c = jnp.clip(z0 - HALO, 0, 128 - BOX)
        for k, (src_m, src_h, w) in enumerate(((own_m, own_h, w_own), (part_m, part_h, w_part))):
            yield None, pltpu.make_async_copy(
                src_m.at[pl.ds(c, BOX)], w.at[b, pl.ds(HALO, BOX)], in_sems.at[b, 2 * k])
            yield z0 < HALO, pltpu.make_async_copy(
                src_h.at[pl.ds(0, HALO)], w.at[b, pl.ds(0, HALO)], in_sems.at[b, 2 * k + 1])
            yield z0 > 128 - HALO, pltpu.make_async_copy(
                src_h.at[pl.ds(40, HALO)], w.at[b, pl.ds(HALO + BOX, HALO)], in_sems.at[b, 2 * k + 1])

    def begin(j, b):
        for cond, c in copies(j, b):
            if cond is None:
                c.start()
            else:
                pl.when(cond)(c.start)

    def finish(j, b):
        for cond, c in copies(j, b):
            if cond is None:
                c.wait()
            else:
                pl.when(cond)(c.wait)

    def out_copy(k, b):
        return pltpu.make_async_copy(obuf.at[b], outs[k], out_sems.at[b])

    for b in range(G):
        t1[b * 72 + 64:b * 72 + 72, :] = jnp.zeros((8, 128), F32)

    def compute(j, b):
        x0 = info[1, j]
        y0 = info[2, j]
        z0 = info[3, j]
        zoff = z0 - jnp.clip(z0 - HALO, 0, 128 - BOX)
        k = lax.broadcasted_iota(jnp.int32, (128, 128), 0)
        col = lax.broadcasted_iota(jnp.int32, (128, 128), 1)
        half = col & 63
        near = jnp.where(col < 64, col, col - 4) - y0
        far = jnp.where(col < 64, -1, col - 124 - y0)
        hot_y = jnp.logical_and(half < NY_LOCAL, jnp.logical_or(k == near, k == far))
        a1 = placed(thi[...], tlo[...], hot_y)
        a3 = placed(thi[...], tlo[...], k == col - x0)
        a2 = a2_ref[...]
        for p in range(BOX // 2):
            z = zoff + 2 * p
            own = jnp.concatenate([w_own[b, z], w_own[b, z + 1]], axis=1)
            part = jnp.concatenate([w_part[b, z], w_part[b, z + 1]], axis=1)
            rhs = split_rows(jnp.concatenate([own, part], axis=0))
            t = folded(jnp.dot(a1, rhs, preferred_element_type=F32))
            t1[pl.ds(2 * p, G, stride=72), :] = t[:, :128]
            t1[pl.ds(2 * p + 1, G, stride=72), :] = t[:, 128:]
        for q in range(0, G, 2):
            f = jnp.concatenate([t1[q * 72:q * 72 + 72, :], t1[q * 72 + 72:q * 72 + 144, :]], axis=1)
            t = folded(jnp.dot(a2, split_rows(f), preferred_element_type=F32))
            t2[q * G:q * G + G, :] = t[:, :128]
            t2[q * G + G:q * G + 2 * G, :] = t[:, 128:]
        for m in range(9):
            f = t2[256 * m:256 * m + 256, :]
            hi = f.astype(BF16)
            lo = (f - hi.astype(F32)).astype(BF16)
            rhs = jnp.concatenate([hi, lo], axis=1)
            r = lax.dot_general(a3, rhs, (((1,), (1,)), ((), ())), preferred_element_type=F32)
            t = folded(r)
            obuf[b, pl.ds(2 * m, G, stride=18), :] = t[:, :128]
            obuf[b, pl.ds(2 * m + 1, G, stride=18), :] = t[:, 128:]

    @pl.when(info[0, 0] == 1)
    def _():
        begin(0, 0)

    def step(j, carry):
        b = lax.rem(j, 2)

        @pl.when(info[0, j + 1] == 1)
        def _():
            begin(j + 1, 1 - b)

        @pl.when(info[0, j] == 1)
        def _():
            finish(j, b)
            compute(j, b)
            for k in range(n):
                @pl.when(j == k)
                def _(k=k):
                    out_copy(k, b).start()
            out_copy(0, b).wait()

        return carry

    lax.fori_loop(0, n, step, 0)


def fields(shifts, sizes, slot, roots, place, thi, tlo, a2, own_m, part_m, own_h, part_h):
    n = len(shifts)
    out = jax.ShapeDtypeStruct((ROWS, 128), F32)
    smem = pl.BlockSpec(memory_space=SMEM)
    vmem = pl.BlockSpec(memory_space=VMEM)
    hbm = pl.BlockSpec(memory_space=ANY)

    def kernel(*refs):
        field_kernel(shifts, sizes, slot, *refs)

    return pl.pallas_call(
        kernel,
        out_shape=(out,) * n,
        in_specs=[smem, smem, vmem, vmem, vmem, hbm, hbm, hbm, hbm],
        out_specs=(hbm,) * n,
        scratch_shapes=[
            VMEM((2, 2 * HALO + BOX, YPAD, 128), F32),
            VMEM((2, 2 * HALO + BOX, YPAD, 128), F32),
            VMEM((G * 72, 128), F32),
            VMEM((G * G, 128), F32),
            VMEM((2, ROWS, 128), F32),
            SMEM((4, n + 1), jnp.int32),
            pltpu.SemaphoreType.DMA((2, 4)),
            pltpu.SemaphoreType.DMA((2,)),
        ],
        compiler_params=vm(),
        cost_estimate=cost(FIELD_COST * n),
        name="fields",
    )(roots, place, thi, tlo, a2, own_m, part_m, own_h, part_h)


def pick_kernel(order, sizes, slot, own_root, place, *rest):
    srcs = rest[:16]
    out, buf, sems = rest[16:]
    nx, bx = sizes[0], sizes[3]
    gx = place[0]
    py = gx // 4
    px = gx % 4
    for s in range(slot):
        r = own_root[0, s] + HALO
        for k, (dy, dx) in enumerate(order):
            anchor = ((py + 4 - dy) % 4) * 4 + (px + 4 - dx) % 4
            v = r - anchor * bx
            v = jnp.where(v < 0, v + nx, jnp.where(v >= nx, v - nx, v))

            @pl.when(v < bx)
            def _(k=k, s=s):
                pltpu.make_async_copy(srcs[k], buf.at[s], sems.at[s]).start()
    for s in range(slot):
        pltpu.make_async_copy(srcs[0], buf.at[s], sems.at[s]).wait()
        out[:, s, :] = buf[s]


def pick(order, sizes, slot, own_root, place, parts):
    smem = pl.BlockSpec(memory_space=SMEM)

    def kernel(*refs):
        pick_kernel(order, sizes, slot, *refs)

    return pl.pallas_call(
        kernel,
        out_shape=jax.ShapeDtypeStruct((ROWS, slot, 128), F32),
        in_specs=[smem, smem] + [pl.BlockSpec(memory_space=ANY)] * 16,
        scratch_shapes=[VMEM((slot, ROWS, 128), F32), pltpu.SemaphoreType.DMA((slot,))],
        compiler_params=vm(),
        name="pick",
    )(own_root, place, *parts)


def program(potential, frag_root):
    bx, by, bz = potential.shape
    groups = lax.axis_size("gx")
    zs = lax.axis_size("gz")
    sizes = (bx * groups, by * lax.axis_size("gy"), bz * zs, bx, by, bz)
    slot = frag_root.shape[1]
    place = jnp.stack([lax.axis_index("gx"), lax.axis_index("gy"), lax.axis_index("gz")]).astype(jnp.int32)

    def moved(v, sx, sz):
        if sz == 0:
            return lax.ppermute(v, "gx", [(i, (i + sx) % groups) for i in range(groups)])
        if sx == 0:
            return lax.ppermute(v, "gz", [(i, (i + sz) % zs) for i in range(zs)])
        perm = []
        for i in range(groups):
            for j in range(zs):
                perm.append((i * zs + j, ((i + sx) % groups) * zs + (j + sz) % zs))
        return lax.ppermute(v, ("gx", "gz"), perm)

    before = moved(potential[bx - HALO:], 1, 0)
    after = moved(potential[:HALO], -1, 0)
    za, zb, lo_a, hi_a, lo_b, hi_b = pack(potential)
    got_zb = moved(zb, 0, 1)
    got_za = moved(za, 0, -1)
    got_lb = moved(hi_b, 1, 1)
    got_rb = moved(lo_b, -1, 1)
    got_la = moved(hi_a, 1, -1)
    got_ra = moved(lo_a, -1, -1)
    roots = lax.all_to_all(
        jnp.broadcast_to(frag_root[None], (groups, 3, slot)), "gx", 0, 0, tiled=True
    )

    swap = [(0, 1), (1, 0)]
    own_m = middle(before, potential, after, zb)
    part_m = lax.ppermute(own_m, "gy", swap)
    own_h = halos(got_zb, got_za, got_lb, got_la, got_rb, got_ra, roots)
    part_h = lax.ppermute(own_h, "gy", swap)

    table = interp_matrix()
    hi = np.asarray(table.astype(BF16))
    lo = (table - hi.astype(np.float32)).astype(BF16)
    thi = np.zeros((G, 128), BF16)
    tlo = np.zeros((G, 128), BF16)
    thi[:, :BOX] = hi
    tlo[:, :BOX] = lo
    a2 = np.zeros((2 * G, 144), BF16)
    a2[:G, :BOX] = hi
    a2[:G, 72:72 + BOX] = hi
    a2[G:, :BOX] = lo

    order = []
    parts = []
    for shifts in GROUPS:
        done = fields(shifts, sizes, slot, roots, place, thi, tlo, a2, own_m, part_m, own_h, part_h)
        for (dy, dx), v in zip(shifts, done):
            order.append((dy, dx))
            if (dy, dx) != (0, 0):
                perm = [(4 * y + x, 4 * ((y + dy) % 4) + (x + dx) % 4) for y in range(4) for x in range(4)]
                v = lax.ppermute(v, "gx", perm)
            parts.append(v)
    out = pick(tuple(order), sizes, slot, frag_root, place, parts)
    return jnp.transpose(out, (1, 0, 2)).reshape(slot, ROWS * 128)


def solution(mesh):
    return jax.shard_map(
        program,
        mesh=mesh,
        in_specs=(P("gx", "gy", "gz"), P(None, ("gx", "gy", "gz"))),
        out_specs=P(("gx", "gy", "gz"), None),
        check_vma=False,
    )
```

profile of v0, /device:TPU:75, one launch (start us, length us, event | category | flops | bytes accessed | tf_op | source)
XLA Modules:
  0.0 235.3 jit_solution(7549605605650421136)
XLA Ops:
  0.0 2.0 fusion
  2.0 1.3 collective-permute-start
  3.3 0.3 collective-permute-start.1
  3.5 2.3 pack.1
  5.8 21.7 %collective-permute-done.before = f32[34,60,128]{2,1,0:T(8,128)S(1)} collective-permute-done((f32[34,60,128]{2,1,0:T(8,128)S(1)}, f32[34,60,128]{2,1,0:T(8,128)S(1)}, u32[]{:S(2)}, u32[]{:S(2)}) %collective-permute-start) | collective-permute-done | bytes 1044512 | tf_op jit(solution)/shard_map/ppermute | solution.py:375
  27.5 0.9 collective-permute-done.1.after
  28.4 6.8 %middle.1.refs_5_ = f32[128,64,128]{2,1,0:T(8,128)} custom-call(f32[34,60,128]{2,1,0:T(8,128)S(1)} %collective-permute-done.before, f32[60,60,128]{2,1,0:T(8,128)S(1)} %copy-done, f32[34,60,128]{2,1,0:T(8,128)S(1)} %collective-permute-done.1.after, f32[20,60,128]{2,1,0:T(8,128)S(1)} %get-tuple-element.27.packed), custom_call_target="tpu_custom_call" | custom-call | flops 10000000000 | tf_op jit(solution)/shard_map/middle/pallas_call | solution.py:105
  35.2 1.9 collective-permute-start.2
  37.1 2.0 collective-permute-start.5
  39.1 3.2 %collective-permute-start.6 = (f32[12,60,128]{2,1,0:T(8,128)S(1)}, f32[12,60,128]{2,1,0:T(8,128)S(1)}, u32[]{:S(2)}, u32[]{:S(2)}) collective-permute-start(f32[12,60,128]{2,1,0:T(8,128)S(1)} %get-tuple-element.30), channel_id=1, source_target_pairs={{0,11},{1,8},{2,9},{3,10},{8,19},{9,16},{10,17},{11,18},{16,27},{1... | collective-permute-start | bytes 1105928 | tf_op jit(solution)/shard_map/ppermute | solution.py:382
  42.3 1.3 collective-permute-start.3
  43.6 0.1 collective-permute-start.4
  43.7 4.9 %collective-permute-done.5.lb = f32[12,60,128]{2,1,0:T(8,128)S(1)} collective-permute-done((f32[12,60,128]{2,1,0:T(8,128)S(1)}, f32[12,60,128]{2,1,0:T(8,128)S(1)}, u32[]{:S(2)}, u32[]{:S(2)}) %collective-permute-start.5) | collective-permute-done | bytes 368672 | tf_op jit(solution)/shard_map/ppermute | solution.py:382
  48.7 4.3 %collective-permute-start.7 = (f32[12,60,128]{2,1,0:T(8,128)S(1)}, f32[12,60,128]{2,1,0:T(8,128)S(1)}, u32[]{:S(2)}, u32[]{:S(2)}) collective-permute-start(f32[12,60,128]{2,1,0:T(8,128)S(1)} %get-tuple-element.31), channel_id=1, source_target_pairs={{0,121},{1,122},{2,123},{3,120},{8,1},{9,2},{10,3},{11,0},{16,9},{... | collective-permute-start | bytes 1105928 | tf_op jit(solution)/shard_map/ppermute | solution.py:382
  53.0 4.3 %collective-permute-done.6.la = f32[12,60,128]{2,1,0:T(8,128)S(1)} collective-permute-done((f32[12,60,128]{2,1,0:T(8,128)S(1)}, f32[12,60,128]{2,1,0:T(8,128)S(1)}, u32[]{:S(2)}, u32[]{:S(2)}) %collective-permute-start.6) | collective-permute-done | bytes 368672 | tf_op jit(solution)/shard_map/ppermute | solution.py:382
  57.3 4.1 %collective-permute-start.8 = (f32[12,60,128]{2,1,0:T(8,128)S(1)}, f32[12,60,128]{2,1,0:T(8,128)S(1)}, u32[]{:S(2)}, u32[]{:S(2)}) collective-permute-start(f32[12,60,128]{2,1,0:T(8,128)S(1)} %get-tuple-element.32), channel_id=1, source_target_pairs={{0,123},{1,120},{2,121},{3,122},{8,3},{9,0},{10,1},{11,2},{16,11},... | collective-permute-start | bytes 1105928 | tf_op jit(solution)/shard_map/ppermute | solution.py:382
  61.4 11.0 %all_to_all.5.roots.refs_0_ = s32[16,3,4]{2,1,0:T(4,128)S(1)} all-to-all(s32[16,3,4]{2,1,0:T(4,128)S(1)} %broadcast_in_dim.2), channel_id=1, replica_groups=mesh['gx'=16,'gy'=2,'gz'=4] {'gx'}, dimensions={0} | all-to-all | bytes 1536 | tf_op jit(solution)/shard_map/all_to_all | solution.py:393
  72.4 0.0 collective-permute-done.8.ra
  72.5 3.4 %collective-permute-done.4.za = f32[20,60,128]{2,1,0:T(8,128)S(1)} collective-permute-done((f32[20,60,128]{2,1,0:T(8,128)S(1)}, f32[20,60,128]{2,1,0:T(8,128)S(1)}, u32[]{:S(2)}, u32[]{:S(2)}) %collective-permute-start.4) | collective-permute-done | bytes 614432 | tf_op jit(solution)/shard_map/ppermute | solution.py:377
  75.8 5.7 %halos.1.refs_7_ = f32[80,64,128]{2,1,0:T(8,128)S(1)} custom-call(f32[20,60,128]{2,1,0:T(8,128)S(1)} %collective-permute-done.3.zb, f32[20,60,128]{2,1,0:T(8,128)S(1)} %collective-permute-done.4.za, f32[12,60,128]{2,1,0:T(8,128)S(1)} %collective-permute-done.5.lb, f32[12,60,128]{2,1,0:T(8,128)S(1)} %collective-permute-done.6.la, ...), custom_call_target="tpu_custom_call" | custom-call | flops 5000000000 | tf_op jit(solution)/shard_map/halos/pallas_call | solution.py:138
  81.6 1.9 collective-permute-start.9
  83.4 0.1 pad_add_fusion.refs_1_
  83.5 4.6 %collective-permute-done.9.refs_8_ = f32[80,64,128]{2,1,0:T(8,128)} collective-permute-done((f32[80,64,128]{2,1,0:T(8,128)S(1)}, f32[80,64,128]{2,1,0:T(8,128)}, u32[]{:S(2)}, u32[]{:S(2)}) %collective-permute-start.9) | collective-permute-done | bytes 2621472 | tf_op jit(solution)/shard_map/ppermute | solution.py:401
  88.1 1.5 fields.7
  89.6 0.8 copy-done.1
  90.3 1.8 collective-permute-start.22
  92.2 7.2 %collective-permute-start.23 = (f32[864,128]{1,0:T(8,128)S(1)}, f32[864,128]{1,0:T(8,128)S(1)}, u32[]{:S(2)}, u32[]{:S(2)}) collective-permute-start(f32[864,128]{1,0:T(8,128)S(1)} %get-tuple-element.46), channel_id=1, source_target_pairs={{0,112},{8,120},{16,96},{24,104},{32,16},{40,24},{48,0},{56,8},{64... | collective-permute-start | bytes 1327112 | tf_op jit(solution)/shard_map/ppermute | solution.py:423
  99.4 6.2 %collective-permute-start.24 = (f32[864,128]{1,0:T(8,128)S(1)}, f32[864,128]{1,0:T(8,128)S(1)}, u32[]{:S(2)}, u32[]{:S(2)}) collective-permute-start(f32[864,128]{1,0:T(8,128)S(1)} %get-tuple-element.47), channel_id=1, source_target_pairs={{0,88},{8,64},{16,72},{24,80},{32,120},{40,96},{48,104},{56,112},{... | collective-permute-start | bytes 1327112 | tf_op jit(solution)/shard_map/ppermute | solution.py:423
  105.6 1.4 fields.6
  107.1 0.1 collective-permute-start.18
  107.2 8.3 %collective-permute-start.19 = (f32[864,128]{1,0:T(8,128)S(1)}, f32[864,128]{1,0:T(8,128)S(1)}, u32[]{:S(2)}, u32[]{:S(2)}) collective-permute-start(f32[864,128]{1,0:T(8,128)S(1)} %get-tuple-element.42), channel_id=1, source_target_pairs={{0,56},{8,32},{16,40},{24,48},{32,88},{40,64},{48,72},{56,80},{64,... | collective-permute-start | bytes 1327112 | tf_op jit(solution)/shard_map/ppermute | solution.py:423
  115.4 1.7 fields.5
  117.1 0.0 collective-permute-done.22.refs_14_
  117.1 8.0 %collective-permute-start.20 = (f32[864,128]{1,0:T(8,128)S(1)}, f32[864,128]{1,0:T(8,128)S(1)}, u32[]{:S(2)}, u32[]{:S(2)}) collective-permute-start(f32[864,128]{1,0:T(8,128)S(1)} %get-tuple-element.43), channel_id=1, source_target_pairs={{0,104},{8,112},{16,120},{24,96},{32,8},{40,16},{48,24},{56,0},{64... | collective-permute-start | bytes 1327112 | tf_op jit(solution)/shard_map/ppermute | solution.py:423
  125.1 0.0 collective-permute-done.23.refs_15_
  125.1 12.9 %collective-permute-start.21 = (f32[864,128]{1,0:T(8,128)S(1)}, f32[864,128]{1,0:T(8,128)S(1)}, u32[]{:S(2)}, u32[]{:S(2)}) collective-permute-start(f32[864,128]{1,0:T(8,128)S(1)} %get-tuple-element.44), channel_id=1, source_target_pairs={{0,48},{8,56},{16,32},{24,40},{32,80},{40,88},{48,64},{56,72},{64,... | collective-permute-start | bytes 1327112 | tf_op jit(solution)/shard_map/ppermute | solution.py:423
  138.0 7.1 %collective-permute-start.14 = (f32[864,128]{1,0:T(8,128)S(1)}, f32[864,128]{1,0:T(8,128)S(1)}, u32[]{:S(2)}, u32[]{:S(2)}) collective-permute-start(f32[864,128]{1,0:T(8,128)S(1)} %get-tuple-element.37), channel_id=1, source_target_pairs={{0,80},{8,88},{16,64},{24,72},{32,112},{40,120},{48,96},{56,104},{... | collective-permute-start | bytes 1327112 | tf_op jit(solution)/shard_map/ppermute | solution.py:423
  145.1 14.4 %collective-permute-start.15 = (f32[864,128]{1,0:T(8,128)S(1)}, f32[864,128]{1,0:T(8,128)S(1)}, u32[]{:S(2)}, u32[]{:S(2)}) collective-permute-start(f32[864,128]{1,0:T(8,128)S(1)} %get-tuple-element.38), channel_id=1, source_target_pairs={{0,64},{8,72},{16,80},{24,88},{32,96},{40,104},{48,112},{56,120},{... | collective-permute-start | bytes 1327112 | tf_op jit(solution)/shard_map/ppermute | solution.py:423
  159.6 27.4 %collective-permute-start.16 = (f32[864,128]{1,0:T(8,128)S(1)}, f32[864,128]{1,0:T(8,128)S(1)}, u32[]{:S(2)}, u32[]{:S(2)}) collective-permute-start(f32[864,128]{1,0:T(8,128)S(1)} %get-tuple-element.39), channel_id=1, source_target_pairs={{0,16},{8,24},{16,0},{24,8},{32,48},{40,56},{48,32},{56,40},{64,80... | collective-permute-start | bytes 1327112 | tf_op jit(solution)/shard_map/ppermute | solution.py:423
  187.0 1.4 fields.4
  188.4 12.3 %collective-permute-start.17 = (f32[864,128]{1,0:T(8,128)S(1)}, f32[864,128]{1,0:T(8,128)S(1)}, u32[]{:S(2)}, u32[]{:S(2)}) collective-permute-start(f32[864,128]{1,0:T(8,128)S(1)} %get-tuple-element.40), channel_id=1, source_target_pairs={{0,40},{8,48},{16,56},{24,32},{32,72},{40,80},{48,88},{56,64},{64,... | collective-permute-start | bytes 1327112 | tf_op jit(solution)/shard_map/ppermute | solution.py:423
  200.7 1.5 collective-permute-done.14.refs_6_
  202.3 1.5 collective-permute-start.12
  203.7 15.8 %collective-permute-done.16.refs_8_ = f32[864,128]{1,0:T(8,128)S(1)} collective-permute-done((f32[864,128]{1,0:T(8,128)S(1)}, f32[864,128]{1,0:T(8,128)S(1)}, u32[]{:S(2)}, u32[]{:S(2)}) %collective-permute-start.16) | collective-permute-done | bytes 442400 | tf_op jit(solution)/shard_map/ppermute | solution.py:423
  219.5 0.8 collective-permute-done.10.refs_2_
  220.3 3.3 %collective-permute-done.12.refs_4_ = f32[864,128]{1,0:T(8,128)S(1)} collective-permute-done((f32[864,128]{1,0:T(8,128)S(1)}, f32[864,128]{1,0:T(8,128)S(1)}, u32[]{:S(2)}, u32[]{:S(2)}) %collective-permute-start.12) | collective-permute-done | bytes 442400 | tf_op jit(solution)/shard_map/ppermute | solution.py:423
  223.6 7.0 %collective-permute-done.13.refs_5_ = f32[864,128]{1,0:T(8,128)S(1)} collective-permute-done((f32[864,128]{1,0:T(8,128)S(1)}, f32[864,128]{1,0:T(8,128)S(1)}, u32[]{:S(2)}, u32[]{:S(2)}) %collective-permute-start.13) | collective-permute-done | bytes 442400 | tf_op jit(solution)/shard_map/ppermute | solution.py:423
  230.6 4.5 %pick.1 = f32[864,4,128]{2,1,0:T(4,128)} custom-call(s32[3,4]{1,0:T(4,128)S(1)} %copy-done.2, s32[3]{0:T(128)S(1)} %pad_add_fusion.refs_1_, f32[864,128]{1,0:T(8,128)S(1)} %collective-permute-done.10.refs_2_, f32[864,128]{1,0:T(8,128)S(1)} %collective-permute-done.11.refs_3_, f32[864,128]{1,0:T(8,128)S(1)} %collective-permute-done.12.refs_4_, ...), custom_call_target="tpu_custom_call" | custom-call | tf_op jit(solution)/shard_map/pick/pallas_call | solution.py:355
  (28 shorter events, 0.1 us)
Async XLA Ops:
  0.0 3.5 %copy-start = (f32[60,60,128]{2,1,0:T(8,128)S(1)}, f32[60,60,128]{2,1,0:T(8,128)}, u32[]{:S(2)}) copy-start(f32[60,60,128]{2,1,0:T(8,128)} %own.1) | copy-start | bytes 5529604
  2.0 25.5 %collective-permute-start = (f32[34,60,128]{2,1,0:T(8,128)S(1)}, f32[34,60,128]{2,1,0:T(8,128)S(1)}, u32[]{:S(2)}, u32[]{:S(2)}) collective-permute-start(f32[34,60,128]{2,1,0:T(8,128)S(1)} %get-tuple-element.50), channel_id=1, source_target_pairs={{0,8},{8,16},{16,24},{24,32},{32,40},{40,48},{48,56},{56,64},{64,7... | collective-permute-start | bytes 3133448 | tf_op jit(solution)/shard_map/ppermute | solution.py:375
  3.3 25.2 %collective-permute-start.1 = (f32[34,60,128]{2,1,0:T(8,128)S(1)}, f32[34,60,128]{2,1,0:T(8,128)S(1)}, u32[]{:S(2)}, u32[]{:S(2)}) collective-permute-start(f32[34,60,128]{2,1,0:T(8,128)S(1)} %get-tuple-element.49), channel_id=1, source_target_pairs={{0,120},{8,0},{16,8},{24,16},{32,24},{40,32},{48,40},{56,48},{64,5... | collective-permute-start | bytes 3133448 | tf_op jit(solution)/shard_map/ppermute | solution.py:375
  28.4 33.0 %copy-start.2 = (s32[3,4]{1,0:T(4,128)S(1)}, s32[3,4]{1,0:T(4,128)}, u32[]{:S(2)}) copy-start(s32[3,4]{1,0:T(4,128)} %refs_0_.1) | copy-start | bytes 148
  35.2 52.8 %collective-permute-start.2 = (f32[128,64,128]{2,1,0:T(8,128)}, f32[128,64,128]{2,1,0:T(8,128)}, u32[]{:S(2)}, u32[]{:S(2)}) collective-permute-start(f32[128,64,128]{2,1,0:T(8,128)} %middle.1.refs_5_), channel_id=1, source_target_pairs={{0,4},{4,0},{1,5},{5,1},{2,6},{6,2},{3,7},{7,3},{8,12},{12,8},{9,1... | collective-permute-start | bytes 12582920 | tf_op jit(solution)/shard_map/ppermute | solution.py:399
  37.1 11.5 %collective-permute-start.5 = (f32[12,60,128]{2,1,0:T(8,128)S(1)}, f32[12,60,128]{2,1,0:T(8,128)S(1)}, u32[]{:S(2)}, u32[]{:S(2)}) collective-permute-start(f32[12,60,128]{2,1,0:T(8,128)S(1)} %get-tuple-element.29), channel_id=1, source_target_pairs={{0,9},{1,10},{2,11},{3,8},{8,17},{9,18},{10,19},{11,16},{16,25},{1... | collective-permute-start | bytes 1105928 | tf_op jit(solution)/shard_map/ppermute | solution.py:382
  39.1 18.2 %collective-permute-start.6 = (f32[12,60,128]{2,1,0:T(8,128)S(1)}, f32[12,60,128]{2,1,0:T(8,128)S(1)}, u32[]{:S(2)}, u32[]{:S(2)}) collective-permute-start(f32[12,60,128]{2,1,0:T(8,128)S(1)} %get-tuple-element.30), channel_id=1, source_target_pairs={{0,11},{1,8},{2,9},{3,10},{8,19},{9,16},{10,17},{11,18},{16,27},{1... | collective-permute-start | bytes 1105928 | tf_op jit(solution)/shard_map/ppermute | solution.py:382
  42.3 30.2 %collective-permute-start.3 = (f32[20,60,128]{2,1,0:T(8,128)S(1)}, f32[20,60,128]{2,1,0:T(8,128)S(1)}, u32[]{:S(2)}, u32[]{:S(2)}) collective-permute-start(f32[20,60,128]{2,1,0:T(8,128)S(1)} %get-tuple-element.27.packed), channel_id=1, source_target_pairs={{0,1},{1,2},{2,3},{3,0},{4,5},{5,6},{6,7},{7,4},{8,9},{9,10},{10,1... | collective-permute-start | bytes 1843208 | tf_op jit(solution)/shard_map/ppermute | solution.py:377
  43.6 32.2 %collective-permute-start.4 = (f32[20,60,128]{2,1,0:T(8,128)S(1)}, f32[20,60,128]{2,1,0:T(8,128)S(1)}, u32[]{:S(2)}, u32[]{:S(2)}) collective-permute-start(f32[20,60,128]{2,1,0:T(8,128)S(1)} %get-tuple-element.28), channel_id=1, source_target_pairs={{0,3},{1,0},{2,1},{3,2},{4,7},{5,4},{6,5},{7,6},{8,11},{9,8},{10,9... | collective-permute-start | bytes 1843208 | tf_op jit(solution)/shard_map/ppermute | solution.py:377
  48.7 23.8 %collective-permute-start.7 = (f32[12,60,128]{2,1,0:T(8,128)S(1)}, f32[12,60,128]{2,1,0:T(8,128)S(1)}, u32[]{:S(2)}, u32[]{:S(2)}) collective-permute-start(f32[12,60,128]{2,1,0:T(8,128)S(1)} %get-tuple-element.31), channel_id=1, source_target_pairs={{0,121},{1,122},{2,123},{3,120},{8,1},{9,2},{10,3},{11,0},{16,9},{... | collective-permute-start | bytes 1105928 | tf_op jit(solution)/shard_map/ppermute | solution.py:382
  57.3 15.2 %collective-permute-start.8 = (f32[12,60,128]{2,1,0:T(8,128)S(1)}, f32[12,60,128]{2,1,0:T(8,128)S(1)}, u32[]{:S(2)}, u32[]{:S(2)}) collective-permute-start(f32[12,60,128]{2,1,0:T(8,128)S(1)} %get-tuple-element.32), channel_id=1, source_target_pairs={{0,123},{1,120},{2,121},{3,122},{8,3},{9,0},{10,1},{11,2},{16,11},... | collective-permute-start | bytes 1105928 | tf_op jit(solution)/shard_map/ppermute | solution.py:382
  72.4 15.7 %copy-start.3 = (bf16[96,144]{1,0:T(8,128)(2,1)S(1)}, bf16[96,144]{1,0:T(8,128)(2,1)}, u32[]{:S(2)}) copy-start(bf16[96,144]{1,0:T(8,128)(2,1)} %constant.22.clone.refs_4_) | copy-start | bytes 82948
  72.4 15.7 %copy-start.4 = (bf16[48,128]{1,0:T(8,128)(2,1)S(1)}, bf16[48,128]{1,0:T(8,128)(2,1)}, u32[]{:S(2)}) copy-start(bf16[48,128]{1,0:T(8,128)(2,1)} %constant.20.clone.refs_2_) | copy-start | bytes 36868
  72.4 15.7 %copy-start.5 = (bf16[48,128]{1,0:T(8,128)(2,1)S(1)}, bf16[48,128]{1,0:T(8,128)(2,1)}, u32[]{:S(2)}) copy-start(bf16[48,128]{1,0:T(8,128)(2,1)} %constant.21.clone.refs_3_) | copy-start | bytes 36868
  81.6 6.5 %collective-permute-start.9 = (f32[80,64,128]{2,1,0:T(8,128)S(1)}, f32[80,64,128]{2,1,0:T(8,128)}, u32[]{:S(2)}, u32[]{:S(2)}) collective-permute-start(f32[80,64,128]{2,1,0:T(8,128)S(1)} %halos.1.refs_7_), channel_id=1, source_target_pairs={{0,4},{4,0},{1,5},{5,1},{2,6},{6,2},{3,7},{7,3},{8,12},{12,8},{9,1... | collective-permute-start | bytes 7864328 | tf_op jit(solution)/shard_map/ppermute | solution.py:401
  89.6 0.8 copy-start.1
  90.3 26.8 %collective-permute-start.22 = (f32[864,128]{1,0:T(8,128)S(1)}, f32[864,128]{1,0:T(8,128)S(1)}, u32[]{:S(2)}, u32[]{:S(2)}) collective-permute-start(f32[864,128]{1,0:T(8,128)S(1)} %get-tuple-element.45), channel_id=1, source_target_pairs={{0,72},{8,80},{16,88},{24,64},{32,104},{40,112},{48,120},{56,96},{... | collective-permute-start | bytes 1327112 | tf_op jit(solution)/shard_map/ppermute | solution.py:423
  92.2 32.9 %collective-permute-start.23 = (f32[864,128]{1,0:T(8,128)S(1)}, f32[864,128]{1,0:T(8,128)S(1)}, u32[]{:S(2)}, u32[]{:S(2)}) collective-permute-start(f32[864,128]{1,0:T(8,128)S(1)} %get-tuple-element.46), channel_id=1, source_target_pairs={{0,112},{8,120},{16,96},{24,104},{32,16},{40,24},{48,0},{56,8},{64... | collective-permute-start | bytes 1327112 | tf_op jit(solution)/shard_map/ppermute | solution.py:423
  99.4 38.6 %collective-permute-start.24 = (f32[864,128]{1,0:T(8,128)S(1)}, f32[864,128]{1,0:T(8,128)S(1)}, u32[]{:S(2)}, u32[]{:S(2)}) collective-permute-start(f32[864,128]{1,0:T(8,128)S(1)} %get-tuple-element.47), channel_id=1, source_target_pairs={{0,88},{8,64},{16,72},{24,80},{32,120},{40,96},{48,104},{56,112},{... | collective-permute-start | bytes 1327112 | tf_op jit(solution)/shard_map/ppermute | solution.py:423
  107.1 38.0 %collective-permute-start.18 = (f32[864,128]{1,0:T(8,128)S(1)}, f32[864,128]{1,0:T(8,128)S(1)}, u32[]{:S(2)}, u32[]{:S(2)}) collective-permute-start(f32[864,128]{1,0:T(8,128)S(1)} %get-tuple-element.41), channel_id=1, source_target_pairs={{0,120},{8,96},{16,104},{24,112},{32,24},{40,0},{48,8},{56,16},{64... | collective-permute-start | bytes 1327112 | tf_op jit(solution)/shard_map/ppermute | solution.py:423
  107.2 52.4 %collective-permute-start.19 = (f32[864,128]{1,0:T(8,128)S(1)}, f32[864,128]{1,0:T(8,128)S(1)}, u32[]{:S(2)}, u32[]{:S(2)}) collective-permute-start(f32[864,128]{1,0:T(8,128)S(1)} %get-tuple-element.42), channel_id=1, source_target_pairs={{0,56},{8,32},{16,40},{24,48},{32,88},{40,64},{48,72},{56,80},{64,... | collective-permute-start | bytes 1327112 | tf_op jit(solution)/shard_map/ppermute | solution.py:423
  117.1 71.3 %collective-permute-start.20 = (f32[864,128]{1,0:T(8,128)S(1)}, f32[864,128]{1,0:T(8,128)S(1)}, u32[]{:S(2)}, u32[]{:S(2)}) collective-permute-start(f32[864,128]{1,0:T(8,128)S(1)} %get-tuple-element.43), channel_id=1, source_target_pairs={{0,104},{8,112},{16,120},{24,96},{32,8},{40,16},{48,24},{56,0},{64... | collective-permute-start | bytes 1327112 | tf_op jit(solution)/shard_map/ppermute | solution.py:423
  125.1 75.6 %collective-permute-start.21 = (f32[864,128]{1,0:T(8,128)S(1)}, f32[864,128]{1,0:T(8,128)S(1)}, u32[]{:S(2)}, u32[]{:S(2)}) collective-permute-start(f32[864,128]{1,0:T(8,128)S(1)} %get-tuple-element.44), channel_id=1, source_target_pairs={{0,48},{8,56},{16,32},{24,40},{32,80},{40,88},{48,64},{56,72},{64,... | collective-permute-start | bytes 1327112 | tf_op jit(solution)/shard_map/ppermute | solution.py:423
  138.0 50.4 %copy-start.6 = (f32[864,128]{1,0:T(8,128)}, f32[864,128]{1,0:T(8,128)S(1)}, u32[]{:S(2)}) copy-start(f32[864,128]{1,0:T(8,128)S(1)} %collective-permute-done.24.refs_16_) | copy-start | bytes 1327108
  138.0 64.2 %collective-permute-start.14 = (f32[864,128]{1,0:T(8,128)S(1)}, f32[864,128]{1,0:T(8,128)S(1)}, u32[]{:S(2)}, u32[]{:S(2)}) collective-permute-start(f32[864,128]{1,0:T(8,128)S(1)} %get-tuple-element.37), channel_id=1, source_target_pairs={{0,80},{8,88},{16,64},{24,72},{32,112},{40,120},{48,96},{56,104},{... | collective-permute-start | bytes 1327112 | tf_op jit(solution)/shard_map/ppermute | solution.py:423
  145.1 57.1 %collective-permute-start.15 = (f32[864,128]{1,0:T(8,128)S(1)}, f32[864,128]{1,0:T(8,128)S(1)}, u32[]{:S(2)}, u32[]{:S(2)}) collective-permute-start(f32[864,128]{1,0:T(8,128)S(1)} %get-tuple-element.38), channel_id=1, source_target_pairs={{0,64},{8,72},{16,80},{24,88},{32,96},{40,104},{48,112},{56,120},{... | collective-permute-start | bytes 1327112 | tf_op jit(solution)/shard_map/ppermute | solution.py:423
  159.6 60.0 %collective-permute-start.16 = (f32[864,128]{1,0:T(8,128)S(1)}, f32[864,128]{1,0:T(8,128)S(1)}, u32[]{:S(2)}, u32[]{:S(2)}) collective-permute-start(f32[864,128]{1,0:T(8,128)S(1)} %get-tuple-element.39), channel_id=1, source_target_pairs={{0,16},{8,24},{16,0},{24,8},{32,48},{40,56},{48,32},{56,40},{64,80... | collective-permute-start | bytes 1327112 | tf_op jit(solution)/shard_map/ppermute | solution.py:423
  188.4 31.1 %collective-permute-start.17 = (f32[864,128]{1,0:T(8,128)S(1)}, f32[864,128]{1,0:T(8,128)S(1)}, u32[]{:S(2)}, u32[]{:S(2)}) collective-permute-start(f32[864,128]{1,0:T(8,128)S(1)} %get-tuple-element.40), channel_id=1, source_target_pairs={{0,40},{8,48},{16,56},{24,32},{32,72},{40,80},{48,88},{56,64},{64,... | collective-permute-start | bytes 1327112 | tf_op jit(solution)/shard_map/ppermute | solution.py:423
  200.7 19.6 %collective-permute-start.10 = (f32[864,128]{1,0:T(8,128)S(1)}, f32[864,128]{1,0:T(8,128)S(1)}, u32[]{:S(2)}, u32[]{:S(2)}) collective-permute-start(f32[864,128]{1,0:T(8,128)S(1)} %get-tuple-element.33), channel_id=1, source_target_pairs={{0,8},{8,16},{16,24},{24,0},{32,40},{40,48},{48,56},{56,32},{64,72... | collective-permute-start | bytes 1327112 | tf_op jit(solution)/shard_map/ppermute | solution.py:423
  202.3 18.1 %collective-permute-start.11 = (f32[864,128]{1,0:T(8,128)S(1)}, f32[864,128]{1,0:T(8,128)S(1)}, u32[]{:S(2)}, u32[]{:S(2)}) collective-permute-start(f32[864,128]{1,0:T(8,128)S(1)} %get-tuple-element.34), channel_id=1, source_target_pairs={{0,96},{8,104},{16,112},{24,120},{32,0},{40,8},{48,16},{56,24},{64... | collective-permute-start | bytes 1327112 | tf_op jit(solution)/shard_map/ppermute | solution.py:423
  202.3 21.4 %collective-permute-start.12 = (f32[864,128]{1,0:T(8,128)S(1)}, f32[864,128]{1,0:T(8,128)S(1)}, u32[]{:S(2)}, u32[]{:S(2)}) collective-permute-start(f32[864,128]{1,0:T(8,128)S(1)} %get-tuple-element.35), channel_id=1, source_target_pairs={{0,32},{8,40},{16,48},{24,56},{32,64},{40,72},{48,80},{56,88},{64,... | collective-permute-start | bytes 1327112 | tf_op jit(solution)/shard_map/ppermute | solution.py:423
  219.5 11.1 %collective-permute-start.13 = (f32[864,128]{1,0:T(8,128)S(1)}, f32[864,128]{1,0:T(8,128)S(1)}, u32[]{:S(2)}, u32[]{:S(2)}) collective-permute-start(f32[864,128]{1,0:T(8,128)S(1)} %get-tuple-element.36), channel_id=1, source_target_pairs={{0,24},{8,0},{16,8},{24,16},{32,56},{40,32},{48,40},{56,48},{64,88... | collective-permute-start | bytes 1327112 | tf_op jit(solution)/shard_map/ppermute | solution.py:423
where the time goes:
time: 235 us
  starting transfers between devices  128 us (54%)
  waiting for transfers between devices  68.3 us (29%)
  Pallas kernels  25.3 us (11%)
  blocking collectives  11 us (5%)
  local copies, waits for them, and re-layouts  2.76 us (1%)
    ppermute x15, starting transfers between devices, program(): v = lax.ppermute(v, 'gx', perm)  107 us
    ppermute x15, waiting for transfers between devices, program(): v = lax.ppermute(v, 'gx', perm)  28.4 us
    ppermute x2, waiting for transfers between devices, moved(): lax.ppermute(v, 'gx', [(i, (i + sx) % groups) for i in range(groups)])  22.6 us
    ppermute x4, starting transfers between devices, moved(): return lax.ppermute(v, ('gx', 'gz'), perm)  13.6 us
    all_to_all x1, blocking collectives, program(): lax.all_to_all(jnp.broadcast_to(frag_root[None], (groups, 3, slot)), 'gx'...  11 us
    ppermute x4, waiting for transfers between devices, moved(): return lax.ppermute(v, ('gx', 'gz'), perm)  9.25 us
    pallas_call x1, Pallas kernels, middle(): pl.pallas_call(mid_kernel, out_shape=jax.ShapeDtypeStruct((128, YPAD, 128...  6.8 us
    pallas_call x4, Pallas kernels, fields(): pl.pallas_call(kernel, out_shape=(out,) * n, in_specs=[smem, smem, vmem,...  6 us
  transfers between devices with their start and end apart: 25, of which 11 were waited for; matrix products, arithmetic and copies ran while one was open for 0% of the time, Pallas kernels for 5%

commit v1 on v0

--- a/solution.py
+++ b/solution.py
@@ -24,10 +24,9 @@
 SMEM = pltpu.SMEM
 
 GROUPS = (
-    ((0, 1), (3, 0), (1, 0), (0, 3)),
-    ((2, 2), (2, 0), (0, 2), (1, 1)),
-    ((3, 3), (1, 3), (3, 1), (1, 2)),
-    ((2, 1), (3, 2), (2, 3), (0, 0)),
+    ((1, 2), (3, 2), (2, 1), (2, 3)),
+    ((1, 1), (3, 3), (1, 3), (3, 1), (2, 2)),
+    ((0, 1), (0, 3), (1, 0), (3, 0), (0, 2), (2, 0), (0, 0)),
 )
 
 
@@ -48,36 +47,30 @@
     return pltpu.CompilerParams(vmem_limit_bytes=limit << 20)
 
 
-def pack_rows(p_ref, x0, n, side, i, lane):
+def pack_rows(p_ref, side, i, lane):
     base, first = (0, 40) if side == 0 else (128 - HALO, 0)
     rows = []
     for g in range(3):
-        v = p_ref[x0 + g * n + i]
+        v = p_ref[3 * i + g]
         shift = (first + HALO * g - base) % 128
         rows.append(pltpu.roll(v, shift, 1) if shift else v)
     at = jnp.where(lane < first, lane + 128 - first, lane - first)
     return jnp.where(at < HALO, rows[0], jnp.where(at < 2 * HALO, rows[1], rows[2]))
 
 
-def pack_kernel(p_ref, za, zb, lo_a, hi_a, lo_b, hi_b):
+def pack_kernel(p_ref, za, zb):
     lane = lax.broadcasted_iota(jnp.int32, (NY_LOCAL, 128), 1)
     for i in range(20):
-        za[i] = pack_rows(p_ref, 0, 20, 0, i, lane)
-        zb[i] = pack_rows(p_ref, 0, 20, 1, i, lane)
-    for i in range(12):
-        lo_a[i] = pack_rows(p_ref, 0, 12, 0, i, lane)
-        hi_a[i] = pack_rows(p_ref, 24, 12, 0, i, lane)
-        lo_b[i] = pack_rows(p_ref, 0, 12, 1, i, lane)
-        hi_b[i] = pack_rows(p_ref, 24, 12, 1, i, lane)
+        za[i, :NY_LOCAL] = pack_rows(p_ref, 0, i, lane)
+        zb[i, :NY_LOCAL] = pack_rows(p_ref, 1, i, lane)
 
 
 def pack(p):
-    big = jax.ShapeDtypeStruct((20, NY_LOCAL, 128), F32)
-    small = jax.ShapeDtypeStruct((12, NY_LOCAL, 128), F32)
+    big = jax.ShapeDtypeStruct((20, YPAD, 128), F32)
     return pl.pallas_call(
         pack_kernel,
-        out_shape=(big, big, small, small, small, small),
-        compiler_params=vm(),
+        out_shape=(big, big),
+        compiler_params=vm(16),
         name="pack",
     )(p)
 
@@ -107,48 +100,88 @@
         out_shape=jax.ShapeDtypeStruct((128, YPAD, 128), F32),
         in_specs=[pl.BlockSpec(memory_space=ANY)] * 4,
         scratch_shapes=[VMEM((128, NY_LOCAL, 128), F32), pltpu.SemaphoreType.DMA((3,))],
-        compiler_params=vm(),
+        compiler_params=vm(20),
         cost_estimate=cost(MID_COST),
         name="middle",
     )(before, own, after, packed)
 
 
-def halo_kernel(zb, za, lb, la, rb, ra, roots, out, x_ref):
+def halo_kernel(zb, za, left, right, roots, out, x_ref):
     lane = lax.broadcasted_iota(jnp.int32, (NY_LOCAL, 128), 1)
 
-    def place(b_ref, a_ref, i, g, row):
+    def place(b, a, g, row):
         mine = jnp.logical_and(lane >= HALO * g, lane < HALO * g + HALO)
-        v = jnp.where(mine, b_ref[i], a_ref[i])
+        v = jnp.where(mine, b, a)
         x_ref[row] = pltpu.roll(v, 128 - HALO * g, 1) if g else v
 
     for g in range(3):
         for i in range(20):
-            place(zb, za, i, g, HALO + 20 * g + i)
+            place(zb[i, :NY_LOCAL], za[i, :NY_LOCAL], g, HALO + 3 * i + g)
         for i in range(12):
-            x = 12 * g + i - 2
+            x = 3 * i + g - 2
             if x >= 0:
-                place(lb, la, i, g, x)
-            x = 12 * g + i
+                place(left[i, :NY_LOCAL], left[12 + i, :NY_LOCAL], g, x)
+            x = 3 * i + g
             if x < HALO:
-                place(rb, ra, i, g, HALO + 60 + x)
+                place(right[i, :NY_LOCAL], right[12 + i, :NY_LOCAL], g, HALO + 60 + x)
     turn(x_ref, out, 80)
 
 
-def halos(zb, za, lb, la, rb, ra, roots):
+def halos(zb, za, left, right, roots):
     return pl.pallas_call(
         halo_kernel,
         out_shape=jax.ShapeDtypeStruct((80, YPAD, 128), F32),
-        in_specs=[pl.BlockSpec(memory_space=VMEM)] * 6 + [pl.BlockSpec(memory_space=SMEM)],
+        in_specs=[pl.BlockSpec(memory_space=VMEM)] * 4 + [pl.BlockSpec(memory_space=SMEM)],
         scratch_shapes=[VMEM((128, NY_LOCAL, 128), F32)],
-        compiler_params=vm(),
+        compiler_params=vm(20),
         cost_estimate=cost(5),
         name="halos",
-    )(zb, za, lb, la, rb, ra, roots)
+    )(zb, za, left, right, roots)
 
 
 def split_rows(f):
     hi = f.astype(BF16).astype(F32)
     return jnp.concatenate([hi, f - hi], axis=0).astype(BF16)
+
+
+def both(own, part):
+    return split_rows(jnp.concatenate([own, part], axis=0))
+
+
+def join_mid_kernel(own, part, out):
+    def step(z, carry):
+        out[HALO + z] = both(own[z], part[z])
+        return carry
+
+    lax.fori_loop(0, 128, step, 0, unroll=4)
+
+
+def join_halo_kernel(full, own, part, out):
+    for z in range(HALO):
+        out[z] = both(own[z], part[z])
+        out[HALO + 128 + z] = both(own[40 + z], part[40 + z])
+
+
+def join_mid(own, part):
+    return pl.pallas_call(
+        join_mid_kernel,
+        out_shape=jax.ShapeDtypeStruct((128 + 2 * HALO, 4 * YPAD, 128), BF16),
+        compiler_params=vm(32),
+        cost_estimate=cost(2),
+        name="join_mid",
+    )(own, part)
+
+
+def join_halo(full, own, part):
+    return pl.pallas_call(
+        join_halo_kernel,
+        out_shape=jax.ShapeDtypeStruct(full.shape, full.dtype),
+        in_specs=[pl.BlockSpec(memory_space=ANY)] + [pl.BlockSpec(memory_space=VMEM)] * 2,
+        input_output_aliases={0: 0},
+        compiler_params=vm(32),
+        cost_estimate=cost(2),
+        name="join_halo",
+    )(full, own, part)
 
 
 def placed(table_hi, table_lo, hot):
@@ -182,10 +215,10 @@
     return ok, x0, y0, z0
 
 
-def field_kernel(shifts, sizes, slot, roots, place, thi, tlo, a2_ref, own_m, part_m, own_h, part_h, *rest):
+def field_kernel(shifts, sizes, slot, roots, place, thi, tlo, a2_ref, full, *rest):
     n = len(shifts)
     outs = rest[:n]
-    w_own, w_part, t1, t2, obuf, info, in_sems, out_sems = rest[n:]
+    t1, t2, obuf, info, sems = rest[n:]
     gx = place[0]
     py = gx // 4
     px = gx % 4
@@ -197,35 +230,9 @@
         info[1, j] = x0
         info[2, j] = y0
         info[3, j] = z0
-    info[0, n] = jnp.int32(0)
-
-    def copies(j, b):
-        z0 = info[3, j]
-        c = jnp.clip(z0 - HALO, 0, 128 - BOX)
-        for k, (src_m, src_h, w) in enumerate(((own_m, own_h, w_own), (part_m, part_h, w_part))):
-            yield None, pltpu.make_async_copy(
-                src_m.at[pl.ds(c, BOX)], w.at[b, pl.ds(HALO, BOX)], in_sems.at[b, 2 * k])
-            yield z0 < HALO, pltpu.make_async_copy(
-                src_h.at[pl.ds(0, HALO)], w.at[b, pl.ds(0, HALO)], in_sems.at[b, 2 * k + 1])
-            yield z0 > 128 - HALO, pltpu.make_async_copy(
-                src_h.at[pl.ds(40, HALO)], w.at[b, pl.ds(HALO + BOX, HALO)], in_sems.at[b, 2 * k + 1])
-
-    def begin(j, b):
-        for cond, c in copies(j, b):
-            if cond is None:
-                c.start()
-            else:
-                pl.when(cond)(c.start)
-
-    def finish(j, b):
-        for cond, c in copies(j, b):
-            if cond is None:
-                c.wait()
-            else:
-                pl.when(cond)(c.wait)
 
     def out_copy(k, b):
-        return pltpu.make_async_copy(obuf.at[b], outs[k], out_sems.at[b])
+        return pltpu.make_async_copy(obuf.at[b], outs[k], sems.at[b])
 
     for b in range(G):
         t1[b * 72 + 64:b * 72 + 72, :] = jnp.zeros((8, 128), F32)
@@ -234,7 +241,6 @@
         x0 = info[1, j]
         y0 = info[2, j]
         z0 = info[3, j]
-        zoff = z0 - jnp.clip(z0 - HALO, 0, 128 - BOX)
         k = lax.broadcasted_iota(jnp.int32, (128, 128), 0)
         col = lax.broadcasted_iota(jnp.int32, (128, 128), 1)
         half = col & 63
@@ -245,10 +251,7 @@
         a3 = placed(thi[...], tlo[...], k == col - x0)
         a2 = a2_ref[...]
         for p in range(BOX // 2):
-            z = zoff + 2 * p
-            own = jnp.concatenate([w_own[b, z], w_own[b, z + 1]], axis=1)
-            part = jnp.concatenate([w_part[b, z], w_part[b, z + 1]], axis=1)
-            rhs = split_rows(jnp.concatenate([own, part], axis=0))
+            rhs = jnp.concatenate([full[z0 + 2 * p], full[z0 + 2 * p + 1]], axis=1)
             t = folded(jnp.dot(a1, rhs, preferred_element_type=F32))
             t1[pl.ds(2 * p, G, stride=72), :] = t[:, :128]
             t1[pl.ds(2 * p + 1, G, stride=72), :] = t[:, 128:]
@@ -267,33 +270,34 @@
             obuf[b, pl.ds(2 * m, G, stride=18), :] = t[:, :128]
             obuf[b, pl.ds(2 * m + 1, G, stride=18), :] = t[:, 128:]
 
-    @pl.when(info[0, 0] == 1)
-    def _():
-        begin(0, 0)
+    def drain(j, b):
+        @pl.when(info[0, j] == 1)
+        def _():
+            out_copy(0, b).wait()
 
     def step(j, carry):
         b = lax.rem(j, 2)
 
-        @pl.when(info[0, j + 1] == 1)
+        @pl.when(j >= 2)
         def _():
-            begin(j + 1, 1 - b)
+            drain(j - 2, b)
 
         @pl.when(info[0, j] == 1)
         def _():
-            finish(j, b)
             compute(j, b)
             for k in range(n):
                 @pl.when(j == k)
                 def _(k=k):
                     out_copy(k, b).start()
-            out_copy(0, b).wait()
 
         return carry
 
     lax.fori_loop(0, n, step, 0)
-
-
-def fields(shifts, sizes, slot, roots, place, thi, tlo, a2, own_m, part_m, own_h, part_h):
+    drain(n - 2, (n - 2) % 2)
+    drain(n - 1, (n - 1) % 2)
+
+
+def fields(shifts, sizes, slot, roots, place, thi, tlo, a2, full):
     n = len(shifts)
     out = jax.ShapeDtypeStruct((ROWS, 128), F32)
     smem = pl.BlockSpec(memory_space=SMEM)
@@ -306,22 +310,19 @@
     return pl.pallas_call(
         kernel,
         out_shape=(out,) * n,
-        in_specs=[smem, smem, vmem, vmem, vmem, hbm, hbm, hbm, hbm],
+        in_specs=[smem, smem, vmem, vmem, vmem, vmem],
         out_specs=(hbm,) * n,
         scratch_shapes=[
-            VMEM((2, 2 * HALO + BOX, YPAD, 128), F32),
-            VMEM((2, 2 * HALO + BOX, YPAD, 128), F32),
             VMEM((G * 72, 128), F32),
             VMEM((G * G, 128), F32),
             VMEM((2, ROWS, 128), F32),
-            SMEM((4, n + 1), jnp.int32),
-            pltpu.SemaphoreType.DMA((2, 4)),
+            SMEM((4, n), jnp.int32),
             pltpu.SemaphoreType.DMA((2,)),
         ],
-        compiler_params=vm(),
+        compiler_params=vm(24),
         cost_estimate=cost(FIELD_COST * n),
         name="fields",
-    )(roots, place, thi, tlo, a2, own_m, part_m, own_h, part_h)
+    )(roots, place, thi, tlo, a2, full)
 
 
 def pick_kernel(order, sizes, slot, own_root, place, *rest):
@@ -357,7 +358,7 @@
         out_shape=jax.ShapeDtypeStruct((ROWS, slot, 128), F32),
         in_specs=[smem, smem] + [pl.BlockSpec(memory_space=ANY)] * 16,
         scratch_shapes=[VMEM((slot, ROWS, 128), F32), pltpu.SemaphoreType.DMA((slot,))],
-        compiler_params=vm(),
+        compiler_params=vm(8),
         name="pick",
     )(own_root, place, *parts)
 
@@ -370,26 +371,17 @@
     slot = frag_root.shape[1]
     place = jnp.stack([lax.axis_index("gx"), lax.axis_index("gy"), lax.axis_index("gz")]).astype(jnp.int32)
 
-    def moved(v, sx, sz):
-        if sz == 0:
-            return lax.ppermute(v, "gx", [(i, (i + sx) % groups) for i in range(groups)])
-        if sx == 0:
-            return lax.ppermute(v, "gz", [(i, (i + sz) % zs) for i in range(zs)])
-        perm = []
-        for i in range(groups):
-            for j in range(zs):
-                perm.append((i * zs + j, ((i + sx) % groups) * zs + (j + sz) % zs))
-        return lax.ppermute(v, ("gx", "gz"), perm)
-
-    before = moved(potential[bx - HALO:], 1, 0)
-    after = moved(potential[:HALO], -1, 0)
-    za, zb, lo_a, hi_a, lo_b, hi_b = pack(potential)
-    got_zb = moved(zb, 0, 1)
-    got_za = moved(za, 0, -1)
-    got_lb = moved(hi_b, 1, 1)
-    got_rb = moved(lo_b, -1, 1)
-    got_la = moved(hi_a, 1, -1)
-    got_ra = moved(lo_a, -1, -1)
+    def move(v, sx, sz):
+        axis, count, by = ("gx", groups, sx) if sx else ("gz", zs, sz)
+        return lax.ppermute(v, axis, [(i, (i + by) % count) for i in range(count)])
+
+    before = move(potential[bx - HALO:], 1, 0)
+    after = move(potential[:HALO], -1, 0)
+    za, zb = pack(potential)
+    got_zb = move(zb, 0, 1)
+    got_za = move(za, 0, -1)
+    left = move(jnp.concatenate([got_zb[8:], got_za[8:]], axis=0), 1, 0)
+    right = move(jnp.concatenate([got_zb[:12], got_za[:12]], axis=0), -1, 0)
     roots = lax.all_to_all(
         jnp.broadcast_to(frag_root[None], (groups, 3, slot)), "gx", 0, 0, tiled=True
     )
@@ -397,8 +389,10 @@
     swap = [(0, 1), (1, 0)]
     own_m = middle(before, potential, after, zb)
     part_m = lax.ppermute(own_m, "gy", swap)
-    own_h = halos(got_zb, got_za, got_lb, got_la, got_rb, got_ra, roots)
+    full = join_mid(own_m, part_m)
+    own_h = halos(got_zb, got_za, left, right, roots)
     part_h = lax.ppermute(own_h, "gy", swap)
+    full = join_halo(full, own_h, part_h)
 
     table = interp_matrix()
     hi = np.asarray(table.astype(BF16))
@@ -415,7 +409,7 @@
     order = []
     parts = []
     for shifts in GROUPS:
-        done = fields(shifts, sizes, slot, roots, place, thi, tlo, a2, own_m, part_m, own_h, part_h)
+        done = fields(shifts, sizes, slot, roots, place, thi, tlo, a2, full)
         for (dy, dx), v in zip(shifts, done):
             order.append((dy, dx))
             if (dy, dx) != (0, 0):

time: 235 us -> 210 us (0.89)
  the two profiles are of different devices: /device:TPU:75 before, /device:TPU:86 now
where the time goes in v1:
time: 210 us; the launch traced here: 209 us
  waiting for transfers between devices  95.3 us (45%)
  starting transfers between devices  58.1 us (28%)
  Pallas kernels  31.3 us (15%)
  blocking collectives  22.1 us (11%)
  local copies, waits for them, and re-layouts  2.12 us (1%)
    ppermute x15, waiting for transfers between devices, program(): v = lax.ppermute(v, 'gx', perm)  70.5 us
    ppermute x15, starting transfers between devices, program(): v = lax.ppermute(v, 'gx', perm)  51.7 us
    ppermute x6, waiting for transfers between devices, move(): return lax.ppermute(v, axis, [(i, (i + by) % count) for i in range(count)])  24 us
    all_to_all x1, blocking collectives, program(): lax.all_to_all(jnp.broadcast_to(frag_root[None], (groups, 3, slot)), 'gx'...  22.1 us
    pallas_call x1, Pallas kernels, halos(): pl.pallas_call(halo_kernel, out_shape=jax.ShapeDtypeStruct((80, YPAD, 128...  7.07 us
    pallas_call x1, Pallas kernels, middle(): pl.pallas_call(mid_kernel, out_shape=jax.ShapeDtypeStruct((128, YPAD, 128...  6.78 us
    ppermute x6, starting transfers between devices, move(): return lax.ppermute(v, axis, [(i, (i + by) % count) for i in range(count)])  6.35 us
    pallas_call x1, Pallas kernels, pick(): pl.pallas_call(kernel, out_shape=jax.ShapeDtypeStruct((ROWS, slot, 128),...  4.59 us
  transfers between devices with their start and end apart: 23, of which 9 were waited for; matrix products, arithmetic and copies ran while one was open for 0% of the time, Pallas kernels for 11%

profile of v1, /device:TPU:86, one launch (start us, length us, event | category | flops | bytes accessed | tf_op | source)
XLA Modules:
  0.0 209.5 jit_solution(8201564173611446169)
XLA Ops:
  0.0 1.9 fusion
  1.9 1.3 collective-permute-start
  3.2 0.8 collective-permute-start.1
  4.0 1.1 pack.1
  5.1 1.7 collective-permute-start.3
  6.8 0.4 collective-permute-start.4
  7.2 13.9 %collective-permute-done.3.zb = f32[20,64,128]{2,1,0:T(8,128)S(1)} collective-permute-done((f32[20,64,128]{2,1,0:T(8,128)S(1)}, f32[20,64,128]{2,1,0:T(8,128)S(1)}, u32[]{:S(2)}, u32[]{:S(2)}) %collective-permute-start.3) | collective-permute-done | bytes 655392 | tf_op jit(solution)/shard_map/ppermute | solution.py:376
  21.1 0.1 fusion.1
  21.2 7.1 %collective-permute-done.before = f32[34,60,128]{2,1,0:T(8,128)S(1)} collective-permute-done((f32[34,60,128]{2,1,0:T(8,128)S(1)}, f32[34,60,128]{2,1,0:T(8,128)S(1)}, u32[]{:S(2)}, u32[]{:S(2)}) %collective-permute-start) | collective-permute-done | bytes 1044512 | tf_op jit(solution)/shard_map/ppermute | solution.py:376
  28.3 3.0 %collective-permute-done.1.after = f32[34,60,128]{2,1,0:T(8,128)S(1)} collective-permute-done((f32[34,60,128]{2,1,0:T(8,128)S(1)}, f32[34,60,128]{2,1,0:T(8,128)S(1)}, u32[]{:S(2)}, u32[]{:S(2)}) %collective-permute-start.1) | collective-permute-done | bytes 1044512 | tf_op jit(solution)/shard_map/ppermute | solution.py:376
  31.3 6.8 %middle.1.own = f32[128,64,128]{2,1,0:T(8,128)} custom-call(f32[34,60,128]{2,1,0:T(8,128)S(1)} %collective-permute-done.before, f32[60,60,128]{2,1,0:T(8,128)S(1)} %copy-done, f32[34,60,128]{2,1,0:T(8,128)S(1)} %collective-permute-done.1.after, f32[20,64,128]{2,1,0:T(8,128)S(1)} %get-tuple-element.23.packed), custom_call_target="tpu_custom_call" | custom-call | flops 10000000000 | tf_op jit(solution)/shard_map/middle/pallas_call | solution.py:98
  38.1 0.1 collective-permute-start.2
  38.2 0.0 collective-permute-done.4.za
  38.2 0.1 fusion.2
  38.3 0.0 copy-start.1
  38.3 0.1 pad_maximum_fusion
  38.4 0.4 collective-permute-start.5
  38.8 0.1 pad_maximum_fusion.1
  38.8 1.8 collective-permute-start.6
  40.7 22.1 %all_to_all.5.roots.refs_0_ = s32[16,3,4]{2,1,0:T(4,128)S(1)} all-to-all(s32[16,3,4]{2,1,0:T(4,128)S(1)} %broadcast_in_dim.2), channel_id=1, replica_groups=mesh['gx'=16,'gy'=2,'gz'=4] {'gx'}, dimensions={0} | all-to-all | bytes 1536 | tf_op jit(solution)/shard_map/all_to_all | solution.py:385
  62.7 7.1 %halos.1.own = f32[80,64,128]{2,1,0:T(8,128)} custom-call(f32[20,64,128]{2,1,0:T(8,128)S(1)} %collective-permute-done.3.zb, f32[20,64,128]{2,1,0:T(8,128)S(1)} %collective-permute-done.4.za, f32[24,64,128]{2,1,0:T(8,128)S(1)} %collective-permute-done.5.left, f32[24,64,128]{2,1,0:T(8,128)S(1)} %collective-permute-done.6.right, ...), custom_call_target="tpu_custom_call" | custom-call | flops 5000000000 | tf_op jit(solution)/shard_map/halos/pallas_call | solution.py:131
  69.8 0.1 pad_add_fusion.refs_1_
  69.9 4.4 %join_mid.1.full = bf16[196,256,128]{2,1,0:T(8,128)(2,1)S(1)} custom-call(f32[128,64,128]{2,1,0:T(8,128)} %middle.1.own, f32[128,64,128]{2,1,0:T(8,128)} %collective-permute-done.2.part), custom_call_target="tpu_custom_call" | custom-call | flops 2000000000 | tf_op jit(solution)/shard_map/join_mid/pallas_call | solution.py:166
  74.3 0.0 copy-start.2
  74.3 0.0 copy-start.3
  74.4 0.0 copy-start.4
  74.4 0.7 collective-permute-done.7.part
  75.1 3.0 %join_halo.1.refs_5_ = bf16[196,256,128]{2,1,0:T(8,128)(2,1)S(1)} custom-call(bf16[196,256,128]{2,1,0:T(8,128)(2,1)S(1)} %join_mid.1.full, f32[80,64,128]{2,1,0:T(8,128)} %halos.1.own, f32[80,64,128]{2,1,0:T(8,128)} %collective-permute-done.7.part), custom_call_target="tpu_custom_call", output_to_operand_aliasing={{}: (0, {})} | custom-call | flops 2000000000 | tf_op jit(solution)/shard_map/join_halo/pallas_call | solution.py:176
  78.1 1.6 fields.5
  79.7 6.2 %collective-permute-start.17 = (f32[864,128]{1,0:T(8,128)S(1)}, f32[864,128]{1,0:T(8,128)S(1)}, u32[]{:S(2)}, u32[]{:S(2)}) collective-permute-start(f32[864,128]{1,0:T(8,128)S(1)} %get-tuple-element.34), channel_id=1, source_target_pairs={{0,8},{8,16},{16,24},{24,0},{32,40},{40,48},{48,56},{56,32},{64,72... | collective-permute-start | bytes 1327112 | tf_op jit(solution)/shard_map/ppermute | solution.py:417
  85.8 1.6 collective-permute-start.18
  87.4 4.2 %collective-permute-start.19 = (f32[864,128]{1,0:T(8,128)S(1)}, f32[864,128]{1,0:T(8,128)S(1)}, u32[]{:S(2)}, u32[]{:S(2)}) collective-permute-start(f32[864,128]{1,0:T(8,128)S(1)} %get-tuple-element.36), channel_id=1, source_target_pairs={{0,32},{8,40},{16,48},{24,56},{32,64},{40,72},{48,80},{56,88},{64,... | collective-permute-start | bytes 1327112 | tf_op jit(solution)/shard_map/ppermute | solution.py:417
  91.5 1.4 fields.4
  93.0 4.8 %collective-permute-done.17.refs_11_ = f32[864,128]{1,0:T(8,128)S(1)} collective-permute-done((f32[864,128]{1,0:T(8,128)S(1)}, f32[864,128]{1,0:T(8,128)S(1)}, u32[]{:S(2)}, u32[]{:S(2)}) %collective-permute-start.17) | collective-permute-done | bytes 442400 | tf_op jit(solution)/shard_map/ppermute | solution.py:417
  97.7 10.8 %collective-permute-start.22 = (f32[864,128]{1,0:T(8,128)S(1)}, f32[864,128]{1,0:T(8,128)S(1)}, u32[]{:S(2)}, u32[]{:S(2)}) collective-permute-start(f32[864,128]{1,0:T(8,128)S(1)} %get-tuple-element.39), channel_id=1, source_target_pairs={{0,64},{8,72},{16,80},{24,88},{32,96},{40,104},{48,112},{56,120},{... | collective-permute-start | bytes 1327112 | tf_op jit(solution)/shard_map/ppermute | solution.py:417
  108.5 3.1 %collective-permute-start.12 = (f32[864,128]{1,0:T(8,128)S(1)}, f32[864,128]{1,0:T(8,128)S(1)}, u32[]{:S(2)}, u32[]{:S(2)}) collective-permute-start(f32[864,128]{1,0:T(8,128)S(1)} %get-tuple-element.29), channel_id=1, source_target_pairs={{0,40},{8,48},{16,56},{24,32},{32,72},{40,80},{48,88},{56,64},{64,... | collective-permute-start | bytes 1327112 | tf_op jit(solution)/shard_map/ppermute | solution.py:417
  111.7 11.0 %collective-permute-start.14 = (f32[864,128]{1,0:T(8,128)S(1)}, f32[864,128]{1,0:T(8,128)S(1)}, u32[]{:S(2)}, u32[]{:S(2)}) collective-permute-start(f32[864,128]{1,0:T(8,128)S(1)} %get-tuple-element.31), channel_id=1, source_target_pairs={{0,56},{8,32},{16,40},{24,48},{32,88},{40,64},{48,72},{56,80},{64,... | collective-permute-start | bytes 1327112 | tf_op jit(solution)/shard_map/ppermute | solution.py:417
  122.7 0.0 collective-permute-start.15
  122.7 1.4 fields.3
  124.1 14.3 %collective-permute-done.22.refs_16_ = f32[864,128]{1,0:T(8,128)S(1)} collective-permute-done((f32[864,128]{1,0:T(8,128)S(1)}, f32[864,128]{1,0:T(8,128)S(1)}, u32[]{:S(2)}, u32[]{:S(2)}) %collective-permute-start.22) | collective-permute-done | bytes 442400 | tf_op jit(solution)/shard_map/ppermute | solution.py:417
  138.4 6.0 %collective-permute-start.16 = (f32[864,128]{1,0:T(8,128)S(1)}, f32[864,128]{1,0:T(8,128)S(1)}, u32[]{:S(2)}, u32[]{:S(2)}) collective-permute-start(f32[864,128]{1,0:T(8,128)S(1)} %get-tuple-element.33), channel_id=1, source_target_pairs={{0,80},{8,88},{16,64},{24,72},{32,112},{40,120},{48,96},{56,104},{... | collective-permute-start | bytes 1327112 | tf_op jit(solution)/shard_map/ppermute | solution.py:417
  144.4 2.1 collective-permute-start.10
  146.5 2.3 %collective-permute-start.11 = (f32[864,128]{1,0:T(8,128)S(1)}, f32[864,128]{1,0:T(8,128)S(1)}, u32[]{:S(2)}, u32[]{:S(2)}) collective-permute-start(f32[864,128]{1,0:T(8,128)S(1)} %get-tuple-element.28), channel_id=1, source_target_pairs={{0,88},{8,64},{16,72},{24,80},{32,120},{40,96},{48,104},{56,112},{... | collective-permute-start | bytes 1327112 | tf_op jit(solution)/shard_map/ppermute | solution.py:417
  148.8 4.4 %collective-permute-start.9 = (f32[864,128]{1,0:T(8,128)S(1)}, f32[864,128]{1,0:T(8,128)S(1)}, u32[]{:S(2)}, u32[]{:S(2)}) collective-permute-start(f32[864,128]{1,0:T(8,128)S(1)} %get-tuple-element.26), channel_id=1, source_target_pairs={{0,112},{8,120},{16,96},{24,104},{32,16},{40,24},{48,0},{56,8},{64... | collective-permute-start | bytes 1327112 | tf_op jit(solution)/shard_map/ppermute | solution.py:417
  153.3 15.5 %collective-permute-done.16.refs_10_ = f32[864,128]{1,0:T(8,128)S(1)} collective-permute-done((f32[864,128]{1,0:T(8,128)S(1)}, f32[864,128]{1,0:T(8,128)S(1)}, u32[]{:S(2)}, u32[]{:S(2)}) %collective-permute-start.16) | collective-permute-done | bytes 442400 | tf_op jit(solution)/shard_map/ppermute | solution.py:417
  168.8 13.3 %collective-permute-done.10.refs_4_ = f32[864,128]{1,0:T(8,128)S(1)} collective-permute-done((f32[864,128]{1,0:T(8,128)S(1)}, f32[864,128]{1,0:T(8,128)S(1)}, u32[]{:S(2)}, u32[]{:S(2)}) %collective-permute-start.10) | collective-permute-done | bytes 442400 | tf_op jit(solution)/shard_map/ppermute | solution.py:417
  182.0 22.7 %collective-permute-done.11.refs_5_ = f32[864,128]{1,0:T(8,128)S(1)} collective-permute-done((f32[864,128]{1,0:T(8,128)S(1)}, f32[864,128]{1,0:T(8,128)S(1)}, u32[]{:S(2)}, u32[]{:S(2)}) %collective-permute-start.11) | collective-permute-done | bytes 442400 | tf_op jit(solution)/shard_map/ppermute | solution.py:417
  204.7 4.6 %pick.1 = f32[864,4,128]{2,1,0:T(4,128)} custom-call(s32[3,4]{1,0:T(4,128)S(1)} %copy-done.1, s32[3]{0:T(128)S(1)} %pad_add_fusion.refs_1_, f32[864,128]{1,0:T(8,128)S(1)} %collective-permute-done.8.refs_2_, f32[864,128]{1,0:T(8,128)S(1)} %collective-permute-done.9.refs_3_, f32[864,128]{1,0:T(8,128)S(1)} %collective-permute-done.10.refs_4_, ...), custom_call_target="tpu_custom_call" | custom-call | tf_op jit(solution)/shard_map/pick/pallas_call | solution.py:356
  (25 shorter events, 0.1 us)
Async XLA Ops:
  0.0 4.0 %copy-start = (f32[60,60,128]{2,1,0:T(8,128)S(1)}, f32[60,60,128]{2,1,0:T(8,128)}, u32[]{:S(2)}) copy-start(f32[60,60,128]{2,1,0:T(8,128)} %own.1) | copy-start | bytes 5529604
  1.9 26.4 %collective-permute-start = (f32[34,60,128]{2,1,0:T(8,128)S(1)}, f32[34,60,128]{2,1,0:T(8,128)S(1)}, u32[]{:S(2)}, u32[]{:S(2)}) collective-permute-start(f32[34,60,128]{2,1,0:T(8,128)S(1)} %get-tuple-element.42), channel_id=1, source_target_pairs={{0,8},{8,16},{16,24},{24,32},{32,40},{40,48},{48,56},{56,64},{64,7... | collective-permute-start | bytes 3133448 | tf_op jit(solution)/shard_map/ppermute | solution.py:376
  3.2 28.1 %collective-permute-start.1 = (f32[34,60,128]{2,1,0:T(8,128)S(1)}, f32[34,60,128]{2,1,0:T(8,128)S(1)}, u32[]{:S(2)}, u32[]{:S(2)}) collective-permute-start(f32[34,60,128]{2,1,0:T(8,128)S(1)} %get-tuple-element.41), channel_id=1, source_target_pairs={{0,120},{8,0},{16,8},{24,16},{32,24},{40,32},{48,40},{56,48},{64,5... | collective-permute-start | bytes 3133448 | tf_op jit(solution)/shard_map/ppermute | solution.py:376
  5.1 16.0 %collective-permute-start.3 = (f32[20,64,128]{2,1,0:T(8,128)S(1)}, f32[20,64,128]{2,1,0:T(8,128)S(1)}, u32[]{:S(2)}, u32[]{:S(2)}) collective-permute-start(f32[20,64,128]{2,1,0:T(8,128)S(1)} %get-tuple-element.23.packed), channel_id=1, source_target_pairs={{0,1},{1,2},{2,3},{3,0},{4,5},{5,6},{6,7},{7,4},{8,9},{9,10},{10,1... | collective-permute-start | bytes 1966088 | tf_op jit(solution)/shard_map/ppermute | solution.py:376
  6.8 31.4 %collective-permute-start.4 = (f32[20,64,128]{2,1,0:T(8,128)S(1)}, f32[20,64,128]{2,1,0:T(8,128)S(1)}, u32[]{:S(2)}, u32[]{:S(2)}) collective-permute-start(f32[20,64,128]{2,1,0:T(8,128)S(1)} %get-tuple-element.24), channel_id=1, source_target_pairs={{0,3},{1,0},{2,1},{3,2},{4,7},{5,4},{6,5},{7,6},{8,11},{9,8},{10,9... | collective-permute-start | bytes 1966088 | tf_op jit(solution)/shard_map/ppermute | solution.py:376
  38.1 31.8 %collective-permute-start.2 = (f32[128,64,128]{2,1,0:T(8,128)}, f32[128,64,128]{2,1,0:T(8,128)}, u32[]{:S(2)}, u32[]{:S(2)}) collective-permute-start(f32[128,64,128]{2,1,0:T(8,128)} %middle.1.own), channel_id=1, source_target_pairs={{0,4},{4,0},{1,5},{5,1},{2,6},{6,2},{3,7},{7,3},{8,12},{12,8},{9,1... | collective-permute-start | bytes 12582920 | tf_op jit(solution)/shard_map/ppermute | solution.py:391
  38.3 2.3 %copy-start.1 = (s32[3,4]{1,0:T(4,128)S(1)}, s32[3,4]{1,0:T(4,128)}, u32[]{:S(2)}) copy-start(s32[3,4]{1,0:T(4,128)} %refs_0_.1) | copy-start | bytes 148
  38.4 24.3 %collective-permute-start.5 = (f32[24,64,128]{2,1,0:T(8,128)S(1)}, f32[24,64,128]{2,1,0:T(8,128)S(1)}, u32[]{:S(2)}, u32[]{:S(2)}) collective-permute-start(f32[24,64,128]{2,1,0:T(8,128)S(1)} %pad_maximum_fusion), channel_id=1, source_target_pairs={{0,8},{8,16},{16,24},{24,32},{32,40},{40,48},{48,56},{56,64},{64,7... | collective-permute-start | bytes 2359304 | tf_op jit(solution)/shard_map/ppermute | solution.py:376
  38.8 23.9 %collective-permute-start.6 = (f32[24,64,128]{2,1,0:T(8,128)S(1)}, f32[24,64,128]{2,1,0:T(8,128)S(1)}, u32[]{:S(2)}, u32[]{:S(2)}) collective-permute-start(f32[24,64,128]{2,1,0:T(8,128)S(1)} %pad_maximum_fusion.1), channel_id=1, source_target_pairs={{0,120},{8,0},{16,8},{24,16},{32,24},{40,32},{48,40},{56,48},{64,5... | collective-permute-start | bytes 2359304 | tf_op jit(solution)/shard_map/ppermute | solution.py:376
  69.8 5.3 %collective-permute-start.7 = (f32[80,64,128]{2,1,0:T(8,128)}, f32[80,64,128]{2,1,0:T(8,128)}, u32[]{:S(2)}, u32[]{:S(2)}) collective-permute-start(f32[80,64,128]{2,1,0:T(8,128)} %halos.1.own), channel_id=1, source_target_pairs={{0,4},{4,0},{1,5},{5,1},{2,6},{6,2},{3,7},{7,3},{8,12},{12,8},{9,1... | collective-permute-start | bytes 7864328 | tf_op jit(solution)/shard_map/ppermute | solution.py:394
  74.3 3.7 %copy-start.2 = (bf16[96,144]{1,0:T(8,128)(2,1)S(1)}, bf16[96,144]{1,0:T(8,128)(2,1)}, u32[]{:S(2)}) copy-start(bf16[96,144]{1,0:T(8,128)(2,1)} %constant.22.clone.refs_4_) | copy-start | bytes 82948
  74.3 3.7 %copy-start.3 = (bf16[48,128]{1,0:T(8,128)(2,1)S(1)}, bf16[48,128]{1,0:T(8,128)(2,1)}, u32[]{:S(2)}) copy-start(bf16[48,128]{1,0:T(8,128)(2,1)} %constant.20.clone.refs_2_) | copy-start | bytes 36868
  74.4 3.7 %copy-start.4 = (bf16[48,128]{1,0:T(8,128)(2,1)S(1)}, bf16[48,128]{1,0:T(8,128)(2,1)}, u32[]{:S(2)}) copy-start(bf16[48,128]{1,0:T(8,128)(2,1)} %constant.21.clone.refs_3_) | copy-start | bytes 36868
  79.7 18.1 %collective-permute-start.17 = (f32[864,128]{1,0:T(8,128)S(1)}, f32[864,128]{1,0:T(8,128)S(1)}, u32[]{:S(2)}, u32[]{:S(2)}) collective-permute-start(f32[864,128]{1,0:T(8,128)S(1)} %get-tuple-element.34), channel_id=1, source_target_pairs={{0,8},{8,16},{16,24},{24,0},{32,40},{40,48},{48,56},{56,32},{64,72... | collective-permute-start | bytes 1327112 | tf_op jit(solution)/shard_map/ppermute | solution.py:417
  85.8 22.7 %collective-permute-start.18 = (f32[864,128]{1,0:T(8,128)S(1)}, f32[864,128]{1,0:T(8,128)S(1)}, u32[]{:S(2)}, u32[]{:S(2)}) collective-permute-start(f32[864,128]{1,0:T(8,128)S(1)} %get-tuple-element.35), channel_id=1, source_target_pairs={{0,24},{8,0},{16,8},{24,16},{32,56},{40,32},{48,40},{56,48},{64,88... | collective-permute-start | bytes 1327112 | tf_op jit(solution)/shard_map/ppermute | solution.py:417
  87.4 24.3 %collective-permute-start.19 = (f32[864,128]{1,0:T(8,128)S(1)}, f32[864,128]{1,0:T(8,128)S(1)}, u32[]{:S(2)}, u32[]{:S(2)}) collective-permute-start(f32[864,128]{1,0:T(8,128)S(1)} %get-tuple-element.36), channel_id=1, source_target_pairs={{0,32},{8,40},{16,48},{24,56},{32,64},{40,72},{48,80},{56,88},{64,... | collective-permute-start | bytes 1327112 | tf_op jit(solution)/shard_map/ppermute | solution.py:417
  91.5 20.2 %collective-permute-start.20 = (f32[864,128]{1,0:T(8,128)S(1)}, f32[864,128]{1,0:T(8,128)S(1)}, u32[]{:S(2)}, u32[]{:S(2)}) collective-permute-start(f32[864,128]{1,0:T(8,128)S(1)} %get-tuple-element.37), channel_id=1, source_target_pairs={{0,96},{8,104},{16,112},{24,120},{32,0},{40,8},{48,16},{56,24},{64... | collective-permute-start | bytes 1327112 | tf_op jit(solution)/shard_map/ppermute | solution.py:417
  91.5 31.2 %collective-permute-start.21 = (f32[864,128]{1,0:T(8,128)S(1)}, f32[864,128]{1,0:T(8,128)S(1)}, u32[]{:S(2)}, u32[]{:S(2)}) collective-permute-start(f32[864,128]{1,0:T(8,128)S(1)} %get-tuple-element.38), channel_id=1, source_target_pairs={{0,16},{8,24},{16,0},{24,8},{32,48},{40,56},{48,32},{56,40},{64,80... | collective-permute-start | bytes 1327112 | tf_op jit(solution)/shard_map/ppermute | solution.py:417
  97.7 40.6 %collective-permute-start.22 = (f32[864,128]{1,0:T(8,128)S(1)}, f32[864,128]{1,0:T(8,128)S(1)}, u32[]{:S(2)}, u32[]{:S(2)}) collective-permute-start(f32[864,128]{1,0:T(8,128)S(1)} %get-tuple-element.39), channel_id=1, source_target_pairs={{0,64},{8,72},{16,80},{24,88},{32,96},{40,104},{48,112},{56,120},{... | collective-permute-start | bytes 1327112 | tf_op jit(solution)/shard_map/ppermute | solution.py:417
  108.5 35.8 %collective-permute-start.12 = (f32[864,128]{1,0:T(8,128)S(1)}, f32[864,128]{1,0:T(8,128)S(1)}, u32[]{:S(2)}, u32[]{:S(2)}) collective-permute-start(f32[864,128]{1,0:T(8,128)S(1)} %get-tuple-element.29), channel_id=1, source_target_pairs={{0,40},{8,48},{16,56},{24,32},{32,72},{40,80},{48,88},{56,64},{64,... | collective-permute-start | bytes 1327112 | tf_op jit(solution)/shard_map/ppermute | solution.py:417
  111.7 34.8 %collective-permute-start.13 = (f32[864,128]{1,0:T(8,128)S(1)}, f32[864,128]{1,0:T(8,128)S(1)}, u32[]{:S(2)}, u32[]{:S(2)}) collective-permute-start(f32[864,128]{1,0:T(8,128)S(1)} %get-tuple-element.30), channel_id=1, source_target_pairs={{0,120},{8,96},{16,104},{24,112},{32,24},{40,0},{48,8},{56,16},{64... | collective-permute-start | bytes 1327112 | tf_op jit(solution)/shard_map/ppermute | solution.py:417
  111.7 37.2 %collective-permute-start.14 = (f32[864,128]{1,0:T(8,128)S(1)}, f32[864,128]{1,0:T(8,128)S(1)}, u32[]{:S(2)}, u32[]{:S(2)}) collective-permute-start(f32[864,128]{1,0:T(8,128)S(1)} %get-tuple-element.31), channel_id=1, source_target_pairs={{0,56},{8,32},{16,40},{24,48},{32,88},{40,64},{48,72},{56,80},{64,... | collective-permute-start | bytes 1327112 | tf_op jit(solution)/shard_map/ppermute | solution.py:417
  122.7 26.1 %collective-permute-start.15 = (f32[864,128]{1,0:T(8,128)S(1)}, f32[864,128]{1,0:T(8,128)S(1)}, u32[]{:S(2)}, u32[]{:S(2)}) collective-permute-start(f32[864,128]{1,0:T(8,128)S(1)} %get-tuple-element.32), channel_id=1, source_target_pairs={{0,104},{8,112},{16,120},{24,96},{32,8},{40,16},{48,24},{56,0},{64... | collective-permute-start | bytes 1327112 | tf_op jit(solution)/shard_map/ppermute | solution.py:417
  138.4 30.4 %collective-permute-start.16 = (f32[864,128]{1,0:T(8,128)S(1)}, f32[864,128]{1,0:T(8,128)S(1)}, u32[]{:S(2)}, u32[]{:S(2)}) collective-permute-start(f32[864,128]{1,0:T(8,128)S(1)} %get-tuple-element.33), channel_id=1, source_target_pairs={{0,80},{8,88},{16,64},{24,72},{32,112},{40,120},{48,96},{56,104},{... | collective-permute-start | bytes 1327112 | tf_op jit(solution)/shard_map/ppermute | solution.py:417
  144.4 37.7 %collective-permute-start.10 = (f32[864,128]{1,0:T(8,128)S(1)}, f32[864,128]{1,0:T(8,128)S(1)}, u32[]{:S(2)}, u32[]{:S(2)}) collective-permute-start(f32[864,128]{1,0:T(8,128)S(1)} %get-tuple-element.27), channel_id=1, source_target_pairs={{0,72},{8,80},{16,88},{24,64},{32,104},{40,112},{48,120},{56,96},{... | collective-permute-start | bytes 1327112 | tf_op jit(solution)/shard_map/ppermute | solution.py:417
  146.5 58.2 %collective-permute-start.11 = (f32[864,128]{1,0:T(8,128)S(1)}, f32[864,128]{1,0:T(8,128)S(1)}, u32[]{:S(2)}, u32[]{:S(2)}) collective-permute-start(f32[864,128]{1,0:T(8,128)S(1)} %get-tuple-element.28), channel_id=1, source_target_pairs={{0,88},{8,64},{16,72},{24,80},{32,120},{40,96},{48,104},{56,112},{... | collective-permute-start | bytes 1327112 | tf_op jit(solution)/shard_map/ppermute | solution.py:417
  148.8 55.9 %collective-permute-start.8 = (f32[864,128]{1,0:T(8,128)S(1)}, f32[864,128]{1,0:T(8,128)S(1)}, u32[]{:S(2)}, u32[]{:S(2)}) collective-permute-start(f32[864,128]{1,0:T(8,128)S(1)} %get-tuple-element.25), channel_id=1, source_target_pairs={{0,48},{8,56},{16,32},{24,40},{32,80},{40,88},{48,64},{56,72},{64,... | collective-permute-start | bytes 1327112 | tf_op jit(solution)/shard_map/ppermute | solution.py:417
  148.8 55.9 %collective-permute-start.9 = (f32[864,128]{1,0:T(8,128)S(1)}, f32[864,128]{1,0:T(8,128)S(1)}, u32[]{:S(2)}, u32[]{:S(2)}) collective-permute-start(f32[864,128]{1,0:T(8,128)S(1)} %get-tuple-element.26), channel_id=1, source_target_pairs={{0,112},{8,120},{16,96},{24,104},{32,16},{40,24},{48,0},{56,8},{64... | collective-permute-start | bytes 1327112 | tf_op jit(solution)/shard_map/ppermute | solution.py:417

commit v2 on v1

--- a/solution.py
+++ b/solution.py
@@ -14,6 +14,7 @@
 HALO = 34
 NY_LOCAL = 60
 YPAD = 64
+YSTEP = 72
 ROWS = G * G * G // 128
 F32 = jnp.float32
 BF16 = jnp.bfloat16
@@ -24,7 +25,8 @@
 SMEM = pltpu.SMEM
 
 GROUPS = (
-    ((1, 2), (3, 2), (2, 1), (2, 3)),
+    ((1, 2), (3, 2)),
+    ((2, 1), (2, 3)),
     ((1, 1), (3, 3), (1, 3), (3, 1), (2, 2)),
     ((0, 1), (0, 3), (1, 0), (3, 0), (0, 2), (2, 0), (0, 0)),
 )
@@ -76,34 +78,38 @@
 
 
 def turn(src, out, count):
-    for y in range(NY_LOCAL):
-        out[:, y, :] = src[:, y, :].T[:count]
-    out[:, NY_LOCAL:, :] = jnp.zeros((count, YPAD - NY_LOCAL, 128), F32)
-
-
-def mid_kernel(before, own, after, packed, out, x_ref, sems):
-    copies = [
-        pltpu.make_async_copy(before, x_ref.at[pl.ds(0, HALO)], sems.at[0]),
-        pltpu.make_async_copy(own, x_ref.at[pl.ds(HALO, 60)], sems.at[1]),
-        pltpu.make_async_copy(after, x_ref.at[pl.ds(HALO + 60, HALO)], sems.at[2]),
-    ]
-    for c in copies:
-        c.start()
-    for c in copies:
-        c.wait()
+    r = lax.broadcasted_iota(jnp.int32, (count, 256), 0)
+    c = lax.broadcasted_iota(jnp.int32, (count, 256), 1) & 127
+    pick_z = jnp.where(r == c, 1.0, 0.0).astype(BF16)
+    for y in range(0, NY_LOCAL, 2):
+        m = jnp.concatenate([src[pl.ds(y + k, 128, stride=YSTEP), :] for k in range(2)], axis=0)
+        hi = m.astype(BF16)
+        lo = (m - hi.astype(F32)).astype(BF16)
+        pair = jnp.concatenate([hi, lo], axis=1)
+        t = lax.dot_general(pick_z, pair, (((1,), (1,)), ((), ())), preferred_element_type=F32)
+        out[pl.ds(y, count, stride=YSTEP), :] = t[:, :128]
+        out[pl.ds(y + 1, count, stride=YSTEP), :] = t[:, 128:]
+    for y in range(NY_LOCAL, YPAD):
+        out[pl.ds(y, count, stride=YSTEP), :] = jnp.zeros((count, 128), F32)
+
+
+def mid_kernel(before, own, after, packed, out, x_ref):
+    for ref, first, n in ((before, 0, HALO), (own, HALO, 60), (after, HALO + 60, HALO)):
+        for i in range(n):
+            x_ref[pl.ds(YSTEP * (first + i), NY_LOCAL), :] = ref[i]
     turn(x_ref, out, 128)
 
 
 def middle(before, own, after, packed):
     return pl.pallas_call(
         mid_kernel,
-        out_shape=jax.ShapeDtypeStruct((128, YPAD, 128), F32),
-        in_specs=[pl.BlockSpec(memory_space=ANY)] * 4,
-        scratch_shapes=[VMEM((128, NY_LOCAL, 128), F32), pltpu.SemaphoreType.DMA((3,))],
+        out_shape=jax.ShapeDtypeStruct((128 * YSTEP, 128), F32),
+        in_specs=[pl.BlockSpec(memory_space=VMEM)] * 3 + [pl.BlockSpec(memory_space=ANY)],
+        scratch_shapes=[VMEM((128 * YSTEP, 128), F32)],
         compiler_params=vm(20),
         cost_estimate=cost(MID_COST),
         name="middle",
-    )(before, own, after, packed)
+    )(before, own, after, packed).reshape(128, YSTEP, 128)
 
 
 def halo_kernel(zb, za, left, right, roots, out, x_ref):
@@ -112,7 +118,7 @@
     def place(b, a, g, row):
         mine = jnp.logical_and(lane >= HALO * g, lane < HALO * g + HALO)
         v = jnp.where(mine, b, a)
-        x_ref[row] = pltpu.roll(v, 128 - HALO * g, 1) if g else v
+        x_ref[pl.ds(YSTEP * row, NY_LOCAL), :] = pltpu.roll(v, 128 - HALO * g, 1) if g else v
 
     for g in range(3):
         for i in range(20):
@@ -130,13 +136,13 @@
 def halos(zb, za, left, right, roots):
     return pl.pallas_call(
         halo_kernel,
-        out_shape=jax.ShapeDtypeStruct((80, YPAD, 128), F32),
+        out_shape=jax.ShapeDtypeStruct((80 * YSTEP, 128), F32),
         in_specs=[pl.BlockSpec(memory_space=VMEM)] * 4 + [pl.BlockSpec(memory_space=SMEM)],
-        scratch_shapes=[VMEM((128, NY_LOCAL, 128), F32)],
+        scratch_shapes=[VMEM((128 * YSTEP, 128), F32)],
         compiler_params=vm(20),
         cost_estimate=cost(5),
         name="halos",
-    )(zb, za, left, right, roots)
+    )(zb, za, left, right, roots).reshape(80, YSTEP, 128)
 
 
 def split_rows(f):
@@ -150,7 +156,7 @@
 
 def join_mid_kernel(own, part, out):
     def step(z, carry):
-        out[HALO + z] = both(own[z], part[z])
+        out[HALO + z] = both(own[z, :YPAD], part[z, :YPAD])
         return carry
 
     lax.fori_loop(0, 128, step, 0, unroll=4)
@@ -158,8 +164,8 @@
 
 def join_halo_kernel(full, own, part, out):
     for z in range(HALO):
-        out[z] = both(own[z], part[z])
-        out[HALO + 128 + z] = both(own[40 + z], part[40 + z])
+        out[z] = both(own[z, :YPAD], part[z, :YPAD])
+        out[HALO + 128 + z] = both(own[40 + z, :YPAD], part[40 + z, :YPAD])
 
 
 def join_mid(own, part):
@@ -344,7 +350,7 @@
                 pltpu.make_async_copy(srcs[k], buf.at[s], sems.at[s]).start()
     for s in range(slot):
         pltpu.make_async_copy(srcs[0], buf.at[s], sems.at[s]).wait()
-        out[:, s, :] = buf[s]
+        out[pl.ds(s, ROWS, stride=slot), :] = buf[s]
 
 
 def pick(order, sizes, slot, own_root, place, parts):
@@ -355,7 +361,7 @@
 
     return pl.pallas_call(
         kernel,
-        out_shape=jax.ShapeDtypeStruct((ROWS, slot, 128), F32),
+        out_shape=jax.ShapeDtypeStruct((ROWS * slot, 128), F32),
         in_specs=[smem, smem] + [pl.BlockSpec(memory_space=ANY)] * 16,
         scratch_shapes=[VMEM((slot, ROWS, 128), F32), pltpu.SemaphoreType.DMA((slot,))],
         compiler_params=vm(8),
@@ -417,7 +423,7 @@
                 v = lax.ppermute(v, "gx", perm)
             parts.append(v)
     out = pick(tuple(order), sizes, slot, frag_root, place, parts)
-    return jnp.transpose(out, (1, 0, 2)).reshape(slot, ROWS * 128)
+    return jnp.transpose(out.reshape(ROWS, slot, 128), (1, 0, 2)).reshape(slot, ROWS * 128)
 
 
 def solution(mesh):

time: 210 us -> 202 us (0.962)
  the two profiles are of different devices: /device:TPU:86 before, /device:TPU:106 now
where the time goes in v2:
time: 202 us
  waiting for transfers between devices  86.5 us (43%)
  starting transfers between devices  57.9 us (29%)
  Pallas kernels  31.1 us (15%)
  blocking collectives  23.9 us (12%)
  local copies, waits for them, and re-layouts  2.12 us (1%)
    ppermute x15, waiting for transfers between devices, program(): v = lax.ppermute(v, 'gx', perm)  63.3 us
    ppermute x15, starting transfers between devices, program(): v = lax.ppermute(v, 'gx', perm)  51.6 us
    all_to_all x1, blocking collectives, program(): lax.all_to_all(jnp.broadcast_to(frag_root[None], (groups, 3, slot)), 'gx'...  23.9 us
    ppermute x6, waiting for transfers between devices, move(): return lax.ppermute(v, axis, [(i, (i + by) % count) for i in range(count)])  22.3 us
    pallas_call x4, Pallas kernels, fields(): pl.pallas_call(kernel, out_shape=(out,) * n, in_specs=[smem, smem, vmem,...  9.78 us
    ppermute x6, starting transfers between devices, move(): return lax.ppermute(v, axis, [(i, (i + by) % count) for i in range(count)])  6.35 us
    pallas_call x1, Pallas kernels, join_mid(): pl.pallas_call(join_mid_kernel, out_shape=jax.ShapeDtypeStruct((128 + 2 *...  4.75 us
    pallas_call x1, Pallas kernels, halos(): pl.pallas_call(halo_kernel, out_shape=jax.ShapeDtypeStruct((80 * YSTEP, 1...  4.4 us
  transfers between devices with their start and end apart: 23, of which 7 were waited for; matrix products, arithmetic and copies ran while one was open for 0% of the time, Pallas kernels for 11%

profile of v2, /device:TPU:106, one launch (start us, length us, event | category | flops | bytes accessed | tf_op | source)
XLA Modules:
  0.0 202.1 jit_solution(9300252429272578731)
XLA Ops:
  0.0 1.9 fusion
  1.9 1.6 collective-permute-start
  3.5 0.5 collective-permute-start.1
  4.0 1.1 pack.1
  5.1 0.1 collective-permute-start.3
  5.2 2.0 collective-permute-start.4
  7.2 21.1 %collective-permute-done.before = f32[34,60,128]{2,1,0:T(8,128)S(1)} collective-permute-done((f32[34,60,128]{2,1,0:T(8,128)S(1)}, f32[34,60,128]{2,1,0:T(8,128)S(1)}, u32[]{:S(2)}, u32[]{:S(2)}) %collective-permute-start) | collective-permute-done | bytes 1044512 | tf_op jit(solution)/shard_map/ppermute | solution.py:382
  28.3 1.2 collective-permute-done.1.after
  29.5 4.1 %middle.1 = f32[9216,128]{1,0:T(8,128)} custom-call(f32[34,60,128]{2,1,0:T(8,128)S(1)} %collective-permute-done.before, f32[60,60,128]{2,1,0:T(8,128)S(1)} %copy-done, f32[34,60,128]{2,1,0:T(8,128)S(1)} %collective-permute-done.1.after, f32[20,64,128]{2,1,0:T(8,128)S(1)} %get-tuple-element.23.packed), custom_call_target="tpu_custom_call" | custom-call | flops 10000000000 | tf_op jit(solution)/shard_map/middle/pallas_call | solution.py:104
  33.6 0.0 collective-permute-start.2
  33.7 0.1 fusion.1
  33.8 0.1 fusion.2
  33.8 0.0 copy-start.1
  33.9 0.1 pad_maximum_fusion
  33.9 1.3 collective-permute-start.5
  35.2 0.1 pad_maximum_fusion.1
  35.3 0.9 collective-permute-start.6
  36.2 23.9 %all_to_all.5.roots.refs_0_ = s32[16,3,4]{2,1,0:T(4,128)S(1)} all-to-all(s32[16,3,4]{2,1,0:T(4,128)S(1)} %broadcast_in_dim.2), channel_id=1, replica_groups=mesh['gx'=16,'gy'=2,'gz'=4] {'gx'}, dimensions={0} | all-to-all | bytes 1536 | tf_op jit(solution)/shard_map/all_to_all | solution.py:391
  60.1 4.4 %halos.1 = f32[5760,128]{1,0:T(8,128)} custom-call(f32[20,64,128]{2,1,0:T(8,128)S(1)} %collective-permute-done.3.zb, f32[20,64,128]{2,1,0:T(8,128)S(1)} %collective-permute-done.4.za, f32[24,64,128]{2,1,0:T(8,128)S(1)} %collective-permute-done.5.left, f32[24,64,128]{2,1,0:T(8,128)S(1)} %collective-permute-done.6.right, s32[16,3,4]{2,1,0:T(4,128)S(1)} %all_to_all.5.roots.refs_0_), custom_call_target="tpu_custom_call" | custom-call | flops 5000000000 | tf_op jit(solution)/shard_map/halos/pallas_call | solution.py:137
  64.5 0.1 pad_add_fusion.refs_1_
  64.5 4.7 %join_mid.1.full = bf16[196,256,128]{2,1,0:T(8,128)(2,1)S(1)} custom-call(f32[128,72,128]{2,1,0:T(8,128)} %bitcast.3.own, f32[128,72,128]{2,1,0:T(8,128)} %collective-permute-done.2.part), custom_call_target="tpu_custom_call" | custom-call | flops 2000000000 | tf_op jit(solution)/shard_map/join_mid/pallas_call | solution.py:172
  69.3 0.0 copy-start.2
  69.3 0.0 copy-start.3
  69.3 0.0 copy-start.4
  69.3 0.8 collective-permute-done.7.part
  70.2 3.2 %join_halo.1.refs_5_ = bf16[196,256,128]{2,1,0:T(8,128)(2,1)S(1)} custom-call(bf16[196,256,128]{2,1,0:T(8,128)(2,1)S(1)} %join_mid.1.full, f32[80,72,128]{2,1,0:T(8,128)} %bitcast.4.own, f32[80,72,128]{2,1,0:T(8,128)} %collective-permute-done.7.part), custom_call_target="tpu_custom_call", output_to_operand_aliasing={{}: (0, {})} | custom-call | flops 2000000000 | tf_op jit(solution)/shard_map/join_halo/pallas_call | solution.py:182
  73.4 1.6 fields.7
  75.0 0.7 collective-permute-start.17
  75.7 10.9 %collective-permute-start.18 = (f32[864,128]{1,0:T(8,128)S(1)}, f32[864,128]{1,0:T(8,128)S(1)}, u32[]{:S(2)}, u32[]{:S(2)}) collective-permute-start(f32[864,128]{1,0:T(8,128)S(1)} %get-tuple-element.35), channel_id=1, source_target_pairs={{0,24},{8,0},{16,8},{24,16},{32,56},{40,32},{48,40},{56,48},{64,88... | collective-permute-start | bytes 1327112 | tf_op jit(solution)/shard_map/ppermute | solution.py:423
  86.6 0.4 collective-permute-start.19
  87.0 4.3 %collective-permute-start.20 = (f32[864,128]{1,0:T(8,128)S(1)}, f32[864,128]{1,0:T(8,128)S(1)}, u32[]{:S(2)}, u32[]{:S(2)}) collective-permute-start(f32[864,128]{1,0:T(8,128)S(1)} %get-tuple-element.37), channel_id=1, source_target_pairs={{0,96},{8,104},{16,112},{24,120},{32,0},{40,8},{48,16},{56,24},{64... | collective-permute-start | bytes 1327112 | tf_op jit(solution)/shard_map/ppermute | solution.py:423
  91.3 1.5 collective-permute-start.21
  92.8 5.7 %fields.6 = (f32[864,128]{1,0:T(8,128)S(1)}, f32[864,128]{1,0:T(8,128)S(1)}, f32[864,128]{1,0:T(8,128)S(1)}, f32[864,128]{1,0:T(8,128)S(1)}, f32[864,128]{1,0:T(8,128)S(1)}) custom-call(s32[16,3,4]{2,1,0:T(4,128)S(1)} %all_to_all.5.roots.refs_0_, s32[3]{0:T(128)S(1)} %pad_add_fusion.refs_1_, bf16[48,128]{1,0:T(8,128)(2,1)S(1)} %copy-done.3, ...), custom_call_target="tpu_custom_call" | custom-call | flops 15000000512 | tf_op jit(solution)/shard_map/fields/pallas_call | solution.py:316
  98.5 1.2 fields.5
  99.7 6.4 %collective-permute-start.22 = (f32[864,128]{1,0:T(8,128)S(1)}, f32[864,128]{1,0:T(8,128)S(1)}, u32[]{:S(2)}, u32[]{:S(2)}) collective-permute-start(f32[864,128]{1,0:T(8,128)S(1)} %get-tuple-element.39), channel_id=1, source_target_pairs={{0,64},{8,72},{16,80},{24,88},{32,96},{40,104},{48,112},{56,120},{... | collective-permute-start | bytes 1327112 | tf_op jit(solution)/shard_map/ppermute | solution.py:423
  106.2 1.5 collective-permute-start.12
  107.7 1.4 collective-permute-start.13
  109.1 4.2 %collective-permute-start.14 = (f32[864,128]{1,0:T(8,128)S(1)}, f32[864,128]{1,0:T(8,128)S(1)}, u32[]{:S(2)}, u32[]{:S(2)}) collective-permute-start(f32[864,128]{1,0:T(8,128)S(1)} %get-tuple-element.31), channel_id=1, source_target_pairs={{0,56},{8,32},{16,40},{24,48},{32,88},{40,64},{48,72},{56,80},{64,... | collective-permute-start | bytes 1327112 | tf_op jit(solution)/shard_map/ppermute | solution.py:423
  113.3 0.9 collective-permute-start.15
  114.2 1.2 fields.4
  115.5 17.1 %collective-permute-done.22.refs_16_ = f32[864,128]{1,0:T(8,128)S(1)} collective-permute-done((f32[864,128]{1,0:T(8,128)S(1)}, f32[864,128]{1,0:T(8,128)S(1)}, u32[]{:S(2)}, u32[]{:S(2)}) %collective-permute-start.22) | collective-permute-done | bytes 442400 | tf_op jit(solution)/shard_map/ppermute | solution.py:423
  132.5 7.5 %collective-permute-start.16 = (f32[864,128]{1,0:T(8,128)S(1)}, f32[864,128]{1,0:T(8,128)S(1)}, u32[]{:S(2)}, u32[]{:S(2)}) collective-permute-start(f32[864,128]{1,0:T(8,128)S(1)} %get-tuple-element.33), channel_id=1, source_target_pairs={{0,80},{8,88},{16,64},{24,72},{32,112},{40,120},{48,96},{56,104},{... | collective-permute-start | bytes 1327112 | tf_op jit(solution)/shard_map/ppermute | solution.py:423
  140.1 5.5 %collective-permute-start.10 = (f32[864,128]{1,0:T(8,128)S(1)}, f32[864,128]{1,0:T(8,128)S(1)}, u32[]{:S(2)}, u32[]{:S(2)}) collective-permute-start(f32[864,128]{1,0:T(8,128)S(1)} %get-tuple-element.27), channel_id=1, source_target_pairs={{0,72},{8,80},{16,88},{24,64},{32,104},{40,112},{48,120},{56,96},{... | collective-permute-start | bytes 1327112 | tf_op jit(solution)/shard_map/ppermute | solution.py:423
  145.5 6.4 %collective-permute-start.8 = (f32[864,128]{1,0:T(8,128)S(1)}, f32[864,128]{1,0:T(8,128)S(1)}, u32[]{:S(2)}, u32[]{:S(2)}) collective-permute-start(f32[864,128]{1,0:T(8,128)S(1)} %get-tuple-element.25), channel_id=1, source_target_pairs={{0,48},{8,56},{16,32},{24,40},{32,80},{40,88},{48,64},{56,72},{64,... | collective-permute-start | bytes 1327112 | tf_op jit(solution)/shard_map/ppermute | solution.py:423
  151.9 18.9 %collective-permute-done.10.refs_4_ = f32[864,128]{1,0:T(8,128)S(1)} collective-permute-done((f32[864,128]{1,0:T(8,128)S(1)}, f32[864,128]{1,0:T(8,128)S(1)}, u32[]{:S(2)}, u32[]{:S(2)}) %collective-permute-start.10) | collective-permute-done | bytes 442400 | tf_op jit(solution)/shard_map/ppermute | solution.py:423
  170.7 18.9 %collective-permute-done.8.refs_2_ = f32[864,128]{1,0:T(8,128)S(1)} collective-permute-done((f32[864,128]{1,0:T(8,128)S(1)}, f32[864,128]{1,0:T(8,128)S(1)}, u32[]{:S(2)}, u32[]{:S(2)}) %collective-permute-start.8) | collective-permute-done | bytes 442400 | tf_op jit(solution)/shard_map/ppermute | solution.py:423
  189.7 8.5 %collective-permute-done.9.refs_3_ = f32[864,128]{1,0:T(8,128)S(1)} collective-permute-done((f32[864,128]{1,0:T(8,128)S(1)}, f32[864,128]{1,0:T(8,128)S(1)}, u32[]{:S(2)}, u32[]{:S(2)}) %collective-permute-start.9) | collective-permute-done | bytes 442400 | tf_op jit(solution)/shard_map/ppermute | solution.py:423
  198.1 3.8 %pick.1 = f32[3456,128]{1,0:T(8,128)} custom-call(s32[3,4]{1,0:T(4,128)S(1)} %copy-done.1, s32[3]{0:T(128)S(1)} %pad_add_fusion.refs_1_, f32[864,128]{1,0:T(8,128)S(1)} %collective-permute-done.8.refs_2_, f32[864,128]{1,0:T(8,128)S(1)} %collective-permute-done.9.refs_3_, f32[864,128]{1,0:T(8,128)S(1)} %collective-permute-done.10.refs_4_, ...), custom_call_target="tpu_custom_call" | custom-call | tf_op jit(solution)/shard_map/pick/pallas_call | solution.py:362
  (26 shorter events, 0.1 us)
Async XLA Ops:
  0.0 4.0 %copy-start = (f32[60,60,128]{2,1,0:T(8,128)S(1)}, f32[60,60,128]{2,1,0:T(8,128)}, u32[]{:S(2)}) copy-start(f32[60,60,128]{2,1,0:T(8,128)} %own.1) | copy-start | bytes 5529604
  1.9 26.4 %collective-permute-start = (f32[34,60,128]{2,1,0:T(8,128)S(1)}, f32[34,60,128]{2,1,0:T(8,128)S(1)}, u32[]{:S(2)}, u32[]{:S(2)}) collective-permute-start(f32[34,60,128]{2,1,0:T(8,128)S(1)} %get-tuple-element.42), channel_id=1, source_target_pairs={{0,8},{8,16},{16,24},{24,32},{32,40},{40,48},{48,56},{56,64},{64,7... | collective-permute-start | bytes 3133448 | tf_op jit(solution)/shard_map/ppermute | solution.py:382
  3.5 26.0 %collective-permute-start.1 = (f32[34,60,128]{2,1,0:T(8,128)S(1)}, f32[34,60,128]{2,1,0:T(8,128)S(1)}, u32[]{:S(2)}, u32[]{:S(2)}) collective-permute-start(f32[34,60,128]{2,1,0:T(8,128)S(1)} %get-tuple-element.41), channel_id=1, source_target_pairs={{0,120},{8,0},{16,8},{24,16},{32,24},{40,32},{48,40},{56,48},{64,5... | collective-permute-start | bytes 3133448 | tf_op jit(solution)/shard_map/ppermute | solution.py:382
  5.1 28.5 %collective-permute-start.3 = (f32[20,64,128]{2,1,0:T(8,128)S(1)}, f32[20,64,128]{2,1,0:T(8,128)S(1)}, u32[]{:S(2)}, u32[]{:S(2)}) collective-permute-start(f32[20,64,128]{2,1,0:T(8,128)S(1)} %get-tuple-element.23.packed), channel_id=1, source_target_pairs={{0,1},{1,2},{2,3},{3,0},{4,5},{5,6},{6,7},{7,4},{8,9},{9,10},{10,1... | collective-permute-start | bytes 1966088 | tf_op jit(solution)/shard_map/ppermute | solution.py:382
  5.2 28.6 %collective-permute-start.4 = (f32[20,64,128]{2,1,0:T(8,128)S(1)}, f32[20,64,128]{2,1,0:T(8,128)S(1)}, u32[]{:S(2)}, u32[]{:S(2)}) collective-permute-start(f32[20,64,128]{2,1,0:T(8,128)S(1)} %get-tuple-element.24), channel_id=1, source_target_pairs={{0,3},{1,0},{2,1},{3,2},{4,7},{5,4},{6,5},{7,6},{8,11},{9,8},{10,9... | collective-permute-start | bytes 1966088 | tf_op jit(solution)/shard_map/ppermute | solution.py:382
  33.6 30.9 %collective-permute-start.2 = (f32[128,72,128]{2,1,0:T(8,128)}, f32[128,72,128]{2,1,0:T(8,128)}, u32[]{:S(2)}, u32[]{:S(2)}) collective-permute-start(f32[128,72,128]{2,1,0:T(8,128)} %bitcast.3.own), channel_id=1, source_target_pairs={{0,4},{4,0},{1,5},{5,1},{2,6},{6,2},{3,7},{7,3},{8,12},{12,8},{9,1... | collective-permute-start | bytes 14155784 | tf_op jit(solution)/shard_map/ppermute | solution.py:397
  33.8 2.3 %copy-start.1 = (s32[3,4]{1,0:T(4,128)S(1)}, s32[3,4]{1,0:T(4,128)}, u32[]{:S(2)}) copy-start(s32[3,4]{1,0:T(4,128)} %refs_0_.1) | copy-start | bytes 148
  33.9 26.1 %collective-permute-start.5 = (f32[24,64,128]{2,1,0:T(8,128)S(1)}, f32[24,64,128]{2,1,0:T(8,128)S(1)}, u32[]{:S(2)}, u32[]{:S(2)}) collective-permute-start(f32[24,64,128]{2,1,0:T(8,128)S(1)} %pad_maximum_fusion), channel_id=1, source_target_pairs={{0,8},{8,16},{16,24},{24,32},{32,40},{40,48},{48,56},{56,64},{64,7... | collective-permute-start | bytes 2359304 | tf_op jit(solution)/shard_map/ppermute | solution.py:382
  35.3 24.8 %collective-permute-start.6 = (f32[24,64,128]{2,1,0:T(8,128)S(1)}, f32[24,64,128]{2,1,0:T(8,128)S(1)}, u32[]{:S(2)}, u32[]{:S(2)}) collective-permute-start(f32[24,64,128]{2,1,0:T(8,128)S(1)} %pad_maximum_fusion.1), channel_id=1, source_target_pairs={{0,120},{8,0},{16,8},{24,16},{32,24},{40,32},{48,40},{56,48},{64,5... | collective-permute-start | bytes 2359304 | tf_op jit(solution)/shard_map/ppermute | solution.py:382
  64.5 5.7 %collective-permute-start.7 = (f32[80,72,128]{2,1,0:T(8,128)}, f32[80,72,128]{2,1,0:T(8,128)}, u32[]{:S(2)}, u32[]{:S(2)}) collective-permute-start(f32[80,72,128]{2,1,0:T(8,128)} %bitcast.4.own), channel_id=1, source_target_pairs={{0,4},{4,0},{1,5},{5,1},{2,6},{6,2},{3,7},{7,3},{8,12},{12,8},{9,1... | collective-permute-start | bytes 8847368 | tf_op jit(solution)/shard_map/ppermute | solution.py:400
  69.3 4.0 %copy-start.2 = (bf16[96,144]{1,0:T(8,128)(2,1)S(1)}, bf16[96,144]{1,0:T(8,128)(2,1)}, u32[]{:S(2)}) copy-start(bf16[96,144]{1,0:T(8,128)(2,1)} %constant.22.clone.refs_4_) | copy-start | bytes 82948
  69.3 4.0 %copy-start.3 = (bf16[48,128]{1,0:T(8,128)(2,1)S(1)}, bf16[48,128]{1,0:T(8,128)(2,1)}, u32[]{:S(2)}) copy-start(bf16[48,128]{1,0:T(8,128)(2,1)} %constant.20.clone.refs_2_) | copy-start | bytes 36868
  69.3 4.0 %copy-start.4 = (bf16[48,128]{1,0:T(8,128)(2,1)S(1)}, bf16[48,128]{1,0:T(8,128)(2,1)}, u32[]{:S(2)}) copy-start(bf16[48,128]{1,0:T(8,128)(2,1)} %constant.21.clone.refs_3_) | copy-start | bytes 36868
  75.0 24.8 %collective-permute-start.17 = (f32[864,128]{1,0:T(8,128)S(1)}, f32[864,128]{1,0:T(8,128)S(1)}, u32[]{:S(2)}, u32[]{:S(2)}) collective-permute-start(f32[864,128]{1,0:T(8,128)S(1)} %get-tuple-element.34), channel_id=1, source_target_pairs={{0,8},{8,16},{16,24},{24,0},{32,40},{40,48},{48,56},{56,32},{64,72... | collective-permute-start | bytes 1327112 | tf_op jit(solution)/shard_map/ppermute | solution.py:423
  75.7 30.5 %collective-permute-start.18 = (f32[864,128]{1,0:T(8,128)S(1)}, f32[864,128]{1,0:T(8,128)S(1)}, u32[]{:S(2)}, u32[]{:S(2)}) collective-permute-start(f32[864,128]{1,0:T(8,128)S(1)} %get-tuple-element.35), channel_id=1, source_target_pairs={{0,24},{8,0},{16,8},{24,16},{32,56},{40,32},{48,40},{56,48},{64,88... | collective-permute-start | bytes 1327112 | tf_op jit(solution)/shard_map/ppermute | solution.py:423
  86.6 21.1 %collective-permute-start.19 = (f32[864,128]{1,0:T(8,128)S(1)}, f32[864,128]{1,0:T(8,128)S(1)}, u32[]{:S(2)}, u32[]{:S(2)}) collective-permute-start(f32[864,128]{1,0:T(8,128)S(1)} %get-tuple-element.36), channel_id=1, source_target_pairs={{0,32},{8,40},{16,48},{24,56},{32,64},{40,72},{48,80},{56,88},{64,... | collective-permute-start | bytes 1327112 | tf_op jit(solution)/shard_map/ppermute | solution.py:423
  87.0 22.1 %collective-permute-start.20 = (f32[864,128]{1,0:T(8,128)S(1)}, f32[864,128]{1,0:T(8,128)S(1)}, u32[]{:S(2)}, u32[]{:S(2)}) collective-permute-start(f32[864,128]{1,0:T(8,128)S(1)} %get-tuple-element.37), channel_id=1, source_target_pairs={{0,96},{8,104},{16,112},{24,120},{32,0},{40,8},{48,16},{56,24},{64... | collective-permute-start | bytes 1327112 | tf_op jit(solution)/shard_map/ppermute | solution.py:423
  91.3 22.0 %collective-permute-start.21 = (f32[864,128]{1,0:T(8,128)S(1)}, f32[864,128]{1,0:T(8,128)S(1)}, u32[]{:S(2)}, u32[]{:S(2)}) collective-permute-start(f32[864,128]{1,0:T(8,128)S(1)} %get-tuple-element.38), channel_id=1, source_target_pairs={{0,16},{8,24},{16,0},{24,8},{32,48},{40,56},{48,32},{56,40},{64,80... | collective-permute-start | bytes 1327112 | tf_op jit(solution)/shard_map/ppermute | solution.py:423
  99.7 32.8 %collective-permute-start.22 = (f32[864,128]{1,0:T(8,128)S(1)}, f32[864,128]{1,0:T(8,128)S(1)}, u32[]{:S(2)}, u32[]{:S(2)}) collective-permute-start(f32[864,128]{1,0:T(8,128)S(1)} %get-tuple-element.39), channel_id=1, source_target_pairs={{0,64},{8,72},{16,80},{24,88},{32,96},{40,104},{48,112},{56,120},{... | collective-permute-start | bytes 1327112 | tf_op jit(solution)/shard_map/ppermute | solution.py:423
  106.2 33.9 %collective-permute-start.12 = (f32[864,128]{1,0:T(8,128)S(1)}, f32[864,128]{1,0:T(8,128)S(1)}, u32[]{:S(2)}, u32[]{:S(2)}) collective-permute-start(f32[864,128]{1,0:T(8,128)S(1)} %get-tuple-element.29), channel_id=1, source_target_pairs={{0,40},{8,48},{16,56},{24,32},{32,72},{40,80},{48,88},{56,64},{64,... | collective-permute-start | bytes 1327112 | tf_op jit(solution)/shard_map/ppermute | solution.py:423
  107.7 37.8 %collective-permute-start.13 = (f32[864,128]{1,0:T(8,128)S(1)}, f32[864,128]{1,0:T(8,128)S(1)}, u32[]{:S(2)}, u32[]{:S(2)}) collective-permute-start(f32[864,128]{1,0:T(8,128)S(1)} %get-tuple-element.30), channel_id=1, source_target_pairs={{0,120},{8,96},{16,104},{24,112},{32,24},{40,0},{48,8},{56,16},{64... | collective-permute-start | bytes 1327112 | tf_op jit(solution)/shard_map/ppermute | solution.py:423
  109.1 36.4 %collective-permute-start.14 = (f32[864,128]{1,0:T(8,128)S(1)}, f32[864,128]{1,0:T(8,128)S(1)}, u32[]{:S(2)}, u32[]{:S(2)}) collective-permute-start(f32[864,128]{1,0:T(8,128)S(1)} %get-tuple-element.31), channel_id=1, source_target_pairs={{0,56},{8,32},{16,40},{24,48},{32,88},{40,64},{48,72},{56,80},{64,... | collective-permute-start | bytes 1327112 | tf_op jit(solution)/shard_map/ppermute | solution.py:423
  113.3 38.6 %collective-permute-start.15 = (f32[864,128]{1,0:T(8,128)S(1)}, f32[864,128]{1,0:T(8,128)S(1)}, u32[]{:S(2)}, u32[]{:S(2)}) collective-permute-start(f32[864,128]{1,0:T(8,128)S(1)} %get-tuple-element.32), channel_id=1, source_target_pairs={{0,104},{8,112},{16,120},{24,96},{32,8},{40,16},{48,24},{56,0},{64... | collective-permute-start | bytes 1327112 | tf_op jit(solution)/shard_map/ppermute | solution.py:423
  132.5 19.4 %collective-permute-start.16 = (f32[864,128]{1,0:T(8,128)S(1)}, f32[864,128]{1,0:T(8,128)S(1)}, u32[]{:S(2)}, u32[]{:S(2)}) collective-permute-start(f32[864,128]{1,0:T(8,128)S(1)} %get-tuple-element.33), channel_id=1, source_target_pairs={{0,80},{8,88},{16,64},{24,72},{32,112},{40,120},{48,96},{56,104},{... | collective-permute-start | bytes 1327112 | tf_op jit(solution)/shard_map/ppermute | solution.py:423
  140.1 30.7 %collective-permute-start.10 = (f32[864,128]{1,0:T(8,128)S(1)}, f32[864,128]{1,0:T(8,128)S(1)}, u32[]{:S(2)}, u32[]{:S(2)}) collective-permute-start(f32[864,128]{1,0:T(8,128)S(1)} %get-tuple-element.27), channel_id=1, source_target_pairs={{0,72},{8,80},{16,88},{24,64},{32,104},{40,112},{48,120},{56,96},{... | collective-permute-start | bytes 1327112 | tf_op jit(solution)/shard_map/ppermute | solution.py:423
  145.5 25.2 %collective-permute-start.11 = (f32[864,128]{1,0:T(8,128)S(1)}, f32[864,128]{1,0:T(8,128)S(1)}, u32[]{:S(2)}, u32[]{:S(2)}) collective-permute-start(f32[864,128]{1,0:T(8,128)S(1)} %get-tuple-element.28), channel_id=1, source_target_pairs={{0,88},{8,64},{16,72},{24,80},{32,120},{40,96},{48,104},{56,112},{... | collective-permute-start | bytes 1327112 | tf_op jit(solution)/shard_map/ppermute | solution.py:423
  145.5 44.1 %collective-permute-start.8 = (f32[864,128]{1,0:T(8,128)S(1)}, f32[864,128]{1,0:T(8,128)S(1)}, u32[]{:S(2)}, u32[]{:S(2)}) collective-permute-start(f32[864,128]{1,0:T(8,128)S(1)} %get-tuple-element.25), channel_id=1, source_target_pairs={{0,48},{8,56},{16,32},{24,40},{32,80},{40,88},{48,64},{56,72},{64,... | collective-permute-start | bytes 1327112 | tf_op jit(solution)/shard_map/ppermute | solution.py:423
  151.9 46.3 %collective-permute-start.9 = (f32[864,128]{1,0:T(8,128)S(1)}, f32[864,128]{1,0:T(8,128)S(1)}, u32[]{:S(2)}, u32[]{:S(2)}) collective-permute-start(f32[864,128]{1,0:T(8,128)S(1)} %get-tuple-element.26), channel_id=1, source_target_pairs={{0,112},{8,120},{16,96},{24,104},{32,16},{40,24},{48,0},{56,8},{64... | collective-permute-start | bytes 1327112 | tf_op jit(solution)/shard_map/ppermute | solution.py:423

commit v3 on v2

--- a/solution.py
+++ b/solution.py
@@ -24,13 +24,6 @@
 VMEM = pltpu.VMEM
 SMEM = pltpu.SMEM
 
-GROUPS = (
-    ((1, 2), (3, 2)),
-    ((2, 1), (2, 3)),
-    ((1, 1), (3, 3), (1, 3), (3, 1), (2, 2)),
-    ((0, 1), (0, 3), (1, 0), (3, 0), (0, 2), (2, 0), (0, 0)),
-)
-
 
 def interp_matrix():
     a = np.arange(G, dtype=np.float64)[:, None]
@@ -72,7 +65,7 @@
     return pl.pallas_call(
         pack_kernel,
         out_shape=(big, big),
-        compiler_params=vm(16),
+        compiler_params=vm(10),
         name="pack",
     )(p)
 
@@ -106,7 +99,7 @@
         out_shape=jax.ShapeDtypeStruct((128 * YSTEP, 128), F32),
         in_specs=[pl.BlockSpec(memory_space=VMEM)] * 3 + [pl.BlockSpec(memory_space=ANY)],
         scratch_shapes=[VMEM((128 * YSTEP, 128), F32)],
-        compiler_params=vm(20),
+        compiler_params=vm(18),
         cost_estimate=cost(MID_COST),
         name="middle",
     )(before, own, after, packed).reshape(128, YSTEP, 128)
@@ -139,7 +132,7 @@
         out_shape=jax.ShapeDtypeStruct((80 * YSTEP, 128), F32),
         in_specs=[pl.BlockSpec(memory_space=VMEM)] * 4 + [pl.BlockSpec(memory_space=SMEM)],
         scratch_shapes=[VMEM((128 * YSTEP, 128), F32)],
-        compiler_params=vm(20),
+        compiler_params=vm(16),
         cost_estimate=cost(5),
         name="halos",
     )(zb, za, left, right, roots).reshape(80, YSTEP, 128)
@@ -154,12 +147,30 @@
     return split_rows(jnp.concatenate([own, part], axis=0))
 
 
-def join_mid_kernel(own, part, out):
-    def step(z, carry):
-        out[HALO + z] = both(own[z, :YPAD], part[z, :YPAD])
-        return carry
-
-    lax.fori_loop(0, 128, step, 0, unroll=4)
+CHUNK = 16
+
+
+def join_mid_kernel(own, part, out, own_v, part_v, sems):
+    def copies(n):
+        rows = pl.ds(n * CHUNK, CHUNK)
+        return (
+            pltpu.make_async_copy(own.at[rows], own_v.at[rows], sems.at[0, n]),
+            pltpu.make_async_copy(part.at[rows], part_v.at[rows], sems.at[1, n]),
+        )
+
+    for n in range(128 // CHUNK):
+        for c in copies(n):
+            c.start()
+    for n in range(128 // CHUNK):
+        for c in copies(n):
+            c.wait()
+
+        def step(i, carry):
+            z = n * CHUNK + i
+            out[HALO + z] = both(own_v[z, :YPAD], part_v[z, :YPAD])
+            return carry
+
+        lax.fori_loop(0, CHUNK, step, 0, unroll=4)
 
 
 def join_halo_kernel(full, own, part, out):
@@ -172,7 +183,13 @@
     return pl.pallas_call(
         join_mid_kernel,
         out_shape=jax.ShapeDtypeStruct((128 + 2 * HALO, 4 * YPAD, 128), BF16),
-        compiler_params=vm(32),
+        in_specs=[pl.BlockSpec(memory_space=ANY)] * 2,
+        scratch_shapes=[
+            VMEM((128, YSTEP, 128), F32),
+            VMEM((128, YSTEP, 128), F32),
+            pltpu.SemaphoreType.DMA((2, 128 // CHUNK)),
+        ],
+        compiler_params=vm(14),
         cost_estimate=cost(2),
         name="join_mid",
     )(own, part)
@@ -182,9 +199,13 @@
     return pl.pallas_call(
         join_halo_kernel,
         out_shape=jax.ShapeDtypeStruct(full.shape, full.dtype),
-        in_specs=[pl.BlockSpec(memory_space=ANY)] + [pl.BlockSpec(memory_space=VMEM)] * 2,
+        in_specs=[
+            pl.BlockSpec(memory_space=ANY),
+            pl.BlockSpec(memory_space=VMEM),
+            pl.BlockSpec(memory_space=VMEM),
+        ],
         input_output_aliases={0: 0},
-        compiler_params=vm(32),
+        compiler_params=vm(10),
         cost_estimate=cost(2),
         name="join_halo",
     )(full, own, part)
@@ -221,24 +242,20 @@
     return ok, x0, y0, z0
 
 
-def field_kernel(shifts, sizes, slot, roots, place, thi, tlo, a2_ref, full, *rest):
-    n = len(shifts)
-    outs = rest[:n]
-    t1, t2, obuf, info, sems = rest[n:]
-    gx = place[0]
-    py = gx // 4
-    px = gx % 4
-
-    for j, (dy, dx) in enumerate(shifts):
-        holder = ((py + dy) % 4) * 4 + (px + dx) % 4
-        ok, x0, y0, z0 = locate(roots, place, sizes, slot, holder)
-        info[0, j] = ok
+def field_kernel(late, sizes, slot, n, roots, place, thi, tlo, a2_ref, full, out, t1, t2, obuf, info, sems):
+    def find(j, carry):
+        ok, x0, y0, z0 = locate(roots, place, sizes, slot, j)
+        inside = jnp.logical_and(z0 >= HALO, z0 <= HALO + 128 - BOX)
+        info[0, j] = jnp.where(inside, 0, ok) if late else jnp.where(inside, ok, 0)
         info[1, j] = x0
         info[2, j] = y0
         info[3, j] = z0
-
-    def out_copy(k, b):
-        return pltpu.make_async_copy(obuf.at[b], outs[k], sems.at[b])
+        return carry
+
+    lax.fori_loop(0, n, find, 0)
+
+    def out_copy(j, b):
+        return pltpu.make_async_copy(obuf.at[b], out.at[j], sems.at[b])
 
     for b in range(G):
         t1[b * 72 + 64:b * 72 + 72, :] = jnp.zeros((8, 128), F32)
@@ -291,10 +308,7 @@
         @pl.when(info[0, j] == 1)
         def _():
             compute(j, b)
-            for k in range(n):
-                @pl.when(j == k)
-                def _(k=k):
-                    out_copy(k, b).start()
+            out_copy(j, b).start()
 
         return carry
 
@@ -303,21 +317,25 @@
     drain(n - 1, (n - 1) % 2)
 
 
-def fields(shifts, sizes, slot, roots, place, thi, tlo, a2, full):
-    n = len(shifts)
-    out = jax.ShapeDtypeStruct((ROWS, 128), F32)
+def fields(sizes, slot, n, roots, place, thi, tlo, a2, full, done=None):
     smem = pl.BlockSpec(memory_space=SMEM)
     vmem = pl.BlockSpec(memory_space=VMEM)
     hbm = pl.BlockSpec(memory_space=ANY)
+    late = done is not None
+    out = jax.ShapeDtypeStruct((n, ROWS, 128), F32)
 
     def kernel(*refs):
-        field_kernel(shifts, sizes, slot, *refs)
-
+        if late:
+            field_kernel(True, sizes, slot, n, *refs[:6], *refs[7:])
+        else:
+            field_kernel(False, sizes, slot, n, *refs[:7], *refs[8:])
+
+    args = (roots, place, thi, tlo, a2, full) + ((done,) if late else ())
     return pl.pallas_call(
         kernel,
-        out_shape=(out,) * n,
-        in_specs=[smem, smem, vmem, vmem, vmem, vmem],
-        out_specs=(hbm,) * n,
+        out_shape=(out,) if late else (out, jax.ShapeDtypeStruct(full.shape, full.dtype)),
+        in_specs=[smem, smem, vmem, vmem, vmem, vmem] + [hbm] * late,
+        out_specs=(hbm,) if late else (hbm, hbm),
         scratch_shapes=[
             VMEM((G * 72, 128), F32),
             VMEM((G * G, 128), F32),
@@ -325,48 +343,41 @@
             SMEM((4, n), jnp.int32),
             pltpu.SemaphoreType.DMA((2,)),
         ],
-        compiler_params=vm(24),
+        input_output_aliases={6: 0} if late else {5: 1},
+        compiler_params=vm(8),
         cost_estimate=cost(FIELD_COST * n),
         name="fields",
-    )(roots, place, thi, tlo, a2, full)
-
-
-def pick_kernel(order, sizes, slot, own_root, place, *rest):
-    srcs = rest[:16]
-    out, buf, sems = rest[16:]
+    )(*args)
+
+
+def pick_kernel(sizes, slot, n, own_root, parts, out, buf, sems):
     nx, bx = sizes[0], sizes[3]
-    gx = place[0]
-    py = gx // 4
-    px = gx % 4
     for s in range(slot):
         r = own_root[0, s] + HALO
-        for k, (dy, dx) in enumerate(order):
-            anchor = ((py + 4 - dy) % 4) * 4 + (px + 4 - dx) % 4
-            v = r - anchor * bx
-            v = jnp.where(v < 0, v + nx, jnp.where(v >= nx, v - nx, v))
-
-            @pl.when(v < bx)
-            def _(k=k, s=s):
-                pltpu.make_async_copy(srcs[k], buf.at[s], sems.at[s]).start()
+        r = jnp.where(r >= nx, r - nx, r)
+
+        def scan(j, anchor):
+            return jnp.where(r >= j * bx, j, anchor)
+
+        anchor = lax.fori_loop(0, n, scan, jnp.int32(0), unroll=True)
+        pltpu.make_async_copy(parts.at[anchor], buf.at[s], sems.at[s]).start()
     for s in range(slot):
-        pltpu.make_async_copy(srcs[0], buf.at[s], sems.at[s]).wait()
+        pltpu.make_async_copy(parts.at[0], buf.at[s], sems.at[s]).wait()
         out[pl.ds(s, ROWS, stride=slot), :] = buf[s]
 
 
-def pick(order, sizes, slot, own_root, place, parts):
-    smem = pl.BlockSpec(memory_space=SMEM)
-
+def pick(sizes, slot, n, own_root, parts):
     def kernel(*refs):
-        pick_kernel(order, sizes, slot, *refs)
+        pick_kernel(sizes, slot, n, *refs)
 
     return pl.pallas_call(
         kernel,
         out_shape=jax.ShapeDtypeStruct((ROWS * slot, 128), F32),
-        in_specs=[smem, smem] + [pl.BlockSpec(memory_space=ANY)] * 16,
+        in_specs=[pl.BlockSpec(memory_space=SMEM), pl.BlockSpec(memory_space=ANY)],
         scratch_shapes=[VMEM((slot, ROWS, 128), F32), pltpu.SemaphoreType.DMA((slot,))],
         compiler_params=vm(8),
         name="pick",
-    )(own_root, place, *parts)
+    )(own_root, parts)
 
 
 def program(potential, frag_root):
@@ -398,7 +409,6 @@
     full = join_mid(own_m, part_m)
     own_h = halos(got_zb, got_za, left, right, roots)
     part_h = lax.ppermute(own_h, "gy", swap)
-    full = join_halo(full, own_h, part_h)
 
     table = interp_matrix()
     hi = np.asarray(table.astype(BF16))
@@ -412,17 +422,11 @@
     a2[:G, 72:72 + BOX] = hi
     a2[G:, :BOX] = lo
 
-    order = []
-    parts = []
-    for shifts in GROUPS:
-        done = fields(shifts, sizes, slot, roots, place, thi, tlo, a2, full)
-        for (dy, dx), v in zip(shifts, done):
-            order.append((dy, dx))
-            if (dy, dx) != (0, 0):
-                perm = [(4 * y + x, 4 * ((y + dy) % 4) + (x + dx) % 4) for y in range(4) for x in range(4)]
-                v = lax.ppermute(v, "gx", perm)
-            parts.append(v)
-    out = pick(tuple(order), sizes, slot, frag_root, place, parts)
+    done, full = fields(sizes, slot, groups, roots, place, thi, tlo, a2, full)
+    full = join_halo(full, own_h, part_h)
+    (done,) = fields(sizes, slot, groups, roots, place, thi, tlo, a2, full, done)
+    parts = lax.all_to_all(done, "gx", 0, 0, tiled=True)
+    out = pick(sizes, slot, groups, frag_root, parts)
     return jnp.transpose(out.reshape(ROWS, slot, 128), (1, 0, 2)).reshape(slot, ROWS * 128)
 
 

time: 202 us -> 215 us (1.064)
  the two profiles are of different devices: /device:TPU:106 before, /device:TPU:64 now
where the time goes in v3:
time: 215 us
  blocking collectives  114 us (53%)
  waiting for transfers between devices  57.3 us (27%)
  Pallas kernels  22.1 us (10%)
  starting transfers between devices  16.2 us (8%)
  local copies, waits for them, and re-layouts  2.75 us (1%)
    all_to_all x1, blocking collectives, program(): parts = lax.all_to_all(done, 'gx', 0, 0, tiled=True)  114 us
    ppermute x6, waiting for transfers between devices, move(): return lax.ppermute(v, axis, [(i, (i + by) % count) for i in range(count)])  44.6 us
    ppermute x6, starting transfers between devices, move(): return lax.ppermute(v, axis, [(i, (i + by) % count) for i in range(count)])  12.7 us
    all_to_all x1, waiting for transfers between devices, program(): lax.all_to_all(jnp.broadcast_to(frag_root[None], (groups, 3, slot)), 'gx'...  12.6 us
    pallas_call x2, Pallas kernels, fields(): pl.pallas_call(kernel, out_shape=(out,) if late else (out, jax.ShapeDtype...  6.61 us
  transfers between devices with their start and end apart: 9, of which 5 were waited for; matrix products, arithmetic and copies ran while one was open for 1% of the time, Pallas kernels for 6%

profile of v3, /device:TPU:64, one launch (start us, length us, event | category | flops | bytes accessed | tf_op | source)
XLA Modules:
  0.0 214.5 jit_solution(13843947544821988836)
XLA Ops:
  0.0 0.0 copy-start
  0.0 2.0 fusion
  2.0 5.3 %collective-permute-start.1 = (f32[34,60,128]{2,1,0:T(8,128)S(1)}, f32[34,60,128]{2,1,0:T(8,128)S(1)}, u32[]{:S(2)}, u32[]{:S(2)}) collective-permute-start(f32[34,60,128]{2,1,0:T(8,128)S(1)} %get-tuple-element.13), channel_id=1, source_target_pairs={{0,120},{8,0},{16,8},{24,16},{32,24},{40,32},{48,40},{56,48},{64,5... | collective-permute-start | bytes 3133448 | tf_op jit(solution)/shard_map/ppermute | solution.py:393
  7.3 0.0 collective-permute-start
  7.3 0.0 copy-done
  7.3 1.1 pack.1
  8.4 22.7 %collective-permute-done.1.after = f32[34,60,128]{2,1,0:T(8,128)S(1)} collective-permute-done((f32[34,60,128]{2,1,0:T(8,128)S(1)}, f32[34,60,128]{2,1,0:T(8,128)S(1)}, u32[]{:S(2)}, u32[]{:S(2)}) %collective-permute-start.1) | collective-permute-done | bytes 1044512 | tf_op jit(solution)/shard_map/ppermute | solution.py:393
  31.1 5.5 %collective-permute-done.before = f32[34,60,128]{2,1,0:T(8,128)S(1)} collective-permute-done((f32[34,60,128]{2,1,0:T(8,128)S(1)}, f32[34,60,128]{2,1,0:T(8,128)S(1)}, u32[]{:S(2)}, u32[]{:S(2)}) %collective-permute-start) | collective-permute-done | bytes 1044512 | tf_op jit(solution)/shard_map/ppermute | solution.py:393
  36.6 4.1 %middle.1 = f32[9216,128]{1,0:T(8,128)} custom-call(f32[34,60,128]{2,1,0:T(8,128)S(1)} %collective-permute-done.before, f32[60,60,128]{2,1,0:T(8,128)S(1)} %copy-done, f32[34,60,128]{2,1,0:T(8,128)S(1)} %collective-permute-done.1.after, f32[20,64,128]{2,1,0:T(8,128)S(1)} %get-tuple-element.9.packed), custom_call_target="tpu_custom_call" | custom-call | flops 10000000000 | tf_op jit(solution)/shard_map/middle/pallas_call | solution.py:97
  40.7 0.0 collective-permute-start.2
  40.7 1.6 collective-permute-start.3
  42.4 0.0 copy-start.1
  42.4 0.4 collective-permute-start.4
  42.8 15.1 %collective-permute-done.3.zb = f32[20,64,128]{2,1,0:T(8,128)S(1)} collective-permute-done((f32[20,64,128]{2,1,0:T(8,128)S(1)}, f32[20,64,128]{2,1,0:T(8,128)S(1)}, u32[]{:S(2)}, u32[]{:S(2)}) %collective-permute-start.3) | collective-permute-done | bytes 655392 | tf_op jit(solution)/shard_map/ppermute | solution.py:393
  57.9 0.1 fusion.1
  58.0 1.3 collective-permute-done.4.za
  59.2 0.1 fusion.2
  59.3 1.0 pad_maximum_fusion
  60.3 0.0 collective-permute-start.5
  60.3 0.9 pad_maximum_fusion.1
  61.2 5.3 %collective-permute-start.6 = (f32[24,64,128]{2,1,0:T(8,128)}, f32[24,64,128]{2,1,0:T(8,128)S(1)}, u32[]{:S(2)}, u32[]{:S(2)}) collective-permute-start(f32[24,64,128]{2,1,0:T(8,128)} %pad_maximum_fusion.1), channel_id=1, source_target_pairs={{0,120},{8,0},{16,8},{24,16},{32,24},{40,32},{48,40},{56,48},{64,5... | collective-permute-start | bytes 2359304 | tf_op jit(solution)/shard_map/ppermute | solution.py:393
  66.6 0.0 copy-done.1
  66.6 0.6 broadcast_in_dim.2
  67.2 3.4 %all-to-all-start = ((s32[16,3,4]{2,1,0:T(4,128)}), s32[16,3,4]{2,1,0:T(4,128)S(1)}, u32[]{:S(2)}, u32[]{:S(2)}) async-start(s32[16,3,4]{2,1,0:T(4,128)} %broadcast_in_dim.2), calls=%async_computation | async-start | bytes 65536 | tf_op jit(solution)/shard_map/all_to_all | solution.py:402
  70.6 0.1 pad_add_fusion.refs_1_
  70.7 12.6 %all-to-all-done.refs_0_.roots = s32[16,3,4]{2,1,0:T(4,128)S(1)} async-done(((s32[16,3,4]{2,1,0:T(4,128)}), s32[16,3,4]{2,1,0:T(4,128)S(1)}, u32[]{:S(2)}, u32[]{:S(2)}) %all-to-all-start) | async-done | bytes 800 | tf_op jit(solution)/shard_map/all_to_all | solution.py:402
  83.3 0.0 collective-permute-done.5.left
  83.3 0.0 collective-permute-done.6.right
  83.3 2.8 %halos.1 = f32[5760,128]{1,0:T(8,128)S(1)} custom-call(f32[20,64,128]{2,1,0:T(8,128)S(1)} %collective-permute-done.3.zb, f32[20,64,128]{2,1,0:T(8,128)S(1)} %collective-permute-done.4.za, f32[24,64,128]{2,1,0:T(8,128)S(1)} %collective-permute-done.5.left, f32[24,64,128]{2,1,0:T(8,128)S(1)} %collective-permute-done.6.right, ...), custom_call_target="tpu_custom_call" | custom-call | flops 5000000000 | tf_op jit(solution)/shard_map/halos/pallas_call | solution.py:130
  86.1 0.0 copy-start.2
  86.1 0.0 copy-start.3
  86.2 0.0 copy-start.4
  86.2 0.1 collective-permute-start.7
  86.3 0.0 collective-permute-done.2.part
  86.3 3.9 %join_mid.1.refs_5_ = bf16[196,256,128]{2,1,0:T(8,128)(2,1)S(1)} custom-call(f32[128,72,128]{2,1,0:T(8,128)} %bitcast.3.own, f32[128,72,128]{2,1,0:T(8,128)} %collective-permute-done.2.part), custom_call_target="tpu_custom_call" | custom-call | flops 2000000000 | tf_op jit(solution)/shard_map/join_mid/pallas_call | solution.py:183
  90.2 0.0 copy-done.2
  90.2 0.0 copy-done.3
  90.2 0.0 copy-done.4
  90.2 4.3 %fields.2 = (f32[16,864,128]{2,1,0:T(8,128)S(1)}, bf16[196,256,128]{2,1,0:T(8,128)(2,1)S(1)}) custom-call(s32[16,3,4]{2,1,0:T(4,128)S(1)} %all-to-all-done.refs_0_.roots, s32[3]{0:T(128)S(1)} %pad_add_fusion.refs_1_, bf16[48,128]{1,0:T(8,128)(2,1)S(1)} %copy-done.4, bf16[48,128]{1,0:T(8,128)(2,1)S(1)} %copy-done.3, ...), custom_call_target="tpu_custom_call", output_to_operand_aliasing={{1}: (5, {})} | custom-call | flops 48000000000 | tf_op jit(solution)/shard_map/fields/pallas_call | solution.py:334
  94.6 0.0 collective-permute-done.7.part
  94.6 0.4 join_halo.1.refs_5_
  95.1 2.3 %fields.3 = f32[16,864,128]{2,1,0:T(8,128)S(1)} custom-call(s32[16,3,4]{2,1,0:T(4,128)S(1)} %all-to-all-done.refs_0_.roots, s32[3]{0:T(128)S(1)} %pad_add_fusion.refs_1_, bf16[48,128]{1,0:T(8,128)(2,1)S(1)} %copy-done.4, bf16[48,128]{1,0:T(8,128)(2,1)S(1)} %copy-done.3, bf16[96,144]{1,0:T(8,128)(2,1)S(1)} %copy-done.2, ...), custom_call_target="tpu_custom_call", output_to_operand_aliasing={{}: (6, {})} | custom-call | flops 48000000000 | tf_op jit(solution)/shard_map/fields/pallas_call | solution.py:334
  97.3 114.1 %all_to_all.10.refs_1_ = f32[16,864,128]{2,1,0:T(8,128)S(1)} all-to-all(f32[16,864,128]{2,1,0:T(8,128)S(1)} %fields.3), channel_id=1, replica_groups=mesh['gx'=16,'gy'=2,'gz'=4] {'gx'}, dimensions={0} | all-to-all | bytes 14155776 | tf_op jit(solution)/shard_map/all_to_all | solution.py:428
  211.4 3.1 %pick.1 = f32[3456,128]{1,0:T(8,128)} custom-call(s32[3,4]{1,0:T(4,128)S(1)} %copy-done.1, f32[16,864,128]{2,1,0:T(8,128)S(1)} %all_to_all.10.refs_1_), custom_call_target="tpu_custom_call" | custom-call | tf_op jit(solution)/shard_map/pick/pallas_call | solution.py:373
Async XLA Ops:
  0.0 7.3 %copy-start = (f32[60,60,128]{2,1,0:T(8,128)S(1)}, f32[60,60,128]{2,1,0:T(8,128)}, u32[]{:S(2)}) copy-start(f32[60,60,128]{2,1,0:T(8,128)} %own.1) | copy-start | bytes 5529604
  2.0 29.1 %collective-permute-start.1 = (f32[34,60,128]{2,1,0:T(8,128)S(1)}, f32[34,60,128]{2,1,0:T(8,128)S(1)}, u32[]{:S(2)}, u32[]{:S(2)}) collective-permute-start(f32[34,60,128]{2,1,0:T(8,128)S(1)} %get-tuple-element.13), channel_id=1, source_target_pairs={{0,120},{8,0},{16,8},{24,16},{32,24},{40,32},{48,40},{56,48},{64,5... | collective-permute-start | bytes 3133448 | tf_op jit(solution)/shard_map/ppermute | solution.py:393
  7.3 29.3 %collective-permute-start = (f32[34,60,128]{2,1,0:T(8,128)S(1)}, f32[34,60,128]{2,1,0:T(8,128)S(1)}, u32[]{:S(2)}, u32[]{:S(2)}) collective-permute-start(f32[34,60,128]{2,1,0:T(8,128)S(1)} %get-tuple-element.14), channel_id=1, source_target_pairs={{0,8},{8,16},{16,24},{24,32},{32,40},{40,48},{48,56},{56,64},{64,7... | collective-permute-start | bytes 3133448 | tf_op jit(solution)/shard_map/ppermute | solution.py:393
  40.7 45.5 %collective-permute-start.2 = (f32[128,72,128]{2,1,0:T(8,128)}, f32[128,72,128]{2,1,0:T(8,128)}, u32[]{:S(2)}, u32[]{:S(2)}) collective-permute-start(f32[128,72,128]{2,1,0:T(8,128)} %bitcast.3.own), channel_id=1, source_target_pairs={{0,4},{4,0},{1,5},{5,1},{2,6},{6,2},{3,7},{7,3},{8,12},{12,8},{9,1... | collective-permute-start | bytes 14155784 | tf_op jit(solution)/shard_map/ppermute | solution.py:408
  40.7 17.1 %collective-permute-start.3 = (f32[20,64,128]{2,1,0:T(8,128)S(1)}, f32[20,64,128]{2,1,0:T(8,128)S(1)}, u32[]{:S(2)}, u32[]{:S(2)}) collective-permute-start(f32[20,64,128]{2,1,0:T(8,128)S(1)} %get-tuple-element.9.packed), channel_id=1, source_target_pairs={{0,1},{1,2},{2,3},{3,0},{4,5},{5,6},{6,7},{7,4},{8,9},{9,10},{10,1... | collective-permute-start | bytes 1966088 | tf_op jit(solution)/shard_map/ppermute | solution.py:393
  42.4 24.2 %copy-start.1 = (s32[3,4]{1,0:T(4,128)S(1)}, s32[3,4]{1,0:T(4,128)}, u32[]{:S(2)}) copy-start(s32[3,4]{1,0:T(4,128)} %refs_0_.1) | copy-start | bytes 148
  42.4 16.9 %collective-permute-start.4 = (f32[20,64,128]{2,1,0:T(8,128)S(1)}, f32[20,64,128]{2,1,0:T(8,128)S(1)}, u32[]{:S(2)}, u32[]{:S(2)}) collective-permute-start(f32[20,64,128]{2,1,0:T(8,128)S(1)} %get-tuple-element.11), channel_id=1, source_target_pairs={{0,3},{1,0},{2,1},{3,2},{4,7},{5,4},{6,5},{7,6},{8,11},{9,8},{10,9... | collective-permute-start | bytes 1966088 | tf_op jit(solution)/shard_map/ppermute | solution.py:393
  60.3 23.1 %collective-permute-start.5 = (f32[24,64,128]{2,1,0:T(8,128)}, f32[24,64,128]{2,1,0:T(8,128)S(1)}, u32[]{:S(2)}, u32[]{:S(2)}) collective-permute-start(f32[24,64,128]{2,1,0:T(8,128)} %pad_maximum_fusion), channel_id=1, source_target_pairs={{0,8},{8,16},{16,24},{24,32},{32,40},{40,48},{48,56},{56,64},{64,7... | collective-permute-start | bytes 2359304 | tf_op jit(solution)/shard_map/ppermute | solution.py:393
  61.2 22.1 %collective-permute-start.6 = (f32[24,64,128]{2,1,0:T(8,128)}, f32[24,64,128]{2,1,0:T(8,128)S(1)}, u32[]{:S(2)}, u32[]{:S(2)}) collective-permute-start(f32[24,64,128]{2,1,0:T(8,128)} %pad_maximum_fusion.1), channel_id=1, source_target_pairs={{0,120},{8,0},{16,8},{24,16},{32,24},{40,32},{48,40},{56,48},{64,5... | collective-permute-start | bytes 2359304 | tf_op jit(solution)/shard_map/ppermute | solution.py:393
  67.2 16.2 %all-to-all-start = ((s32[16,3,4]{2,1,0:T(4,128)}), s32[16,3,4]{2,1,0:T(4,128)S(1)}, u32[]{:S(2)}, u32[]{:S(2)}) async-start(s32[16,3,4]{2,1,0:T(4,128)} %broadcast_in_dim.2), calls=%async_computation | async-start | bytes 65536 | tf_op jit(solution)/shard_map/all_to_all | solution.py:402
  86.1 4.1 %copy-start.2 = (bf16[96,144]{1,0:T(8,128)(2,1)S(1)}, bf16[96,144]{1,0:T(8,128)(2,1)}, u32[]{:S(2)}) copy-start(bf16[96,144]{1,0:T(8,128)(2,1)} %constant.22.clone.refs_4_) | copy-start | bytes 82948
  86.1 4.1 %copy-start.3 = (bf16[48,128]{1,0:T(8,128)(2,1)S(1)}, bf16[48,128]{1,0:T(8,128)(2,1)}, u32[]{:S(2)}) copy-start(bf16[48,128]{1,0:T(8,128)(2,1)} %constant.21.clone.refs_3_) | copy-start | bytes 36868
  86.2 4.1 %copy-start.4 = (bf16[48,128]{1,0:T(8,128)(2,1)S(1)}, bf16[48,128]{1,0:T(8,128)(2,1)}, u32[]{:S(2)}) copy-start(bf16[48,128]{1,0:T(8,128)(2,1)} %constant.20.clone.refs_2_) | copy-start | bytes 36868
  86.2 8.4 %collective-permute-start.7 = (f32[80,72,128]{2,1,0:T(8,128)S(1)}, f32[80,72,128]{2,1,0:T(8,128)S(1)}, u32[]{:S(2)}, u32[]{:S(2)}) collective-permute-start(f32[80,72,128]{2,1,0:T(8,128)S(1)} %bitcast.10), channel_id=1, source_target_pairs={{0,4},{4,0},{1,5},{5,1},{2,6},{6,2},{3,7},{7,3},{8,12},{12,8},{9,1... | collective-permute-start | bytes 8847368 | tf_op jit(solution)/shard_map/ppermute | solution.py:411

commit v4 on v3

--- a/solution.py
+++ b/solution.py
@@ -86,23 +86,31 @@
         out[pl.ds(y, count, stride=YSTEP), :] = jnp.zeros((count, 128), F32)
 
 
-def mid_kernel(before, own, after, packed, out, x_ref):
-    for ref, first, n in ((before, 0, HALO), (own, HALO, 60), (after, HALO + 60, HALO)):
-        for i in range(n):
-            x_ref[pl.ds(YSTEP * (first + i), NY_LOCAL), :] = ref[i]
-    turn(x_ref, out, 128)
-
-
-def middle(before, own, after, packed):
+def mid_kernel(before, own, after, part_before, part_own, part_after, packed, out, x_ref, t_own, t_part):
+    for refs, turned in (((before, own, after), t_own), ((part_before, part_own, part_after), t_part)):
+        for ref, first, n in zip(refs, (0, HALO, HALO + 60), (HALO, 60, HALO)):
+            for i in range(n):
+                x_ref[pl.ds(YSTEP * (first + i), NY_LOCAL), :] = ref[i]
+        turn(x_ref, turned, 128)
+
+    def step(z, carry):
+        rows = pl.ds(pl.multiple_of(z * YSTEP, 8), YPAD)
+        out[HALO + z] = both(t_own[rows, :], t_part[rows, :])
+        return carry
+
+    lax.fori_loop(0, 128, step, 0, unroll=4)
+
+
+def middle(before, own, after, part_before, part_own, part_after, packed):
     return pl.pallas_call(
         mid_kernel,
-        out_shape=jax.ShapeDtypeStruct((128 * YSTEP, 128), F32),
-        in_specs=[pl.BlockSpec(memory_space=VMEM)] * 3 + [pl.BlockSpec(memory_space=ANY)],
-        scratch_shapes=[VMEM((128 * YSTEP, 128), F32)],
-        compiler_params=vm(18),
+        out_shape=jax.ShapeDtypeStruct((128 + 2 * HALO, 4 * YPAD, 128), BF16),
+        in_specs=[pl.BlockSpec(memory_space=VMEM)] * 6 + [pl.BlockSpec(memory_space=ANY)],
+        scratch_shapes=[VMEM((128 * YSTEP, 128), F32)] * 3,
+        compiler_params=vm(40),
         cost_estimate=cost(MID_COST),
         name="middle",
-    )(before, own, after, packed).reshape(128, YSTEP, 128)
+    )(before, own, after, part_before, part_own, part_after, packed)
 
 
 def halo_kernel(zb, za, left, right, roots, out, x_ref):
@@ -147,52 +155,10 @@
     return split_rows(jnp.concatenate([own, part], axis=0))
 
 
-CHUNK = 16
-
-
-def join_mid_kernel(own, part, out, own_v, part_v, sems):
-    def copies(n):
-        rows = pl.ds(n * CHUNK, CHUNK)
-        return (
-            pltpu.make_async_copy(own.at[rows], own_v.at[rows], sems.at[0, n]),
-            pltpu.make_async_copy(part.at[rows], part_v.at[rows], sems.at[1, n]),
-        )
-
-    for n in range(128 // CHUNK):
-        for c in copies(n):
-            c.start()
-    for n in range(128 // CHUNK):
-        for c in copies(n):
-            c.wait()
-
-        def step(i, carry):
-            z = n * CHUNK + i
-            out[HALO + z] = both(own_v[z, :YPAD], part_v[z, :YPAD])
-            return carry
-
-        lax.fori_loop(0, CHUNK, step, 0, unroll=4)
-
-
 def join_halo_kernel(full, own, part, out):
     for z in range(HALO):
         out[z] = both(own[z, :YPAD], part[z, :YPAD])
         out[HALO + 128 + z] = both(own[40 + z, :YPAD], part[40 + z, :YPAD])
-
-
-def join_mid(own, part):
-    return pl.pallas_call(
-        join_mid_kernel,
-        out_shape=jax.ShapeDtypeStruct((128 + 2 * HALO, 4 * YPAD, 128), BF16),
-        in_specs=[pl.BlockSpec(memory_space=ANY)] * 2,
-        scratch_shapes=[
-            VMEM((128, YSTEP, 128), F32),
-            VMEM((128, YSTEP, 128), F32),
-            pltpu.SemaphoreType.DMA((2, 128 // CHUNK)),
-        ],
-        compiler_params=vm(14),
-        cost_estimate=cost(2),
-        name="join_mid",
-    )(own, part)
 
 
 def join_halo(full, own, part):
@@ -404,9 +370,10 @@
     )
 
     swap = [(0, 1), (1, 0)]
-    own_m = middle(before, potential, after, zb)
-    part_m = lax.ppermute(own_m, "gy", swap)
-    full = join_mid(own_m, part_m)
+    part_own = lax.ppermute(potential, "gy", swap)
+    part_after = lax.ppermute(after, "gy", swap)
+    part_before = lax.ppermute(before, "gy", swap)
+    full = middle(before, potential, after, part_before, part_own, part_after, zb)
     own_h = halos(got_zb, got_za, left, right, roots)
     part_h = lax.ppermute(own_h, "gy", swap)
 

time: 215 us -> 216 us (level)
  the two profiles are of different devices: /device:TPU:64 before, /device:TPU:0 now
where the time goes in v4:
time: 216 us; the launch traced here: 214 us
  blocking collectives  108 us (50%)
  waiting for transfers between devices  34.7 us (16%)
  local copies, waits for them, and re-layouts  25.7 us (12%)
  Pallas kernels  24.7 us (11%)
  starting transfers between devices  18.7 us (9%)
    all_to_all x1, blocking collectives, program(): parts = lax.all_to_all(done, 'gx', 0, 0, tiled=True)  108 us
    unnamed x26, local copies, waits for them, and re-layouts  24.7 us
    ppermute x6, waiting for transfers between devices, move(): return lax.ppermute(v, axis, [(i, (i + by) % count) for i in range(count)])  23.4 us
    ppermute x6, starting transfers between devices, move(): return lax.ppermute(v, axis, [(i, (i + by) % count) for i in range(count)])  14.9 us
    pallas_call x1, Pallas kernels, middle(): pl.pallas_call(mid_kernel, out_shape=jax.ShapeDtypeStruct((128 + 2 * HALO...  12.4 us
    all_to_all x1, waiting for transfers between devices, program(): lax.all_to_all(jnp.broadcast_to(frag_root[None], (groups, 3, slot)), 'gx'...  11.3 us
    pallas_call x2, Pallas kernels, fields(): pl.pallas_call(kernel, out_shape=(out,) if late else (out, jax.ShapeDtype...  4.52 us
  transfers between devices with their start and end apart: 11, of which 4 were waited for; matrix products, arithmetic and copies ran while one was open for 1% of the time, Pallas kernels for 8%

profile of v4, /device:TPU:0, one launch (start us, length us, event | category | flops | bytes accessed | tf_op | source)
XLA Modules:
  0.0 214.0 jit_solution(9729949804284199971)
XLA Ops:
  0.0 1.5 copy-done.5
  1.5 1.1 pack.1
  2.6 0.0 copy-start.8
  2.6 2.1 collective-permute-start.5
  4.7 2.2 %collective-permute-start.6 = (f32[20,64,128]{2,1,0:T(8,128)S(1)}, f32[20,64,128]{2,1,0:T(8,128)S(1)}, u32[]{:S(2)}, u32[]{:S(2)}) collective-permute-start(f32[20,64,128]{2,1,0:T(8,128)S(1)} %get-tuple-element.11), channel_id=1, source_target_pairs={{0,3},{1,0},{2,1},{3,2},{4,7},{5,4},{6,5},{7,6},{8,11},{9,8},{10,9... | collective-permute-start | bytes 1966088 | tf_op jit(solution)/shard_map/ppermute | solution.py:359
  6.9 0.2 fusion
  7.2 5.3 %collective-permute-start.1 = (f32[34,60,128]{2,1,0:T(8,128)S(1)}, f32[34,60,128]{2,1,0:T(8,128)}, u32[]{:S(2)}, u32[]{:S(2)}) collective-permute-start(f32[34,60,128]{2,1,0:T(8,128)S(1)} %get-tuple-element.13), channel_id=1, source_target_pairs={{0,120},{8,0},{16,8},{24,16},{32,24},{40,32},{48,40},{56,48},{64,5... | collective-permute-start | bytes 3133448 | tf_op jit(solution)/shard_map/ppermute | solution.py:359
  12.5 0.0 collective-permute-start
  12.5 0.0 collective-permute-start.3
  12.5 9.1 %collective-permute-done.5.zb = f32[20,64,128]{2,1,0:T(8,128)S(1)} collective-permute-done((f32[20,64,128]{2,1,0:T(8,128)S(1)}, f32[20,64,128]{2,1,0:T(8,128)S(1)}, u32[]{:S(2)}, u32[]{:S(2)}) %collective-permute-start.5) | collective-permute-done | bytes 655392 | tf_op jit(solution)/shard_map/ppermute | solution.py:359
  21.6 0.1 fusion.1
  21.7 0.0 collective-permute-done.6.za
  21.7 0.1 fusion.2
  21.8 0.0 copy-start.7
  21.8 1.0 pad_maximum_fusion
  22.7 1.5 collective-permute-start.7
  24.2 1.0 pad_maximum_fusion.1
  25.2 3.9 %collective-permute-start.8 = (f32[24,64,128]{2,1,0:T(8,128)}, f32[24,64,128]{2,1,0:T(8,128)}, u32[]{:S(2)}, u32[]{:S(2)}) collective-permute-start(f32[24,64,128]{2,1,0:T(8,128)} %pad_maximum_fusion.1), channel_id=1, source_target_pairs={{0,120},{8,0},{16,8},{24,16},{32,24},{40,32},{48,40},{56,48},{64,5... | collective-permute-start | bytes 2359304 | tf_op jit(solution)/shard_map/ppermute | solution.py:359
  29.0 8.4 %collective-permute-done.1.after = f32[34,60,128]{2,1,0:T(8,128)} collective-permute-done((f32[34,60,128]{2,1,0:T(8,128)S(1)}, f32[34,60,128]{2,1,0:T(8,128)}, u32[]{:S(2)}, u32[]{:S(2)}) %collective-permute-start.1) | collective-permute-done | bytes 1044512 | tf_op jit(solution)/shard_map/ppermute | solution.py:359
  37.4 0.0 collective-permute-start.4
  37.4 5.9 %collective-permute-done.before = f32[34,60,128]{2,1,0:T(8,128)} collective-permute-done((f32[34,60,128]{2,1,0:T(8,128)S(1)}, f32[34,60,128]{2,1,0:T(8,128)}, u32[]{:S(2)}, u32[]{:S(2)}) %collective-permute-start) | collective-permute-done | bytes 1044512 | tf_op jit(solution)/shard_map/ppermute | solution.py:359
  43.3 0.0 collective-permute-start.2
  43.3 0.6 broadcast_in_dim.2
  44.0 3.5 %all-to-all-start = ((s32[16,3,4]{2,1,0:T(4,128)}), s32[16,3,4]{2,1,0:T(4,128)S(1)}, u32[]{:S(2)}, u32[]{:S(2)}) async-start(s32[16,3,4]{2,1,0:T(4,128)} %broadcast_in_dim.2), calls=%async_computation | async-start | bytes 65536 | tf_op jit(solution)/shard_map/all_to_all | solution.py:368
  47.5 0.1 pad_add_fusion.refs_1_
  47.5 11.3 %all-to-all-done.refs_0_.roots = s32[16,3,4]{2,1,0:T(4,128)S(1)} async-done(((s32[16,3,4]{2,1,0:T(4,128)}), s32[16,3,4]{2,1,0:T(4,128)S(1)}, u32[]{:S(2)}, u32[]{:S(2)}) %all-to-all-start) | async-done | bytes 800 | tf_op jit(solution)/shard_map/all_to_all | solution.py:368
  58.8 0.0 collective-permute-done.7.left
  58.8 0.0 collective-permute-done.8.right
  58.8 3.2 %halos.1 = f32[5760,128]{1,0:T(8,128)S(1)} custom-call(f32[20,64,128]{2,1,0:T(8,128)S(1)} %collective-permute-done.5.zb, f32[20,64,128]{2,1,0:T(8,128)S(1)} %collective-permute-done.6.za, f32[24,64,128]{2,1,0:T(8,128)} %collective-permute-done.7.left, f32[24,64,128]{2,1,0:T(8,128)} %collective-permute-done.8.right, s32[16,3,4]{2,1,0:T(4,128)S(1)} %all-to-all-done.refs_0_.roots), custom_call_target="tpu_custom_call" | custom-call | flops 5000000000 | tf_op jit(solution)/shard_map/halos/pallas_call | solution.py:138
  62.0 0.0 copy-start.10
  62.0 0.0 copy-start.11
  62.0 0.0 copy-start.12
  62.1 0.3 collective-permute-start.9
  62.3 0.0 collective-permute-done.3.part_own
  62.3 0.0 collective-permute-done.4.part_after
  62.4 0.0 collective-permute-done.2.part_before
  62.4 12.4 %middle.1.refs_5_ = bf16[196,256,128]{2,1,0:T(8,128)(2,1)} custom-call(f32[34,60,128]{2,1,0:T(8,128)} %collective-permute-done.before, f32[60,60,128]{2,1,0:T(8,128)S(1)} %copy-done.6, f32[34,60,128]{2,1,0:T(8,128)} %collective-permute-done.1.after, f32[34,60,128]{2,1,0:T(8,128)} %collective-permute-done.2.part_before, ...), custom_call_target="tpu_custom_call" | custom-call | flops 10000000000 | tf_op jit(solution)/shard_map/middle/pallas_call | solution.py:105
  74.8 4.6 %copy-done = bf16[196,256,128]{2,1,0:T(8,128)(2,1)S(1)} copy-done((bf16[196,256,128]{2,1,0:T(8,128)(2,1)S(1)}, bf16[196,256,128]{2,1,0:T(8,128)(2,1)}, u32[]{:S(2)}) %copy-start) | copy-done | bytes 12845080
  79.4 2.3 %fields.2 = (f32[16,864,128]{2,1,0:T(8,128)S(1)}, bf16[196,256,128]{2,1,0:T(8,128)(2,1)S(1)}) custom-call(s32[16,3,4]{2,1,0:T(4,128)S(1)} %all-to-all-done.refs_0_.roots, s32[3]{0:T(128)S(1)} %pad_add_fusion.refs_1_, bf16[48,128]{1,0:T(8,128)(2,1)S(1)} %copy-done.12, bf16[48,128]{1,0:T(8,128)(2,1)S(1)} %copy-done.11, ...), custom_call_target="tpu_custom_call", output_to_operand_aliasing={{1}: (5, {})} | custom-call | flops 48000000000 | tf_op jit(solution)/shard_map/fields/pallas_call | solution.py:300
  81.7 4.6 %copy-done.1 = bf16[196,256,128]{2,1,0:T(8,128)(2,1)} copy-done((bf16[196,256,128]{2,1,0:T(8,128)(2,1)}, bf16[196,256,128]{2,1,0:T(8,128)(2,1)S(1)}, u32[]{:S(2)}) %copy-start.1) | copy-done | bytes 12845080
  86.3 0.0 collective-permute-done.9.part
  86.3 4.6 %copy-done.2 = bf16[196,256,128]{2,1,0:T(8,128)(2,1)S(1)} copy-done((bf16[196,256,128]{2,1,0:T(8,128)(2,1)S(1)}, bf16[196,256,128]{2,1,0:T(8,128)(2,1)}, u32[]{:S(2)}) %copy-start.2) | copy-done | bytes 12845080
  91.0 0.4 join_halo.1.refs_5_
  91.4 4.6 %copy-done.3 = bf16[196,256,128]{2,1,0:T(8,128)(2,1)} copy-done((bf16[196,256,128]{2,1,0:T(8,128)(2,1)}, bf16[196,256,128]{2,1,0:T(8,128)(2,1)S(1)}, u32[]{:S(2)}) %copy-start.3) | copy-done | bytes 12845080
  96.0 4.6 %copy-done.4 = bf16[196,256,128]{2,1,0:T(8,128)(2,1)S(1)} copy-done((bf16[196,256,128]{2,1,0:T(8,128)(2,1)S(1)}, bf16[196,256,128]{2,1,0:T(8,128)(2,1)}, u32[]{:S(2)}) %copy-start.4) | copy-done | bytes 12845080
  100.7 2.3 %fields.3 = f32[16,864,128]{2,1,0:T(8,128)S(1)} custom-call(s32[16,3,4]{2,1,0:T(4,128)S(1)} %all-to-all-done.refs_0_.roots, s32[3]{0:T(128)S(1)} %pad_add_fusion.refs_1_, bf16[48,128]{1,0:T(8,128)(2,1)S(1)} %copy-done.12, bf16[48,128]{1,0:T(8,128)(2,1)S(1)} %copy-done.11, bf16[96,144]{1,0:T(8,128)(2,1)S(1)} %copy-done.10, ...), custom_call_target="tpu_custom_call", output_to_operand_aliasing={{}: (6, {})} | custom-call | flops 48000000000 | tf_op jit(solution)/shard_map/fields/pallas_call | solution.py:300
  102.9 107.8 %all_to_all.10.refs_1_ = f32[16,864,128]{2,1,0:T(8,128)S(1)} all-to-all(f32[16,864,128]{2,1,0:T(8,128)S(1)} %fields.3), channel_id=1, replica_groups=mesh['gx'=16,'gy'=2,'gz'=4] {'gx'}, dimensions={0} | all-to-all | bytes 14155776 | tf_op jit(solution)/shard_map/all_to_all | solution.py:395
  210.7 3.1 %pick.1 = f32[3456,128]{1,0:T(8,128)} custom-call(s32[3,4]{1,0:T(4,128)S(1)} %copy-done.7, f32[16,864,128]{2,1,0:T(8,128)S(1)} %all_to_all.10.refs_1_), custom_call_target="tpu_custom_call" | custom-call | tf_op jit(solution)/shard_map/pick/pallas_call | solution.py:339
  (15 shorter events, 0.0 us)
Async XLA Ops:
  0.0 1.5 copy-start.5
  1.5 5.4 %copy-start.6 = (f32[60,60,128]{2,1,0:T(8,128)S(1)}, f32[60,60,128]{2,1,0:T(8,128)}, u32[]{:S(2)}) copy-start(f32[60,60,128]{2,1,0:T(8,128)} %own.1) | copy-start | bytes 5529604
  2.6 4.6 %copy-start.8 = (f32[20,64,128]{2,1,0:T(8,128)}, f32[20,64,128]{2,1,0:T(8,128)S(1)}, u32[]{:S(2)}) copy-start(f32[20,64,128]{2,1,0:T(8,128)S(1)} %get-tuple-element.9.packed) | copy-start | bytes 1966084
  2.6 18.9 %collective-permute-start.5 = (f32[20,64,128]{2,1,0:T(8,128)S(1)}, f32[20,64,128]{2,1,0:T(8,128)S(1)}, u32[]{:S(2)}, u32[]{:S(2)}) collective-permute-start(f32[20,64,128]{2,1,0:T(8,128)S(1)} %get-tuple-element.9.packed), channel_id=1, source_target_pairs={{0,1},{1,2},{2,3},{3,0},{4,5},{5,6},{6,7},{7,4},{8,9},{9,10},{10,1... | collective-permute-start | bytes 1966088 | tf_op jit(solution)/shard_map/ppermute | solution.py:359
  4.7 16.9 %collective-permute-start.6 = (f32[20,64,128]{2,1,0:T(8,128)S(1)}, f32[20,64,128]{2,1,0:T(8,128)S(1)}, u32[]{:S(2)}, u32[]{:S(2)}) collective-permute-start(f32[20,64,128]{2,1,0:T(8,128)S(1)} %get-tuple-element.11), channel_id=1, source_target_pairs={{0,3},{1,0},{2,1},{3,2},{4,7},{5,4},{6,5},{7,6},{8,11},{9,8},{10,9... | collective-permute-start | bytes 1966088 | tf_op jit(solution)/shard_map/ppermute | solution.py:359
  7.2 30.2 %collective-permute-start.1 = (f32[34,60,128]{2,1,0:T(8,128)S(1)}, f32[34,60,128]{2,1,0:T(8,128)}, u32[]{:S(2)}, u32[]{:S(2)}) collective-permute-start(f32[34,60,128]{2,1,0:T(8,128)S(1)} %get-tuple-element.13), channel_id=1, source_target_pairs={{0,120},{8,0},{16,8},{24,16},{32,24},{40,32},{48,40},{56,48},{64,5... | collective-permute-start | bytes 3133448 | tf_op jit(solution)/shard_map/ppermute | solution.py:359
  12.5 30.9 %collective-permute-start = (f32[34,60,128]{2,1,0:T(8,128)S(1)}, f32[34,60,128]{2,1,0:T(8,128)}, u32[]{:S(2)}, u32[]{:S(2)}) collective-permute-start(f32[34,60,128]{2,1,0:T(8,128)S(1)} %get-tuple-element.14), channel_id=1, source_target_pairs={{0,8},{8,16},{16,24},{24,32},{32,40},{40,48},{48,56},{56,64},{64,7... | collective-permute-start | bytes 3133448 | tf_op jit(solution)/shard_map/ppermute | solution.py:359
  12.5 49.9 %collective-permute-start.3 = (f32[60,60,128]{2,1,0:T(8,128)S(1)}, f32[60,60,128]{2,1,0:T(8,128)}, u32[]{:S(2)}, u32[]{:S(2)}) collective-permute-start(f32[60,60,128]{2,1,0:T(8,128)S(1)} %copy-done.6), channel_id=1, source_target_pairs={{0,4},{4,0},{1,5},{5,1},{2,6},{6,2},{3,7},{7,3},{8,12},{12,8},{9,1... | collective-permute-start | bytes 5529608 | tf_op jit(solution)/shard_map/ppermute | solution.py:373
  21.8 21.6 %copy-start.7 = (s32[3,4]{1,0:T(4,128)S(1)}, s32[3,4]{1,0:T(4,128)}, u32[]{:S(2)}) copy-start(s32[3,4]{1,0:T(4,128)} %refs_0_.1) | copy-start | bytes 148
  22.7 36.1 %collective-permute-start.7 = (f32[24,64,128]{2,1,0:T(8,128)}, f32[24,64,128]{2,1,0:T(8,128)}, u32[]{:S(2)}, u32[]{:S(2)}) collective-permute-start(f32[24,64,128]{2,1,0:T(8,128)} %pad_maximum_fusion), channel_id=1, source_target_pairs={{0,8},{8,16},{16,24},{24,32},{32,40},{40,48},{48,56},{56,64},{64,7... | collective-permute-start | bytes 2359304 | tf_op jit(solution)/shard_map/ppermute | solution.py:359
  25.2 33.6 %collective-permute-start.8 = (f32[24,64,128]{2,1,0:T(8,128)}, f32[24,64,128]{2,1,0:T(8,128)}, u32[]{:S(2)}, u32[]{:S(2)}) collective-permute-start(f32[24,64,128]{2,1,0:T(8,128)} %pad_maximum_fusion.1), channel_id=1, source_target_pairs={{0,120},{8,0},{16,8},{24,16},{32,24},{40,32},{48,40},{56,48},{64,5... | collective-permute-start | bytes 2359304 | tf_op jit(solution)/shard_map/ppermute | solution.py:359
  37.4 24.9 %collective-permute-start.4 = (f32[34,60,128]{2,1,0:T(8,128)}, f32[34,60,128]{2,1,0:T(8,128)}, u32[]{:S(2)}, u32[]{:S(2)}) collective-permute-start(f32[34,60,128]{2,1,0:T(8,128)} %collective-permute-done.1.after), channel_id=1, source_target_pairs={{0,4},{4,0},{1,5},{5,1},{2,6},{6,2},{3,7},{7,3},{8,12},{12,8},{9,1... | collective-permute-start | bytes 3133448 | tf_op jit(solution)/shard_map/ppermute | solution.py:374
  43.3 19.0 %collective-permute-start.2 = (f32[34,60,128]{2,1,0:T(8,128)}, f32[34,60,128]{2,1,0:T(8,128)}, u32[]{:S(2)}, u32[]{:S(2)}) collective-permute-start(f32[34,60,128]{2,1,0:T(8,128)} %collective-permute-done.before), channel_id=1, source_target_pairs={{0,4},{4,0},{1,5},{5,1},{2,6},{6,2},{3,7},{7,3},{8,12},{12,8},{9,1... | collective-permute-start | bytes 3133448 | tf_op jit(solution)/shard_map/ppermute | solution.py:375
  44.0 14.9 %all-to-all-start = ((s32[16,3,4]{2,1,0:T(4,128)}), s32[16,3,4]{2,1,0:T(4,128)S(1)}, u32[]{:S(2)}, u32[]{:S(2)}) async-start(s32[16,3,4]{2,1,0:T(4,128)} %broadcast_in_dim.2), calls=%async_computation | async-start | bytes 65536 | tf_op jit(solution)/shard_map/all_to_all | solution.py:368
  58.8 3.5 %copy-start.9 = (f32[20,64,128]{2,1,0:T(8,128)S(1)}, f32[20,64,128]{2,1,0:T(8,128)}, u32[]{:S(2)}) copy-start(f32[20,64,128]{2,1,0:T(8,128)} %copy-done.8) | copy-start | bytes 1966084
  62.0 12.7 %copy-start.10 = (bf16[96,144]{1,0:T(8,128)(2,1)S(1)}, bf16[96,144]{1,0:T(8,128)(2,1)}, u32[]{:S(2)}) copy-start(bf16[96,144]{1,0:T(8,128)(2,1)} %constant.22.clone.refs_4_) | copy-start | bytes 82948
  62.0 12.7 %copy-start.11 = (bf16[48,128]{1,0:T(8,128)(2,1)S(1)}, bf16[48,128]{1,0:T(8,128)(2,1)}, u32[]{:S(2)}) copy-start(bf16[48,128]{1,0:T(8,128)(2,1)} %constant.21.clone.refs_3_) | copy-start | bytes 36868
  62.0 12.7 %copy-start.12 = (bf16[48,128]{1,0:T(8,128)(2,1)S(1)}, bf16[48,128]{1,0:T(8,128)(2,1)}, u32[]{:S(2)}) copy-start(bf16[48,128]{1,0:T(8,128)(2,1)} %constant.20.clone.refs_2_) | copy-start | bytes 36868
  62.1 24.2 %collective-permute-start.9 = (f32[80,72,128]{2,1,0:T(8,128)S(1)}, f32[80,72,128]{2,1,0:T(8,128)S(1)}, u32[]{:S(2)}, u32[]{:S(2)}) collective-permute-start(f32[80,72,128]{2,1,0:T(8,128)S(1)} %bitcast.9), channel_id=1, source_target_pairs={{0,4},{4,0},{1,5},{5,1},{2,6},{6,2},{3,7},{7,3},{8,12},{12,8},{9,1... | collective-permute-start | bytes 8847368 | tf_op jit(solution)/shard_map/ppermute | solution.py:378
  74.8 4.7 %copy-start = (bf16[196,256,128]{2,1,0:T(8,128)(2,1)S(1)}, bf16[196,256,128]{2,1,0:T(8,128)(2,1)}, u32[]{:S(2)}) copy-start(bf16[196,256,128]{2,1,0:T(8,128)(2,1)} %middle.1.refs_5_) | copy-start | bytes 38535172
  81.7 4.6 %copy-start.1 = (bf16[196,256,128]{2,1,0:T(8,128)(2,1)}, bf16[196,256,128]{2,1,0:T(8,128)(2,1)S(1)}, u32[]{:S(2)}) copy-start(bf16[196,256,128]{2,1,0:T(8,128)(2,1)S(1)} %get-tuple-element.10.full) | copy-start | bytes 38535172
  86.3 4.7 %copy-start.2 = (bf16[196,256,128]{2,1,0:T(8,128)(2,1)S(1)}, bf16[196,256,128]{2,1,0:T(8,128)(2,1)}, u32[]{:S(2)}) copy-start(bf16[196,256,128]{2,1,0:T(8,128)(2,1)} %copy-done.1) | copy-start | bytes 38535172
  91.4 4.6 %copy-start.3 = (bf16[196,256,128]{2,1,0:T(8,128)(2,1)}, bf16[196,256,128]{2,1,0:T(8,128)(2,1)S(1)}, u32[]{:S(2)}) copy-start(bf16[196,256,128]{2,1,0:T(8,128)(2,1)S(1)} %join_halo.1.refs_5_) | copy-start | bytes 38535172
  96.0 4.7 %copy-start.4 = (bf16[196,256,128]{2,1,0:T(8,128)(2,1)S(1)}, bf16[196,256,128]{2,1,0:T(8,128)(2,1)}, u32[]{:S(2)}) copy-start(bf16[196,256,128]{2,1,0:T(8,128)(2,1)} %copy-done.3) | copy-start | bytes 38535172

commit v5 on v4

--- a/solution.py
+++ b/solution.py
@@ -15,7 +15,11 @@
 NY_LOCAL = 60
 YPAD = 64
 YSTEP = 72
+T1STEP = 76
 ROWS = G * G * G // 128
+PLANE = G * G // 128
+KEPT = (G - 1) * PLANE
+SENT = KEPT + 2
 F32 = jnp.float32
 BF16 = jnp.bfloat16
 MID_COST = 10
@@ -224,7 +228,7 @@
         return pltpu.make_async_copy(obuf.at[b], out.at[j], sems.at[b])
 
     for b in range(G):
-        t1[b * 72 + 64:b * 72 + 72, :] = jnp.zeros((8, 128), F32)
+        t1[b * T1STEP + 64:b * T1STEP + 72, :] = jnp.zeros((8, 128), F32)
 
     def compute(j, b):
         x0 = info[1, j]
@@ -242,10 +246,10 @@
         for p in range(BOX // 2):
             rhs = jnp.concatenate([full[z0 + 2 * p], full[z0 + 2 * p + 1]], axis=1)
             t = folded(jnp.dot(a1, rhs, preferred_element_type=F32))
-            t1[pl.ds(2 * p, G, stride=72), :] = t[:, :128]
-            t1[pl.ds(2 * p + 1, G, stride=72), :] = t[:, 128:]
+            t1[pl.ds(2 * p, G, stride=T1STEP), :] = t[:, :128]
+            t1[pl.ds(2 * p + 1, G, stride=T1STEP), :] = t[:, 128:]
         for q in range(0, G, 2):
-            f = jnp.concatenate([t1[q * 72:q * 72 + 72, :], t1[q * 72 + 72:q * 72 + 144, :]], axis=1)
+            f = jnp.concatenate([t1[q * T1STEP:q * T1STEP + 72, :], t1[q * T1STEP + T1STEP:q * T1STEP + T1STEP + 72, :]], axis=1)
             t = folded(jnp.dot(a2, split_rows(f), preferred_element_type=F32))
             t2[q * G:q * G + G, :] = t[:, :128]
             t2[q * G + G:q * G + 2 * G, :] = t[:, 128:]
@@ -256,8 +260,8 @@
             rhs = jnp.concatenate([hi, lo], axis=1)
             r = lax.dot_general(a3, rhs, (((1,), (1,)), ((), ())), preferred_element_type=F32)
             t = folded(r)
-            obuf[b, pl.ds(2 * m, G, stride=18), :] = t[:, :128]
-            obuf[b, pl.ds(2 * m + 1, G, stride=18), :] = t[:, 128:]
+            obuf[b, pl.ds(2 * m, G - 1, stride=PLANE), :] = t[:G - 1, :128]
+            obuf[b, pl.ds(2 * m + 1, G - 1, stride=PLANE), :] = t[:G - 1, 128:]
 
     def drain(j, b):
         @pl.when(info[0, j] == 1)
@@ -288,7 +292,7 @@
     vmem = pl.BlockSpec(memory_space=VMEM)
     hbm = pl.BlockSpec(memory_space=ANY)
     late = done is not None
-    out = jax.ShapeDtypeStruct((n, ROWS, 128), F32)
+    out = jax.ShapeDtypeStruct((n, SENT, 128), F32)
 
     def kernel(*refs):
         if late:
@@ -303,9 +307,9 @@
         in_specs=[smem, smem, vmem, vmem, vmem, vmem] + [hbm] * late,
         out_specs=(hbm,) if late else (hbm, hbm),
         scratch_shapes=[
-            VMEM((G * 72, 128), F32),
+            VMEM((G * T1STEP, 128), F32),
             VMEM((G * G, 128), F32),
-            VMEM((2, ROWS, 128), F32),
+            VMEM((2, SENT, 128), F32),
             SMEM((4, n), jnp.int32),
             pltpu.SemaphoreType.DMA((2,)),
         ],
@@ -329,7 +333,12 @@
         pltpu.make_async_copy(parts.at[anchor], buf.at[s], sems.at[s]).start()
     for s in range(slot):
         pltpu.make_async_copy(parts.at[0], buf.at[s], sems.at[s]).wait()
-        out[pl.ds(s, ROWS, stride=slot), :] = buf[s]
+        out[pl.ds(s, KEPT, stride=slot), :] = buf[s, :KEPT]
+        last = buf[s, :PLANE]
+        for a in range(1, G - 1):
+            plane = buf[s, a * PLANE:(a + 1) * PLANE]
+            last = last - plane if a % 2 else last + plane
+        out[pl.ds(KEPT * slot + s, PLANE, stride=slot), :] = last
 
 
 def pick(sizes, slot, n, own_root, parts):
@@ -340,7 +349,7 @@
         kernel,
         out_shape=jax.ShapeDtypeStruct((ROWS * slot, 128), F32),
         in_specs=[pl.BlockSpec(memory_space=SMEM), pl.BlockSpec(memory_space=ANY)],
-        scratch_shapes=[VMEM((slot, ROWS, 128), F32), pltpu.SemaphoreType.DMA((slot,))],
+        scratch_shapes=[VMEM((slot, SENT, 128), F32), pltpu.SemaphoreType.DMA((slot,))],
         compiler_params=vm(8),
         name="pick",
     )(own_root, parts)

time: 216 us -> 215 us (level)
  no operation moved by 1% of the time
where the time goes in v5:
time: 215 us; the launch traced here: 213 us
  blocking collectives  106 us (49%)
  waiting for transfers between devices  34.7 us (16%)
  local copies, waits for them, and re-layouts  25.7 us (12%)
  Pallas kernels  24.9 us (12%)
  starting transfers between devices  18.7 us (9%)
    all_to_all x1, blocking collectives, program(): parts = lax.all_to_all(done, 'gx', 0, 0, tiled=True)  106 us
    unnamed x26, local copies, waits for them, and re-layouts  24.7 us
    ppermute x6, waiting for transfers between devices, move(): return lax.ppermute(v, axis, [(i, (i + by) % count) for i in range(count)])  23.4 us
    ppermute x6, starting transfers between devices, move(): return lax.ppermute(v, axis, [(i, (i + by) % count) for i in range(count)])  14.9 us
    pallas_call x1, Pallas kernels, middle(): pl.pallas_call(mid_kernel, out_shape=jax.ShapeDtypeStruct((128 + 2 * HALO...  12.4 us
    all_to_all x1, waiting for transfers between devices, program(): lax.all_to_all(jnp.broadcast_to(frag_root[None], (groups, 3, slot)), 'gx'...  11.3 us
    pallas_call x2, Pallas kernels, fields(): pl.pallas_call(kernel, out_shape=(out,) if late else (out, jax.ShapeDtype...  4.52 us
  transfers between devices with their start and end apart: 11, of which 4 were waited for; matrix products, arithmetic and copies ran while one was open for 1% of the time, Pallas kernels for 8%

profile of v5, /device:TPU:0, one launch (start us, length us, event | category | flops | bytes accessed | tf_op | source)
XLA Modules:
  0.0 212.9 jit_solution(3984432513049309487)
XLA Ops:
  0.0 1.5 copy-done.5
  1.5 1.1 pack.1
  2.6 0.0 copy-start.8
  2.6 2.1 collective-permute-start.5
  4.7 2.2 %collective-permute-start.6 = (f32[20,64,128]{2,1,0:T(8,128)S(1)}, f32[20,64,128]{2,1,0:T(8,128)S(1)}, u32[]{:S(2)}, u32[]{:S(2)}) collective-permute-start(f32[20,64,128]{2,1,0:T(8,128)S(1)} %get-tuple-element.11), channel_id=1, source_target_pairs={{0,3},{1,0},{2,1},{3,2},{4,7},{5,4},{6,5},{7,6},{8,11},{9,8},{10,9... | collective-permute-start | bytes 1966088 | tf_op jit(solution)/shard_map/ppermute | solution.py:368
  6.9 0.2 fusion
  7.2 5.3 %collective-permute-start.1 = (f32[34,60,128]{2,1,0:T(8,128)S(1)}, f32[34,60,128]{2,1,0:T(8,128)}, u32[]{:S(2)}, u32[]{:S(2)}) collective-permute-start(f32[34,60,128]{2,1,0:T(8,128)S(1)} %get-tuple-element.13), channel_id=1, source_target_pairs={{0,120},{8,0},{16,8},{24,16},{32,24},{40,32},{48,40},{56,48},{64,5... | collective-permute-start | bytes 3133448 | tf_op jit(solution)/shard_map/ppermute | solution.py:368
  12.5 0.0 collective-permute-start
  12.5 0.0 collective-permute-start.3
  12.5 9.1 %collective-permute-done.5.zb = f32[20,64,128]{2,1,0:T(8,128)S(1)} collective-permute-done((f32[20,64,128]{2,1,0:T(8,128)S(1)}, f32[20,64,128]{2,1,0:T(8,128)S(1)}, u32[]{:S(2)}, u32[]{:S(2)}) %collective-permute-start.5) | collective-permute-done | bytes 655392 | tf_op jit(solution)/shard_map/ppermute | solution.py:368
  21.6 0.1 fusion.1
  21.7 0.0 collective-permute-done.6.za
  21.7 0.1 fusion.2
  21.8 0.0 copy-start.7
  21.8 1.0 pad_maximum_fusion
  22.7 1.5 collective-permute-start.7
  24.2 1.0 pad_maximum_fusion.1
  25.2 3.9 %collective-permute-start.8 = (f32[24,64,128]{2,1,0:T(8,128)}, f32[24,64,128]{2,1,0:T(8,128)}, u32[]{:S(2)}, u32[]{:S(2)}) collective-permute-start(f32[24,64,128]{2,1,0:T(8,128)} %pad_maximum_fusion.1), channel_id=1, source_target_pairs={{0,120},{8,0},{16,8},{24,16},{32,24},{40,32},{48,40},{56,48},{64,5... | collective-permute-start | bytes 2359304 | tf_op jit(solution)/shard_map/ppermute | solution.py:368
  29.0 8.4 %collective-permute-done.1.after = f32[34,60,128]{2,1,0:T(8,128)} collective-permute-done((f32[34,60,128]{2,1,0:T(8,128)S(1)}, f32[34,60,128]{2,1,0:T(8,128)}, u32[]{:S(2)}, u32[]{:S(2)}) %collective-permute-start.1) | collective-permute-done | bytes 1044512 | tf_op jit(solution)/shard_map/ppermute | solution.py:368
  37.4 0.0 collective-permute-start.4
  37.4 5.9 %collective-permute-done.before = f32[34,60,128]{2,1,0:T(8,128)} collective-permute-done((f32[34,60,128]{2,1,0:T(8,128)S(1)}, f32[34,60,128]{2,1,0:T(8,128)}, u32[]{:S(2)}, u32[]{:S(2)}) %collective-permute-start) | collective-permute-done | bytes 1044512 | tf_op jit(solution)/shard_map/ppermute | solution.py:368
  43.3 0.0 collective-permute-start.2
  43.3 0.6 broadcast_in_dim.2
  44.0 3.5 %all-to-all-start = ((s32[16,3,4]{2,1,0:T(4,128)}), s32[16,3,4]{2,1,0:T(4,128)S(1)}, u32[]{:S(2)}, u32[]{:S(2)}) async-start(s32[16,3,4]{2,1,0:T(4,128)} %broadcast_in_dim.2), calls=%async_computation | async-start | bytes 65536 | tf_op jit(solution)/shard_map/all_to_all | solution.py:377
  47.5 0.1 pad_add_fusion.refs_1_
  47.5 11.3 %all-to-all-done.refs_0_.roots = s32[16,3,4]{2,1,0:T(4,128)S(1)} async-done(((s32[16,3,4]{2,1,0:T(4,128)}), s32[16,3,4]{2,1,0:T(4,128)S(1)}, u32[]{:S(2)}, u32[]{:S(2)}) %all-to-all-start) | async-done | bytes 800 | tf_op jit(solution)/shard_map/all_to_all | solution.py:377
  58.8 0.0 collective-permute-done.7.left
  58.8 0.0 collective-permute-done.8.right
  58.8 3.2 %halos.1 = f32[5760,128]{1,0:T(8,128)S(1)} custom-call(f32[20,64,128]{2,1,0:T(8,128)S(1)} %collective-permute-done.5.zb, f32[20,64,128]{2,1,0:T(8,128)S(1)} %collective-permute-done.6.za, f32[24,64,128]{2,1,0:T(8,128)} %collective-permute-done.7.left, f32[24,64,128]{2,1,0:T(8,128)} %collective-permute-done.8.right, s32[16,3,4]{2,1,0:T(4,128)S(1)} %all-to-all-done.refs_0_.roots), custom_call_target="tpu_custom_call" | custom-call | flops 5000000000 | tf_op jit(solution)/shard_map/halos/pallas_call | solution.py:142
  62.0 0.0 copy-start.10
  62.0 0.0 copy-start.11
  62.0 0.0 copy-start.12
  62.1 0.3 collective-permute-start.9
  62.3 0.0 collective-permute-done.3.part_own
  62.3 0.0 collective-permute-done.4.part_after
  62.4 0.0 collective-permute-done.2.part_before
  62.4 12.4 %middle.1.refs_5_ = bf16[196,256,128]{2,1,0:T(8,128)(2,1)} custom-call(f32[34,60,128]{2,1,0:T(8,128)} %collective-permute-done.before, f32[60,60,128]{2,1,0:T(8,128)S(1)} %copy-done.6, f32[34,60,128]{2,1,0:T(8,128)} %collective-permute-done.1.after, f32[34,60,128]{2,1,0:T(8,128)} %collective-permute-done.2.part_before, ...), custom_call_target="tpu_custom_call" | custom-call | flops 10000000000 | tf_op jit(solution)/shard_map/middle/pallas_call | solution.py:109
  74.8 4.6 %copy-done = bf16[196,256,128]{2,1,0:T(8,128)(2,1)S(1)} copy-done((bf16[196,256,128]{2,1,0:T(8,128)(2,1)S(1)}, bf16[196,256,128]{2,1,0:T(8,128)(2,1)}, u32[]{:S(2)}) %copy-start) | copy-done | bytes 12845080
  79.4 2.3 %fields.2 = (f32[16,848,128]{2,1,0:T(8,128)S(1)}, bf16[196,256,128]{2,1,0:T(8,128)(2,1)S(1)}) custom-call(s32[16,3,4]{2,1,0:T(4,128)S(1)} %all-to-all-done.refs_0_.roots, s32[3]{0:T(128)S(1)} %pad_add_fusion.refs_1_, bf16[48,128]{1,0:T(8,128)(2,1)S(1)} %copy-done.12, bf16[48,128]{1,0:T(8,128)(2,1)S(1)} %copy-done.11, ...), custom_call_target="tpu_custom_call", output_to_operand_aliasing={{1}: (5, {})} | custom-call | flops 48000000000 | tf_op jit(solution)/shard_map/fields/pallas_call | solution.py:304
  81.7 4.6 %copy-done.1 = bf16[196,256,128]{2,1,0:T(8,128)(2,1)} copy-done((bf16[196,256,128]{2,1,0:T(8,128)(2,1)}, bf16[196,256,128]{2,1,0:T(8,128)(2,1)S(1)}, u32[]{:S(2)}) %copy-start.1) | copy-done | bytes 12845080
  86.3 0.0 collective-permute-done.9.part
  86.3 4.6 %copy-done.2 = bf16[196,256,128]{2,1,0:T(8,128)(2,1)S(1)} copy-done((bf16[196,256,128]{2,1,0:T(8,128)(2,1)S(1)}, bf16[196,256,128]{2,1,0:T(8,128)(2,1)}, u32[]{:S(2)}) %copy-start.2) | copy-done | bytes 12845080
  91.0 0.4 join_halo.1.refs_5_
  91.4 4.6 %copy-done.3 = bf16[196,256,128]{2,1,0:T(8,128)(2,1)} copy-done((bf16[196,256,128]{2,1,0:T(8,128)(2,1)}, bf16[196,256,128]{2,1,0:T(8,128)(2,1)S(1)}, u32[]{:S(2)}) %copy-start.3) | copy-done | bytes 12845080
  96.0 4.6 %copy-done.4 = bf16[196,256,128]{2,1,0:T(8,128)(2,1)S(1)} copy-done((bf16[196,256,128]{2,1,0:T(8,128)(2,1)S(1)}, bf16[196,256,128]{2,1,0:T(8,128)(2,1)}, u32[]{:S(2)}) %copy-start.4) | copy-done | bytes 12845080
  100.7 2.3 %fields.3 = f32[16,848,128]{2,1,0:T(8,128)S(1)} custom-call(s32[16,3,4]{2,1,0:T(4,128)S(1)} %all-to-all-done.refs_0_.roots, s32[3]{0:T(128)S(1)} %pad_add_fusion.refs_1_, bf16[48,128]{1,0:T(8,128)(2,1)S(1)} %copy-done.12, bf16[48,128]{1,0:T(8,128)(2,1)S(1)} %copy-done.11, bf16[96,144]{1,0:T(8,128)(2,1)S(1)} %copy-done.10, ...), custom_call_target="tpu_custom_call", output_to_operand_aliasing={{}: (6, {})} | custom-call | flops 48000000000 | tf_op jit(solution)/shard_map/fields/pallas_call | solution.py:304
  102.9 106.5 %all_to_all.10.refs_1_ = f32[16,848,128]{2,1,0:T(8,128)S(1)} all-to-all(f32[16,848,128]{2,1,0:T(8,128)S(1)} %fields.3), channel_id=1, replica_groups=mesh['gx'=16,'gy'=2,'gz'=4] {'gx'}, dimensions={0} | all-to-all | bytes 13893632 | tf_op jit(solution)/shard_map/all_to_all | solution.py:404
  209.4 3.3 %pick.1 = f32[3456,128]{1,0:T(8,128)} custom-call(s32[3,4]{1,0:T(4,128)S(1)} %copy-done.7, f32[16,848,128]{2,1,0:T(8,128)S(1)} %all_to_all.10.refs_1_), custom_call_target="tpu_custom_call" | custom-call | tf_op jit(solution)/shard_map/pick/pallas_call | solution.py:348
  (15 shorter events, 0.0 us)
Async XLA Ops:
  0.0 1.5 copy-start.5
  1.5 5.4 %copy-start.6 = (f32[60,60,128]{2,1,0:T(8,128)S(1)}, f32[60,60,128]{2,1,0:T(8,128)}, u32[]{:S(2)}) copy-start(f32[60,60,128]{2,1,0:T(8,128)} %own.1) | copy-start | bytes 5529604
  2.6 4.6 %copy-start.8 = (f32[20,64,128]{2,1,0:T(8,128)}, f32[20,64,128]{2,1,0:T(8,128)S(1)}, u32[]{:S(2)}) copy-start(f32[20,64,128]{2,1,0:T(8,128)S(1)} %get-tuple-element.9.packed) | copy-start | bytes 1966084
  2.6 18.9 %collective-permute-start.5 = (f32[20,64,128]{2,1,0:T(8,128)S(1)}, f32[20,64,128]{2,1,0:T(8,128)S(1)}, u32[]{:S(2)}, u32[]{:S(2)}) collective-permute-start(f32[20,64,128]{2,1,0:T(8,128)S(1)} %get-tuple-element.9.packed), channel_id=1, source_target_pairs={{0,1},{1,2},{2,3},{3,0},{4,5},{5,6},{6,7},{7,4},{8,9},{9,10},{10,1... | collective-permute-start | bytes 1966088 | tf_op jit(solution)/shard_map/ppermute | solution.py:368
  4.7 16.9 %collective-permute-start.6 = (f32[20,64,128]{2,1,0:T(8,128)S(1)}, f32[20,64,128]{2,1,0:T(8,128)S(1)}, u32[]{:S(2)}, u32[]{:S(2)}) collective-permute-start(f32[20,64,128]{2,1,0:T(8,128)S(1)} %get-tuple-element.11), channel_id=1, source_target_pairs={{0,3},{1,0},{2,1},{3,2},{4,7},{5,4},{6,5},{7,6},{8,11},{9,8},{10,9... | collective-permute-start | bytes 1966088 | tf_op jit(solution)/shard_map/ppermute | solution.py:368
  7.2 30.2 %collective-permute-start.1 = (f32[34,60,128]{2,1,0:T(8,128)S(1)}, f32[34,60,128]{2,1,0:T(8,128)}, u32[]{:S(2)}, u32[]{:S(2)}) collective-permute-start(f32[34,60,128]{2,1,0:T(8,128)S(1)} %get-tuple-element.13), channel_id=1, source_target_pairs={{0,120},{8,0},{16,8},{24,16},{32,24},{40,32},{48,40},{56,48},{64,5... | collective-permute-start | bytes 3133448 | tf_op jit(solution)/shard_map/ppermute | solution.py:368
  12.5 30.9 %collective-permute-start = (f32[34,60,128]{2,1,0:T(8,128)S(1)}, f32[34,60,128]{2,1,0:T(8,128)}, u32[]{:S(2)}, u32[]{:S(2)}) collective-permute-start(f32[34,60,128]{2,1,0:T(8,128)S(1)} %get-tuple-element.14), channel_id=1, source_target_pairs={{0,8},{8,16},{16,24},{24,32},{32,40},{40,48},{48,56},{56,64},{64,7... | collective-permute-start | bytes 3133448 | tf_op jit(solution)/shard_map/ppermute | solution.py:368
  12.5 49.9 %collective-permute-start.3 = (f32[60,60,128]{2,1,0:T(8,128)S(1)}, f32[60,60,128]{2,1,0:T(8,128)}, u32[]{:S(2)}, u32[]{:S(2)}) collective-permute-start(f32[60,60,128]{2,1,0:T(8,128)S(1)} %copy-done.6), channel_id=1, source_target_pairs={{0,4},{4,0},{1,5},{5,1},{2,6},{6,2},{3,7},{7,3},{8,12},{12,8},{9,1... | collective-permute-start | bytes 5529608 | tf_op jit(solution)/shard_map/ppermute | solution.py:382
  21.8 21.6 %copy-start.7 = (s32[3,4]{1,0:T(4,128)S(1)}, s32[3,4]{1,0:T(4,128)}, u32[]{:S(2)}) copy-start(s32[3,4]{1,0:T(4,128)} %refs_0_.1) | copy-start | bytes 148
  22.7 36.1 %collective-permute-start.7 = (f32[24,64,128]{2,1,0:T(8,128)}, f32[24,64,128]{2,1,0:T(8,128)}, u32[]{:S(2)}, u32[]{:S(2)}) collective-permute-start(f32[24,64,128]{2,1,0:T(8,128)} %pad_maximum_fusion), channel_id=1, source_target_pairs={{0,8},{8,16},{16,24},{24,32},{32,40},{40,48},{48,56},{56,64},{64,7... | collective-permute-start | bytes 2359304 | tf_op jit(solution)/shard_map/ppermute | solution.py:368
  25.2 33.6 %collective-permute-start.8 = (f32[24,64,128]{2,1,0:T(8,128)}, f32[24,64,128]{2,1,0:T(8,128)}, u32[]{:S(2)}, u32[]{:S(2)}) collective-permute-start(f32[24,64,128]{2,1,0:T(8,128)} %pad_maximum_fusion.1), channel_id=1, source_target_pairs={{0,120},{8,0},{16,8},{24,16},{32,24},{40,32},{48,40},{56,48},{64,5... | collective-permute-start | bytes 2359304 | tf_op jit(solution)/shard_map/ppermute | solution.py:368
  37.4 24.9 %collective-permute-start.4 = (f32[34,60,128]{2,1,0:T(8,128)}, f32[34,60,128]{2,1,0:T(8,128)}, u32[]{:S(2)}, u32[]{:S(2)}) collective-permute-start(f32[34,60,128]{2,1,0:T(8,128)} %collective-permute-done.1.after), channel_id=1, source_target_pairs={{0,4},{4,0},{1,5},{5,1},{2,6},{6,2},{3,7},{7,3},{8,12},{12,8},{9,1... | collective-permute-start | bytes 3133448 | tf_op jit(solution)/shard_map/ppermute | solution.py:383
  43.3 19.0 %collective-permute-start.2 = (f32[34,60,128]{2,1,0:T(8,128)}, f32[34,60,128]{2,1,0:T(8,128)}, u32[]{:S(2)}, u32[]{:S(2)}) collective-permute-start(f32[34,60,128]{2,1,0:T(8,128)} %collective-permute-done.before), channel_id=1, source_target_pairs={{0,4},{4,0},{1,5},{5,1},{2,6},{6,2},{3,7},{7,3},{8,12},{12,8},{9,1... | collective-permute-start | bytes 3133448 | tf_op jit(solution)/shard_map/ppermute | solution.py:384
  44.0 14.9 %all-to-all-start = ((s32[16,3,4]{2,1,0:T(4,128)}), s32[16,3,4]{2,1,0:T(4,128)S(1)}, u32[]{:S(2)}, u32[]{:S(2)}) async-start(s32[16,3,4]{2,1,0:T(4,128)} %broadcast_in_dim.2), calls=%async_computation | async-start | bytes 65536 | tf_op jit(solution)/shard_map/all_to_all | solution.py:377
  58.8 3.5 %copy-start.9 = (f32[20,64,128]{2,1,0:T(8,128)S(1)}, f32[20,64,128]{2,1,0:T(8,128)}, u32[]{:S(2)}) copy-start(f32[20,64,128]{2,1,0:T(8,128)} %copy-done.8) | copy-start | bytes 1966084
  62.0 12.7 %copy-start.10 = (bf16[96,144]{1,0:T(8,128)(2,1)S(1)}, bf16[96,144]{1,0:T(8,128)(2,1)}, u32[]{:S(2)}) copy-start(bf16[96,144]{1,0:T(8,128)(2,1)} %constant.22.clone.refs_4_) | copy-start | bytes 82948
  62.0 12.7 %copy-start.11 = (bf16[48,128]{1,0:T(8,128)(2,1)S(1)}, bf16[48,128]{1,0:T(8,128)(2,1)}, u32[]{:S(2)}) copy-start(bf16[48,128]{1,0:T(8,128)(2,1)} %constant.21.clone.refs_3_) | copy-start | bytes 36868
  62.0 12.7 %copy-start.12 = (bf16[48,128]{1,0:T(8,128)(2,1)S(1)}, bf16[48,128]{1,0:T(8,128)(2,1)}, u32[]{:S(2)}) copy-start(bf16[48,128]{1,0:T(8,128)(2,1)} %constant.20.clone.refs_2_) | copy-start | bytes 36868
  62.1 24.2 %collective-permute-start.9 = (f32[80,72,128]{2,1,0:T(8,128)S(1)}, f32[80,72,128]{2,1,0:T(8,128)S(1)}, u32[]{:S(2)}, u32[]{:S(2)}) collective-permute-start(f32[80,72,128]{2,1,0:T(8,128)S(1)} %bitcast.9), channel_id=1, source_target_pairs={{0,4},{4,0},{1,5},{5,1},{2,6},{6,2},{3,7},{7,3},{8,12},{12,8},{9,1... | collective-permute-start | bytes 8847368 | tf_op jit(solution)/shard_map/ppermute | solution.py:387
  74.8 4.7 %copy-start = (bf16[196,256,128]{2,1,0:T(8,128)(2,1)S(1)}, bf16[196,256,128]{2,1,0:T(8,128)(2,1)}, u32[]{:S(2)}) copy-start(bf16[196,256,128]{2,1,0:T(8,128)(2,1)} %middle.1.refs_5_) | copy-start | bytes 38535172
  81.7 4.6 %copy-start.1 = (bf16[196,256,128]{2,1,0:T(8,128)(2,1)}, bf16[196,256,128]{2,1,0:T(8,128)(2,1)S(1)}, u32[]{:S(2)}) copy-start(bf16[196,256,128]{2,1,0:T(8,128)(2,1)S(1)} %get-tuple-element.10.full) | copy-start | bytes 38535172
  86.3 4.7 %copy-start.2 = (bf16[196,256,128]{2,1,0:T(8,128)(2,1)S(1)}, bf16[196,256,128]{2,1,0:T(8,128)(2,1)}, u32[]{:S(2)}) copy-start(bf16[196,256,128]{2,1,0:T(8,128)(2,1)} %copy-done.1) | copy-start | bytes 38535172
  91.4 4.6 %copy-start.3 = (bf16[196,256,128]{2,1,0:T(8,128)(2,1)}, bf16[196,256,128]{2,1,0:T(8,128)(2,1)S(1)}, u32[]{:S(2)}) copy-start(bf16[196,256,128]{2,1,0:T(8,128)(2,1)S(1)} %join_halo.1.refs_5_) | copy-start | bytes 38535172
  96.0 4.7 %copy-start.4 = (bf16[196,256,128]{2,1,0:T(8,128)(2,1)S(1)}, bf16[196,256,128]{2,1,0:T(8,128)(2,1)}, u32[]{:S(2)}) copy-start(bf16[196,256,128]{2,1,0:T(8,128)(2,1)} %copy-done.3) | copy-start | bytes 38535172

commit v6 on v5

--- a/solution.py
+++ b/solution.py
@@ -225,7 +225,7 @@
     lax.fori_loop(0, n, find, 0)
 
     def out_copy(j, b):
-        return pltpu.make_async_copy(obuf.at[b], out.at[j], sems.at[b])
+        return pltpu.make_async_copy(obuf.at[b, pl.ds(0, SENT)], out.at[j], sems.at[b])
 
     for b in range(G):
         t1[b * T1STEP + 64:b * T1STEP + 72, :] = jnp.zeros((8, 128), F32)
@@ -309,7 +309,7 @@
         scratch_shapes=[
             VMEM((G * T1STEP, 128), F32),
             VMEM((G * G, 128), F32),
-            VMEM((2, SENT, 128), F32),
+            VMEM((2, ROWS, 128), F32),
             SMEM((4, n), jnp.int32),
             pltpu.SemaphoreType.DMA((2,)),
         ],
@@ -330,15 +330,15 @@
             return jnp.where(r >= j * bx, j, anchor)
 
         anchor = lax.fori_loop(0, n, scan, jnp.int32(0), unroll=True)
-        pltpu.make_async_copy(parts.at[anchor], buf.at[s], sems.at[s]).start()
+        pltpu.make_async_copy(parts.at[anchor], buf.at[s, pl.ds(0, SENT)], sems.at[s]).start()
     for s in range(slot):
-        pltpu.make_async_copy(parts.at[0], buf.at[s], sems.at[s]).wait()
-        out[pl.ds(s, KEPT, stride=slot), :] = buf[s, :KEPT]
+        pltpu.make_async_copy(parts.at[0], buf.at[s, pl.ds(0, SENT)], sems.at[s]).wait()
         last = buf[s, :PLANE]
         for a in range(1, G - 1):
             plane = buf[s, a * PLANE:(a + 1) * PLANE]
             last = last - plane if a % 2 else last + plane
-        out[pl.ds(KEPT * slot + s, PLANE, stride=slot), :] = last
+        buf[s, KEPT:ROWS] = last
+        out[pl.ds(s, ROWS, stride=slot), :] = buf[s, :ROWS]
 
 
 def pick(sizes, slot, n, own_root, parts):
@@ -349,7 +349,7 @@
         kernel,
         out_shape=jax.ShapeDtypeStruct((ROWS * slot, 128), F32),
         in_specs=[pl.BlockSpec(memory_space=SMEM), pl.BlockSpec(memory_space=ANY)],
-        scratch_shapes=[VMEM((slot, SENT, 128), F32), pltpu.SemaphoreType.DMA((slot,))],
+        scratch_shapes=[VMEM((slot, ROWS + 16, 128), F32), pltpu.SemaphoreType.DMA((slot,))],
         compiler_params=vm(8),
         name="pick",
     )(own_root, parts)

time: 215 us -> 215 us (level)
  no operation moved by 1% of the time
where the time goes in v6:
time: 215 us; the launch traced here: 213 us
  blocking collectives  106 us (49%)
  waiting for transfers between devices  34.7 us (16%)
  local copies, waits for them, and re-layouts  25.7 us (12%)
  Pallas kernels  24.7 us (11%)
  starting transfers between devices  18.7 us (9%)
    all_to_all x1, blocking collectives, program(): parts = lax.all_to_all(done, 'gx', 0, 0, tiled=True)  106 us
    unnamed x26, local copies, waits for them, and re-layouts  24.7 us
    ppermute x6, waiting for transfers between devices, move(): return lax.ppermute(v, axis, [(i, (i + by) % count) for i in range(count)])  23.4 us
    ppermute x6, starting transfers between devices, move(): return lax.ppermute(v, axis, [(i, (i + by) % count) for i in range(count)])  14.9 us
    pallas_call x1, Pallas kernels, middle(): pl.pallas_call(mid_kernel, out_shape=jax.ShapeDtypeStruct((128 + 2 * HALO...  12.4 us
    all_to_all x1, waiting for transfers between devices, program(): lax.all_to_all(jnp.broadcast_to(frag_root[None], (groups, 3, slot)), 'gx'...  11.3 us
    pallas_call x2, Pallas kernels, fields(): pl.pallas_call(kernel, out_shape=(out,) if late else (out, jax.ShapeDtype...  4.52 us
  transfers between devices with their start and end apart: 11, of which 4 were waited for; matrix products, arithmetic and copies ran while one was open for 1% of the time, Pallas kernels for 8%

profile of v6, /device:TPU:0, one launch (start us, length us, event | category | flops | bytes accessed | tf_op | source)
XLA Modules:
  0.0 212.7 jit_solution(2614157656029776643)
XLA Ops:
  0.0 1.5 copy-done.5
  1.5 1.1 pack.1
  2.6 0.0 copy-start.8
  2.6 2.1 collective-permute-start.5
  4.7 2.2 %collective-permute-start.6 = (f32[20,64,128]{2,1,0:T(8,128)S(1)}, f32[20,64,128]{2,1,0:T(8,128)S(1)}, u32[]{:S(2)}, u32[]{:S(2)}) collective-permute-start(f32[20,64,128]{2,1,0:T(8,128)S(1)} %get-tuple-element.11), channel_id=1, source_target_pairs={{0,3},{1,0},{2,1},{3,2},{4,7},{5,4},{6,5},{7,6},{8,11},{9,8},{10,9... | collective-permute-start | bytes 1966088 | tf_op jit(solution)/shard_map/ppermute | solution.py:368
  6.9 0.2 fusion
  7.2 5.3 %collective-permute-start.1 = (f32[34,60,128]{2,1,0:T(8,128)S(1)}, f32[34,60,128]{2,1,0:T(8,128)}, u32[]{:S(2)}, u32[]{:S(2)}) collective-permute-start(f32[34,60,128]{2,1,0:T(8,128)S(1)} %get-tuple-element.13), channel_id=1, source_target_pairs={{0,120},{8,0},{16,8},{24,16},{32,24},{40,32},{48,40},{56,48},{64,5... | collective-permute-start | bytes 3133448 | tf_op jit(solution)/shard_map/ppermute | solution.py:368
  12.5 0.0 collective-permute-start
  12.5 0.0 collective-permute-start.3
  12.5 9.1 %collective-permute-done.5.zb = f32[20,64,128]{2,1,0:T(8,128)S(1)} collective-permute-done((f32[20,64,128]{2,1,0:T(8,128)S(1)}, f32[20,64,128]{2,1,0:T(8,128)S(1)}, u32[]{:S(2)}, u32[]{:S(2)}) %collective-permute-start.5) | collective-permute-done | bytes 655392 | tf_op jit(solution)/shard_map/ppermute | solution.py:368
  21.6 0.1 fusion.1
  21.7 0.0 collective-permute-done.6.za
  21.7 0.1 fusion.2
  21.8 0.0 copy-start.7
  21.8 1.0 pad_maximum_fusion
  22.7 1.5 collective-permute-start.7
  24.2 1.0 pad_maximum_fusion.1
  25.2 3.9 %collective-permute-start.8 = (f32[24,64,128]{2,1,0:T(8,128)}, f32[24,64,128]{2,1,0:T(8,128)}, u32[]{:S(2)}, u32[]{:S(2)}) collective-permute-start(f32[24,64,128]{2,1,0:T(8,128)} %pad_maximum_fusion.1), channel_id=1, source_target_pairs={{0,120},{8,0},{16,8},{24,16},{32,24},{40,32},{48,40},{56,48},{64,5... | collective-permute-start | bytes 2359304 | tf_op jit(solution)/shard_map/ppermute | solution.py:368
  29.0 8.4 %collective-permute-done.1.after = f32[34,60,128]{2,1,0:T(8,128)} collective-permute-done((f32[34,60,128]{2,1,0:T(8,128)S(1)}, f32[34,60,128]{2,1,0:T(8,128)}, u32[]{:S(2)}, u32[]{:S(2)}) %collective-permute-start.1) | collective-permute-done | bytes 1044512 | tf_op jit(solution)/shard_map/ppermute | solution.py:368
  37.4 0.0 collective-permute-start.4
  37.4 5.9 %collective-permute-done.before = f32[34,60,128]{2,1,0:T(8,128)} collective-permute-done((f32[34,60,128]{2,1,0:T(8,128)S(1)}, f32[34,60,128]{2,1,0:T(8,128)}, u32[]{:S(2)}, u32[]{:S(2)}) %collective-permute-start) | collective-permute-done | bytes 1044512 | tf_op jit(solution)/shard_map/ppermute | solution.py:368
  43.3 0.0 collective-permute-start.2
  43.3 0.6 broadcast_in_dim.2
  44.0 3.5 %all-to-all-start = ((s32[16,3,4]{2,1,0:T(4,128)}), s32[16,3,4]{2,1,0:T(4,128)S(1)}, u32[]{:S(2)}, u32[]{:S(2)}) async-start(s32[16,3,4]{2,1,0:T(4,128)} %broadcast_in_dim.2), calls=%async_computation | async-start | bytes 65536 | tf_op jit(solution)/shard_map/all_to_all | solution.py:377
  47.5 0.1 pad_add_fusion.refs_1_
  47.5 11.3 %all-to-all-done.refs_0_.roots = s32[16,3,4]{2,1,0:T(4,128)S(1)} async-done(((s32[16,3,4]{2,1,0:T(4,128)}), s32[16,3,4]{2,1,0:T(4,128)S(1)}, u32[]{:S(2)}, u32[]{:S(2)}) %all-to-all-start) | async-done | bytes 800 | tf_op jit(solution)/shard_map/all_to_all | solution.py:377
  58.8 0.0 collective-permute-done.7.left
  58.8 0.0 collective-permute-done.8.right
  58.8 3.2 %halos.1 = f32[5760,128]{1,0:T(8,128)S(1)} custom-call(f32[20,64,128]{2,1,0:T(8,128)S(1)} %collective-permute-done.5.zb, f32[20,64,128]{2,1,0:T(8,128)S(1)} %collective-permute-done.6.za, f32[24,64,128]{2,1,0:T(8,128)} %collective-permute-done.7.left, f32[24,64,128]{2,1,0:T(8,128)} %collective-permute-done.8.right, s32[16,3,4]{2,1,0:T(4,128)S(1)} %all-to-all-done.refs_0_.roots), custom_call_target="tpu_custom_call" | custom-call | flops 5000000000 | tf_op jit(solution)/shard_map/halos/pallas_call | solution.py:142
  62.0 0.0 copy-start.10
  62.0 0.0 copy-start.11
  62.0 0.0 copy-start.12
  62.1 0.3 collective-permute-start.9
  62.3 0.0 collective-permute-done.3.part_own
  62.3 0.0 collective-permute-done.4.part_after
  62.4 0.0 collective-permute-done.2.part_before
  62.4 12.4 %middle.1.refs_5_ = bf16[196,256,128]{2,1,0:T(8,128)(2,1)} custom-call(f32[34,60,128]{2,1,0:T(8,128)} %collective-permute-done.before, f32[60,60,128]{2,1,0:T(8,128)S(1)} %copy-done.6, f32[34,60,128]{2,1,0:T(8,128)} %collective-permute-done.1.after, f32[34,60,128]{2,1,0:T(8,128)} %collective-permute-done.2.part_before, ...), custom_call_target="tpu_custom_call" | custom-call | flops 10000000000 | tf_op jit(solution)/shard_map/middle/pallas_call | solution.py:109
  74.8 4.6 %copy-done = bf16[196,256,128]{2,1,0:T(8,128)(2,1)S(1)} copy-done((bf16[196,256,128]{2,1,0:T(8,128)(2,1)S(1)}, bf16[196,256,128]{2,1,0:T(8,128)(2,1)}, u32[]{:S(2)}) %copy-start) | copy-done | bytes 12845080
  79.4 2.3 %fields.2 = (f32[16,848,128]{2,1,0:T(8,128)S(1)}, bf16[196,256,128]{2,1,0:T(8,128)(2,1)S(1)}) custom-call(s32[16,3,4]{2,1,0:T(4,128)S(1)} %all-to-all-done.refs_0_.roots, s32[3]{0:T(128)S(1)} %pad_add_fusion.refs_1_, bf16[48,128]{1,0:T(8,128)(2,1)S(1)} %copy-done.12, bf16[48,128]{1,0:T(8,128)(2,1)S(1)} %copy-done.11, ...), custom_call_target="tpu_custom_call", output_to_operand_aliasing={{1}: (5, {})} | custom-call | flops 48000000000 | tf_op jit(solution)/shard_map/fields/pallas_call | solution.py:304
  81.7 4.6 %copy-done.1 = bf16[196,256,128]{2,1,0:T(8,128)(2,1)} copy-done((bf16[196,256,128]{2,1,0:T(8,128)(2,1)}, bf16[196,256,128]{2,1,0:T(8,128)(2,1)S(1)}, u32[]{:S(2)}) %copy-start.1) | copy-done | bytes 12845080
  86.3 0.0 collective-permute-done.9.part
  86.3 4.6 %copy-done.2 = bf16[196,256,128]{2,1,0:T(8,128)(2,1)S(1)} copy-done((bf16[196,256,128]{2,1,0:T(8,128)(2,1)S(1)}, bf16[196,256,128]{2,1,0:T(8,128)(2,1)}, u32[]{:S(2)}) %copy-start.2) | copy-done | bytes 12845080
  91.0 0.4 join_halo.1.refs_5_
  91.4 4.6 %copy-done.3 = bf16[196,256,128]{2,1,0:T(8,128)(2,1)} copy-done((bf16[196,256,128]{2,1,0:T(8,128)(2,1)}, bf16[196,256,128]{2,1,0:T(8,128)(2,1)S(1)}, u32[]{:S(2)}) %copy-start.3) | copy-done | bytes 12845080
  96.0 4.6 %copy-done.4 = bf16[196,256,128]{2,1,0:T(8,128)(2,1)S(1)} copy-done((bf16[196,256,128]{2,1,0:T(8,128)(2,1)S(1)}, bf16[196,256,128]{2,1,0:T(8,128)(2,1)}, u32[]{:S(2)}) %copy-start.4) | copy-done | bytes 12845080
  100.7 2.3 %fields.3 = f32[16,848,128]{2,1,0:T(8,128)S(1)} custom-call(s32[16,3,4]{2,1,0:T(4,128)S(1)} %all-to-all-done.refs_0_.roots, s32[3]{0:T(128)S(1)} %pad_add_fusion.refs_1_, bf16[48,128]{1,0:T(8,128)(2,1)S(1)} %copy-done.12, bf16[48,128]{1,0:T(8,128)(2,1)S(1)} %copy-done.11, bf16[96,144]{1,0:T(8,128)(2,1)S(1)} %copy-done.10, ...), custom_call_target="tpu_custom_call", output_to_operand_aliasing={{}: (6, {})} | custom-call | flops 48000000000 | tf_op jit(solution)/shard_map/fields/pallas_call | solution.py:304
  102.9 106.5 %all_to_all.10.refs_1_ = f32[16,848,128]{2,1,0:T(8,128)S(1)} all-to-all(f32[16,848,128]{2,1,0:T(8,128)S(1)} %fields.3), channel_id=1, replica_groups=mesh['gx'=16,'gy'=2,'gz'=4] {'gx'}, dimensions={0} | all-to-all | bytes 13893632 | tf_op jit(solution)/shard_map/all_to_all | solution.py:404
  209.4 3.2 %pick.1 = f32[3456,128]{1,0:T(8,128)} custom-call(s32[3,4]{1,0:T(4,128)S(1)} %copy-done.7, f32[16,848,128]{2,1,0:T(8,128)S(1)} %all_to_all.10.refs_1_), custom_call_target="tpu_custom_call" | custom-call | tf_op jit(solution)/shard_map/pick/pallas_call | solution.py:348
  (15 shorter events, 0.0 us)
Async XLA Ops:
  0.0 1.5 copy-start.5
  1.5 5.4 %copy-start.6 = (f32[60,60,128]{2,1,0:T(8,128)S(1)}, f32[60,60,128]{2,1,0:T(8,128)}, u32[]{:S(2)}) copy-start(f32[60,60,128]{2,1,0:T(8,128)} %own.1) | copy-start | bytes 5529604
  2.6 4.6 %copy-start.8 = (f32[20,64,128]{2,1,0:T(8,128)}, f32[20,64,128]{2,1,0:T(8,128)S(1)}, u32[]{:S(2)}) copy-start(f32[20,64,128]{2,1,0:T(8,128)S(1)} %get-tuple-element.9.packed) | copy-start | bytes 1966084
  2.6 18.9 %collective-permute-start.5 = (f32[20,64,128]{2,1,0:T(8,128)S(1)}, f32[20,64,128]{2,1,0:T(8,128)S(1)}, u32[]{:S(2)}, u32[]{:S(2)}) collective-permute-start(f32[20,64,128]{2,1,0:T(8,128)S(1)} %get-tuple-element.9.packed), channel_id=1, source_target_pairs={{0,1},{1,2},{2,3},{3,0},{4,5},{5,6},{6,7},{7,4},{8,9},{9,10},{10,1... | collective-permute-start | bytes 1966088 | tf_op jit(solution)/shard_map/ppermute | solution.py:368
  4.7 16.9 %collective-permute-start.6 = (f32[20,64,128]{2,1,0:T(8,128)S(1)}, f32[20,64,128]{2,1,0:T(8,128)S(1)}, u32[]{:S(2)}, u32[]{:S(2)}) collective-permute-start(f32[20,64,128]{2,1,0:T(8,128)S(1)} %get-tuple-element.11), channel_id=1, source_target_pairs={{0,3},{1,0},{2,1},{3,2},{4,7},{5,4},{6,5},{7,6},{8,11},{9,8},{10,9... | collective-permute-start | bytes 1966088 | tf_op jit(solution)/shard_map/ppermute | solution.py:368
  7.2 30.2 %collective-permute-start.1 = (f32[34,60,128]{2,1,0:T(8,128)S(1)}, f32[34,60,128]{2,1,0:T(8,128)}, u32[]{:S(2)}, u32[]{:S(2)}) collective-permute-start(f32[34,60,128]{2,1,0:T(8,128)S(1)} %get-tuple-element.13), channel_id=1, source_target_pairs={{0,120},{8,0},{16,8},{24,16},{32,24},{40,32},{48,40},{56,48},{64,5... | collective-permute-start | bytes 3133448 | tf_op jit(solution)/shard_map/ppermute | solution.py:368
  12.5 30.9 %collective-permute-start = (f32[34,60,128]{2,1,0:T(8,128)S(1)}, f32[34,60,128]{2,1,0:T(8,128)}, u32[]{:S(2)}, u32[]{:S(2)}) collective-permute-start(f32[34,60,128]{2,1,0:T(8,128)S(1)} %get-tuple-element.14), channel_id=1, source_target_pairs={{0,8},{8,16},{16,24},{24,32},{32,40},{40,48},{48,56},{56,64},{64,7... | collective-permute-start | bytes 3133448 | tf_op jit(solution)/shard_map/ppermute | solution.py:368
  12.5 49.9 %collective-permute-start.3 = (f32[60,60,128]{2,1,0:T(8,128)S(1)}, f32[60,60,128]{2,1,0:T(8,128)}, u32[]{:S(2)}, u32[]{:S(2)}) collective-permute-start(f32[60,60,128]{2,1,0:T(8,128)S(1)} %copy-done.6), channel_id=1, source_target_pairs={{0,4},{4,0},{1,5},{5,1},{2,6},{6,2},{3,7},{7,3},{8,12},{12,8},{9,1... | collective-permute-start | bytes 5529608 | tf_op jit(solution)/shard_map/ppermute | solution.py:382
  21.8 21.6 %copy-start.7 = (s32[3,4]{1,0:T(4,128)S(1)}, s32[3,4]{1,0:T(4,128)}, u32[]{:S(2)}) copy-start(s32[3,4]{1,0:T(4,128)} %refs_0_.1) | copy-start | bytes 148
  22.7 36.1 %collective-permute-start.7 = (f32[24,64,128]{2,1,0:T(8,128)}, f32[24,64,128]{2,1,0:T(8,128)}, u32[]{:S(2)}, u32[]{:S(2)}) collective-permute-start(f32[24,64,128]{2,1,0:T(8,128)} %pad_maximum_fusion), channel_id=1, source_target_pairs={{0,8},{8,16},{16,24},{24,32},{32,40},{40,48},{48,56},{56,64},{64,7... | collective-permute-start | bytes 2359304 | tf_op jit(solution)/shard_map/ppermute | solution.py:368
  25.2 33.6 %collective-permute-start.8 = (f32[24,64,128]{2,1,0:T(8,128)}, f32[24,64,128]{2,1,0:T(8,128)}, u32[]{:S(2)}, u32[]{:S(2)}) collective-permute-start(f32[24,64,128]{2,1,0:T(8,128)} %pad_maximum_fusion.1), channel_id=1, source_target_pairs={{0,120},{8,0},{16,8},{24,16},{32,24},{40,32},{48,40},{56,48},{64,5... | collective-permute-start | bytes 2359304 | tf_op jit(solution)/shard_map/ppermute | solution.py:368
  37.4 24.9 %collective-permute-start.4 = (f32[34,60,128]{2,1,0:T(8,128)}, f32[34,60,128]{2,1,0:T(8,128)}, u32[]{:S(2)}, u32[]{:S(2)}) collective-permute-start(f32[34,60,128]{2,1,0:T(8,128)} %collective-permute-done.1.after), channel_id=1, source_target_pairs={{0,4},{4,0},{1,5},{5,1},{2,6},{6,2},{3,7},{7,3},{8,12},{12,8},{9,1... | collective-permute-start | bytes 3133448 | tf_op jit(solution)/shard_map/ppermute | solution.py:383
  43.3 19.0 %collective-permute-start.2 = (f32[34,60,128]{2,1,0:T(8,128)}, f32[34,60,128]{2,1,0:T(8,128)}, u32[]{:S(2)}, u32[]{:S(2)}) collective-permute-start(f32[34,60,128]{2,1,0:T(8,128)} %collective-permute-done.before), channel_id=1, source_target_pairs={{0,4},{4,0},{1,5},{5,1},{2,6},{6,2},{3,7},{7,3},{8,12},{12,8},{9,1... | collective-permute-start | bytes 3133448 | tf_op jit(solution)/shard_map/ppermute | solution.py:384
  44.0 14.9 %all-to-all-start = ((s32[16,3,4]{2,1,0:T(4,128)}), s32[16,3,4]{2,1,0:T(4,128)S(1)}, u32[]{:S(2)}, u32[]{:S(2)}) async-start(s32[16,3,4]{2,1,0:T(4,128)} %broadcast_in_dim.2), calls=%async_computation | async-start | bytes 65536 | tf_op jit(solution)/shard_map/all_to_all | solution.py:377
  58.8 3.5 %copy-start.9 = (f32[20,64,128]{2,1,0:T(8,128)S(1)}, f32[20,64,128]{2,1,0:T(8,128)}, u32[]{:S(2)}) copy-start(f32[20,64,128]{2,1,0:T(8,128)} %copy-done.8) | copy-start | bytes 1966084
  62.0 12.7 %copy-start.10 = (bf16[96,144]{1,0:T(8,128)(2,1)S(1)}, bf16[96,144]{1,0:T(8,128)(2,1)}, u32[]{:S(2)}) copy-start(bf16[96,144]{1,0:T(8,128)(2,1)} %constant.22.clone.refs_4_) | copy-start | bytes 82948
  62.0 12.7 %copy-start.11 = (bf16[48,128]{1,0:T(8,128)(2,1)S(1)}, bf16[48,128]{1,0:T(8,128)(2,1)}, u32[]{:S(2)}) copy-start(bf16[48,128]{1,0:T(8,128)(2,1)} %constant.21.clone.refs_3_) | copy-start | bytes 36868
  62.0 12.7 %copy-start.12 = (bf16[48,128]{1,0:T(8,128)(2,1)S(1)}, bf16[48,128]{1,0:T(8,128)(2,1)}, u32[]{:S(2)}) copy-start(bf16[48,128]{1,0:T(8,128)(2,1)} %constant.20.clone.refs_2_) | copy-start | bytes 36868
  62.1 24.2 %collective-permute-start.9 = (f32[80,72,128]{2,1,0:T(8,128)S(1)}, f32[80,72,128]{2,1,0:T(8,128)S(1)}, u32[]{:S(2)}, u32[]{:S(2)}) collective-permute-start(f32[80,72,128]{2,1,0:T(8,128)S(1)} %bitcast.9), channel_id=1, source_target_pairs={{0,4},{4,0},{1,5},{5,1},{2,6},{6,2},{3,7},{7,3},{8,12},{12,8},{9,1... | collective-permute-start | bytes 8847368 | tf_op jit(solution)/shard_map/ppermute | solution.py:387
  74.8 4.7 %copy-start = (bf16[196,256,128]{2,1,0:T(8,128)(2,1)S(1)}, bf16[196,256,128]{2,1,0:T(8,128)(2,1)}, u32[]{:S(2)}) copy-start(bf16[196,256,128]{2,1,0:T(8,128)(2,1)} %middle.1.refs_5_) | copy-start | bytes 38535172
  81.7 4.6 %copy-start.1 = (bf16[196,256,128]{2,1,0:T(8,128)(2,1)}, bf16[196,256,128]{2,1,0:T(8,128)(2,1)S(1)}, u32[]{:S(2)}) copy-start(bf16[196,256,128]{2,1,0:T(8,128)(2,1)S(1)} %get-tuple-element.10.full) | copy-start | bytes 38535172
  86.3 4.7 %copy-start.2 = (bf16[196,256,128]{2,1,0:T(8,128)(2,1)S(1)}, bf16[196,256,128]{2,1,0:T(8,128)(2,1)}, u32[]{:S(2)}) copy-start(bf16[196,256,128]{2,1,0:T(8,128)(2,1)} %copy-done.1) | copy-start | bytes 38535172
  91.4 4.6 %copy-start.3 = (bf16[196,256,128]{2,1,0:T(8,128)(2,1)}, bf16[196,256,128]{2,1,0:T(8,128)(2,1)S(1)}, u32[]{:S(2)}) copy-start(bf16[196,256,128]{2,1,0:T(8,128)(2,1)S(1)} %join_halo.1.refs_5_) | copy-start | bytes 38535172
  96.0 4.7 %copy-start.4 = (bf16[196,256,128]{2,1,0:T(8,128)(2,1)S(1)}, bf16[196,256,128]{2,1,0:T(8,128)(2,1)}, u32[]{:S(2)}) copy-start(bf16[196,256,128]{2,1,0:T(8,128)(2,1)} %copy-done.3) | copy-start | bytes 38535172
